TPU v7x, 32 devices: a whole 2x2x4 slice. The times are simulated.
32 devices in a mesh: dp: 4 (over z), ctx: 8 (over y, x, core).
Axes of the slice: x: 2, y: 2, z: 4, core: 2. Of those that a mesh axis runs over, the one named last changes fastest.
Arguments:
- hidden_in: bfloat16 [4, 1024, 2048], P('dp', 'ctx'), may hold values from -6 to 6
- w_in_t: bfloat16 [14336, 2048], P(None, ('dp', 'ctx')), may hold values from -4 to 4
- in_bias: bfloat16 [7, 2048], P(None, ('dp', 'ctx')), may hold values from -3 to 3
- ln_gain: bfloat16 [1, 2048], P(None, ('dp', 'ctx')), may hold values from 0.5 to 1.5
- ln_shift: bfloat16 [1, 2048], P(None, ('dp', 'ctx')), may hold values from -2 to 2
- w_out_t: bfloat16 [2048, 10240], P(('dp', 'ctx')), may hold values from -4 to 4
- out_bias: bfloat16 [2048], P(('dp', 'ctx')), may hold values from -3 to 3
- segment_ids: int32 [4, 1024], P('dp'), may hold values from 0 to 3, never falling along the last dimension, each value on 1 to 768 neighbouring positions
- out_grad: bfloat16 [4, 1024, 2048], P('dp', 'ctx'), may hold values from -6 to 6
Outputs:
- layer_out: bfloat16 [4, 1024, 2048], P('dp', 'ctx')
- input_grad: float32 [4, 1024, 2048], P('dp', 'ctx')
- grad_w_in: float32 [14336, 2048], P(None, ('dp', 'ctx'))
- grad_in_bias: float32 [7, 2048], P(None, ('dp', 'ctx'))
- grad_gain: float32 [1, 2048], P(None, ('dp', 'ctx'))
- grad_shift: float32 [1, 2048], P(None, ('dp', 'ctx'))
- grad_w_out: float32 [2048, 10240], P(('dp', 'ctx'))
- grad_out_bias: float32 [2048], P(('dp', 'ctx'))
Inputs may be any that keep to these rules, and one draw needn't show every extreme that they name: `segment_ids`: within each sequence the numbers never fall; every document has 1 to 768 tokens and one has exactly 768.
All inputs are finite; a program needn't handle non-finite values.
Results may differ from a plain program's by a relative error of at most 0.033.
Values may be sent and summed in bfloat16 or wider, within the bound.
A program may use at most 704 MiB of HBM per device.

v0:
```python
import math

import jax
import jax.numpy as jnp
from jax import lax
from jax.sharding import PartitionSpec as P

H = 32
HD = 64
ROT = 32
KEY_BLOCK = 512


epsilon = 1e-05
negative = -1e30


def rotation_tables(positions):
    half_dims = ROT // 2
    frequency = 10000.0 ** (-2.0 * jnp.arange(half_dims, dtype=jnp.float32) / ROT)
    angles = positions[:, None] * frequency[None, :]
    return (jnp.cos(angles)[:, None, :], jnp.sin(angles)[:, None, :])


def rotate(heads_in, cosine_table, sine_table, direction):
    half_dims = ROT // 2
    first_half = heads_in[..., :half_dims]
    second_half = heads_in[..., half_dims:ROT]
    return jnp.concatenate(
        [
            first_half * cosine_table - direction * second_half * sine_table,
            second_half * cosine_table + direction * first_half * sine_table,
            heads_in[..., ROT:],
        ],
        -1,
    )


def masked_scores(queries, key_rows, key_seg, key_index, query_seg, query_index):
    scaling = queries.shape[2] ** (-0.5)
    scores = (
        jnp.einsum("thd,khd->htk", queries, key_rows, preferred_element_type=jnp.float32) * scaling
    )
    allowed = (query_seg[:, None] == key_seg[None, :]) & (
        query_index[:, None] >= key_index[None, :]
    )
    return (jnp.where(allowed[None], scores, negative), allowed)


def score_grads(
    query_part,
    dout_part,
    lse_part,
    dot_part,
    query_seg,
    query_index,
    key_rows,
    value_rows,
    key_seg,
    key_index,
):
    scores, allowed = masked_scores(
        query_part, key_rows, key_seg, key_index, query_seg, query_index
    )
    weights = jnp.where(allowed[None], jnp.exp(scores - lse_part[..., None]), 0.0)
    d_weights = jnp.einsum(
        "thd,khd->htk", dout_part, value_rows, preferred_element_type=jnp.float32
    )
    d_scores = (weights * (d_weights - dot_part[..., None])).astype(jnp.bfloat16)
    return (weights.astype(jnp.bfloat16), d_scores)


def key_grads(
    key_rows,
    value_rows,
    key_seg,
    key_index,
    query_src,
    dout_src,
    lse_src,
    dot_src,
    seg_src,
    index_src,
    query_block,
):
    key_count = key_rows.shape[0]
    scaling = HD ** (-0.5)
    block_count = query_src.shape[0] // query_block

    def query_step(running, block_no):
        weights_low, d_scores = score_grads(
            query_src,
            dout_src,
            lse_src,
            dot_src,
            seg_src,
            index_src,
            key_rows,
            value_rows,
            key_seg,
            key_index,
        )
        d_key = (
            running[0]
            + jnp.einsum("htk,thd->khd", d_scores, query_src, preferred_element_type=jnp.float32)
            * scaling
        )
        d_value = running[1] + jnp.einsum(
            "htk,thd->khd", weights_low, dout_src, preferred_element_type=jnp.float32
        )
        return ((d_key, d_value), None)

    zero_heads = jnp.zeros((key_count, H, HD), jnp.float32)
    (d_key, d_value), _ = lax.scan(query_step, (zero_heads, zero_heads), jnp.arange(block_count))
    return (d_key.reshape(key_count, H * HD), d_value.reshape(key_count, H * HD))


def on_device(
    hidden_in, w_in_t, in_bias, ln_gain, ln_shift, w_out_t, out_bias, segment_ids, out_grad
):
    inputs = hidden_in[0].astype(jnp.float32)
    tok_rows, model_width = inputs.shape
    seg_row = segment_ids[0]
    seq_len = seg_row.shape[0]
    offset = lax.axis_index("ctx") * tok_rows
    index_all = jnp.arange(seq_len, dtype=jnp.int32)
    earlier = jnp.concatenate([seg_row[:1], seg_row[:-1]])
    begins = jnp.where((index_all == 0) | (seg_row != earlier), index_all, 0)
    positions = (index_all - lax.cummax(begins, axis=0)).astype(jnp.float32)
    local_pos = lax.dynamic_slice_in_dim(positions, offset, tok_rows)
    query_seg = lax.dynamic_slice_in_dim(seg_row, offset, tok_rows)
    query_index = offset + jnp.arange(tok_rows, dtype=jnp.int32)
    cosine_table, sine_table = rotation_tables(local_pos)
    scaling = HD ** (-0.5)
    average = jnp.mean(inputs, -1, keepdims=True)
    centred = inputs - average
    inv_std = lax.rsqrt(jnp.mean(centred * centred, -1, keepdims=True) + epsilon)
    normed_hat = centred * inv_std
    joint_width = w_in_t.shape[0]
    bias_rows = in_bias.shape[0]
    weight_piece = lax.all_gather(w_in_t, ("dp", "ctx"), axis=1, tiled=True)
    bias_piece = lax.all_gather(in_bias, ("dp", "ctx"), axis=1, tiled=True)
    gain_piece = lax.all_gather(ln_gain, ("dp", "ctx"), axis=1, tiled=True)
    shift_piece = lax.all_gather(ln_shift, ("dp", "ctx"), axis=1, tiled=True)
    normed_piece = (
        normed_hat * gain_piece.astype(jnp.float32) + shift_piece.astype(jnp.float32)
    ).astype(jnp.bfloat16)
    summed = lax.dot_general(
        normed_piece, weight_piece, (((1,), (1,)), ((), ())), preferred_element_type=jnp.float32
    )
    gain_all = gain_piece.astype(jnp.float32)
    bias_all = bias_piece.astype(jnp.float32)
    projected, normed, gain_all, bias_all = (summed, normed_piece, gain_all, bias_all)
    projected = projected + bias_all.reshape(1, joint_width)
    queries = rotate(
        projected[:, :model_width].reshape(tok_rows, H, HD), cosine_table, sine_table, 1.0
    ).astype(jnp.bfloat16)
    keys_new = (
        rotate(
            projected[:, model_width : 2 * model_width].reshape(tok_rows, H, HD),
            cosine_table,
            sine_table,
            1.0,
        )
        .astype(jnp.bfloat16)
        .reshape(tok_rows, model_width)
    )
    values_new = projected[:, 2 * model_width : 3 * model_width].astype(jnp.bfloat16)
    pre_gelu = projected[:, 3 * model_width :]
    keys_all, values_all = (
        lax.all_gather(keys_new, "ctx", axis=0, tiled=True),
        lax.all_gather(values_new, "ctx", axis=0, tiled=True),
    )
    block_count = seq_len // KEY_BLOCK

    def key_slice(first_key, key_count):
        key_rows = lax.dynamic_slice_in_dim(keys_all, first_key, key_count, 0).reshape(
            key_count, H, HD
        )
        value_rows = lax.dynamic_slice_in_dim(values_all, first_key, key_count, 0).reshape(
            key_count, H, HD
        )
        key_seg = lax.dynamic_slice_in_dim(seg_row, first_key, key_count)
        key_index = first_key + jnp.arange(key_count, dtype=jnp.int32)
        return (key_rows, value_rows, key_seg, key_index)

    def stats_step(running, block_no):
        running_max, running_sum = running
        key_rows, value_rows, key_seg, key_index = key_slice(block_no * KEY_BLOCK, KEY_BLOCK)
        scores, allowed = masked_scores(
            queries, key_rows, key_seg, key_index, query_seg, query_index
        )
        new_max = jnp.maximum(running_max, jnp.max(scores, -1))
        weights = jnp.where(allowed[None], jnp.exp(scores - new_max[..., None]), 0.0)
        running_sum = running_sum * jnp.exp(running_max - new_max) + jnp.sum(weights, -1)
        return ((new_max, running_sum), None)

    stats_init = (
        jnp.full((H, tok_rows), negative, jnp.float32),
        jnp.zeros((H, tok_rows), jnp.float32),
    )
    (final_max, final_sum), _ = lax.scan(stats_step, stats_init, jnp.arange(block_count))
    log_total = final_max + jnp.log(final_sum)

    def value_step(attended, block_no):
        key_rows, value_rows, key_seg, key_index = key_slice(block_no * KEY_BLOCK, KEY_BLOCK)
        scores, allowed = masked_scores(
            queries, key_rows, key_seg, key_index, query_seg, query_index
        )
        weights = jnp.where(allowed[None], jnp.exp(scores - log_total[..., None]), 0.0).astype(
            jnp.bfloat16
        )
        attended = attended + jnp.einsum(
            "htk,khd->thd", weights, value_rows, preferred_element_type=jnp.float32
        )
        return (attended, None)

    attended, _ = lax.scan(
        value_step, jnp.zeros((tok_rows, H, HD), jnp.float32), jnp.arange(block_count)
    )
    hidden = jax.nn.gelu(pre_gelu, approximate=True).astype(jnp.bfloat16)
    joined = jnp.concatenate(
        [attended.reshape(tok_rows, model_width).astype(jnp.bfloat16), hidden], 1
    )
    weight_piece, bias_piece = lax.all_gather(
        (w_out_t, out_bias), ("dp", "ctx"), axis=0, tiled=True
    )
    branch = (
        lax.dot_general(
            joined, weight_piece, (((1,), (1,)), ((), ())), preferred_element_type=jnp.float32
        )
        + bias_piece.astype(jnp.float32)[None, :]
    )
    result = (inputs + branch).astype(jnp.bfloat16)
    cotangent = out_grad[0]
    grad_part = cotangent
    d_joined = jnp.dot(
        grad_part,
        lax.all_gather(w_out_t, ("dp", "ctx"), axis=0, tiled=True),
        preferred_element_type=jnp.float32,
    )
    d_attn = d_joined[:, :model_width].astype(jnp.bfloat16).reshape(tok_rows, H, HD)

    def gelu_tanh(pre_values):
        return jax.nn.gelu(pre_values, approximate=True)

    _, gelu_pull = jax.vjp(gelu_tanh, pre_gelu)
    d_pre = gelu_pull(d_joined[:, model_width:])[0]
    row_dots = jnp.einsum("thd,thd->ht", d_attn.astype(jnp.float32), attended)

    def query_grad_step(d_query, block_no):
        key_rows, value_rows, key_seg, key_index = key_slice(block_no * KEY_BLOCK, KEY_BLOCK)
        _, d_scores = score_grads(
            queries,
            d_attn,
            log_total,
            row_dots,
            query_seg,
            query_index,
            key_rows,
            value_rows,
            key_seg,
            key_index,
        )
        d_query = (
            d_query
            + jnp.einsum("htk,khd->thd", d_scores, key_rows, preferred_element_type=jnp.float32)
            * scaling
        )
        return (d_query, None)

    d_query, _ = lax.scan(
        query_grad_step, jnp.zeros((tok_rows, H, HD), jnp.float32), jnp.arange(block_count)
    )
    count = lax.axis_size("ctx") * tok_rows
    sub_rows = math.gcd(count, KEY_BLOCK)

    def sub_step(carry_none, block_no):
        key_rows, value_rows, key_seg, key_index = key_slice(block_no * sub_rows, sub_rows)
        d_key, d_value = key_grads(
            key_rows,
            value_rows,
            key_seg,
            key_index,
            queries,
            d_attn,
            log_total,
            row_dots,
            query_seg,
            query_index,
            tok_rows,
        )
        return (carry_none, jnp.concatenate([d_key, d_value], 1))

    _, stacked = lax.scan(sub_step, jnp.zeros((), jnp.float32), jnp.arange(count // sub_rows))
    d_kv = lax.psum_scatter(
        stacked.reshape(count, 2 * model_width).astype(jnp.bfloat16),
        "ctx",
        scatter_dimension=0,
        tiled=True,
    ).astype(jnp.float32)
    d_key_local, d_value_local = (d_kv[:, :model_width], d_kv[:, model_width:])
    d_query_pre = rotate(d_query, cosine_table, sine_table, -1.0).reshape(tok_rows, model_width)
    d_key_pre = rotate(
        d_key_local.reshape(tok_rows, H, HD), cosine_table, sine_table, -1.0
    ).reshape(tok_rows, model_width)
    d_joint = jnp.concatenate([d_query_pre, d_key_pre, d_value_local, d_pre], 1).astype(
        jnp.bfloat16
    )
    d_normed = jnp.dot(
        d_joint,
        lax.all_gather(w_in_t, ("dp", "ctx"), axis=1, tiled=True),
        preferred_element_type=jnp.float32,
    )
    grad_part = cotangent
    in_term = lax.dot_general(
        normed, d_joint, (((0,), (0,)), ((), ())), preferred_element_type=jnp.float32
    )
    out_term = lax.dot_general(
        grad_part, joined, (((0,), (0,)), ((), ())), preferred_element_type=jnp.float32
    )
    grad_rows = lax.psum_scatter(
        jnp.concatenate([in_term, out_term], 1), ("dp", "ctx"), scatter_dimension=0, tiled=True
    )
    grad_w_in = grad_rows[:, :joint_width].T
    grad_w_out = grad_rows[:, joint_width:]
    grad_bias_in = jnp.sum(d_joint.astype(jnp.float32), 0).reshape(bias_rows, model_width)
    grad_gain_row = jnp.sum(d_normed * normed_hat, 0, keepdims=True)
    grad_shift_row = jnp.sum(d_normed, 0, keepdims=True)
    grad_bias_out = jnp.sum(cotangent.astype(jnp.float32), 0, keepdims=True)
    grad_in_bias, grad_gain, grad_shift, grad_out_row = (
        lax.psum_scatter(grad_bias_in, ("dp", "ctx"), scatter_dimension=1, tiled=True),
        lax.psum_scatter(grad_gain_row, ("dp", "ctx"), scatter_dimension=1, tiled=True),
        lax.psum_scatter(grad_shift_row, ("dp", "ctx"), scatter_dimension=1, tiled=True),
        lax.psum_scatter(grad_bias_out, ("dp", "ctx"), scatter_dimension=1, tiled=True),
    )
    d_hat = d_normed * gain_all
    d_input = inv_std * (
        d_hat
        - jnp.mean(d_hat, -1, keepdims=True)
        - normed_hat * jnp.mean(d_hat * normed_hat, -1, keepdims=True)
    ) + cotangent.astype(jnp.float32)
    return (
        result[None],
        d_input[None],
        grad_w_in,
        grad_in_bias,
        grad_gain,
        grad_shift,
        grad_w_out,
        grad_out_row[0],
    )


def solution(mesh):
    in_specs = (
        P("dp", "ctx", None),
        P(None, ("dp", "ctx")),
        P(None, ("dp", "ctx")),
        P(None, ("dp", "ctx")),
        P(None, ("dp", "ctx")),
        P(("dp", "ctx"), None),
        P(("dp", "ctx")),
        P("dp", None),
        P("dp", "ctx", None),
    )
    out_specs = (
        P("dp", "ctx", None),
        P("dp", "ctx", None),
        P(None, ("dp", "ctx")),
        P(None, ("dp", "ctx")),
        P(None, ("dp", "ctx")),
        P(None, ("dp", "ctx")),
        P(("dp", "ctx"), None),
        P(("dp", "ctx")),
    )
    return jax.shard_map(
        on_device, mesh=mesh, in_specs=in_specs, out_specs=out_specs, check_vma=False
    )
```

profile of v0, /device:TPU:0, one launch (start us, length us, event | category | flops | bytes accessed | tf_op | source)
XLA Modules:
  0.0 3001.3 jit_solution(11647417623748919152)
XLA Ops:
  14.3 45.4 %all-reduce.3 = (bf16[2048]{0:T(1024)(128)(2,1)S(1)}, bf16[2048]{0:T(1024)(128)(2,1)S(1)}, bf16[2048]{0:T(1024)(128)(2,1)}) all-reduce(bf16[2048]{0:T(1024)(128)(2,1)S(1)} %dynamic-update-slice.1, bf16[2048]{0:T(1024)(128)(2,1)S(1)} %dynamic-update-slice, ...), channel_id=1, replica_groups=mesh['dp'=4,'ctx'=8] {'dp','ctx'}, use_global_device_ids=true, to_apply=%add.1 | all-reduce | flops 6144 | bytes 24576
  59.8 42.6 %all-gather = bf16[32,64,7]{1,2,0:T(8,128)(2,1)S(1)} all-gather(bf16[1,64,7]{1,2,0:T(8,128)(2,1)} %bitcast.344), channel_id=1, replica_groups=mesh['dp'=4,'ctx'=8] {'dp','ctx'}, dimensions={0}, use_global_device_ids=true | all-gather | bytes 29568 | tf_op jit(solution)/shard_map/all_gather | solution.py:142
  104.0 226.2 %all-gather.6.cloned.1.call-done = bf16[14336,2048]{0,1:T(8,128)(2,1)} async-done(((bf16[14336,64]{0,1:T(8,128)(2,1)}), bf16[14336,2048]{0,1:T(8,128)(2,1)}) %all-gather.6.cloned.1.call-update) | async-done | bytes 58720272 | tf_op jit(solution)/shard_map/all_gather | solution.py:141
  330.2 25.2 convolution_add_fusion
  363.4 202.2 %all-gather.12.cloned.1.call-done = bf16[2048,10240]{1,0:T(8,128)(2,1)} async-done(((bf16[64,10240]{1,0:T(8,128)(2,1)}), bf16[2048,10240]{1,0:T(8,128)(2,1)}) %all-gather.12.cloned.1.call-update) | async-done | bytes 41943056 | tf_op jit(solution)/shard_map/all_gather | solution.py:225
  565.7 18.8 fusion.102
  587.2 16.5 all-gather.10.cloned.1.call-done
  603.7 14.6 while.52
  618.3 24.3 all-gather.8.cloned.1.call-done
  642.6 6.4 copy.82
  649.0 22.1 while.53
  665.3 5.8 fusion.186
  672.6 52.8 %while.51 = (s32[]{:T(128)}, bf16[2,512,4096]{1,2,0:T(8,128)(2,1)}, s32[128]{0:T(128)S(1)}, s32[2]{0:T(128)S(1)}, s32[1024]{0:T(1024)S(1)}, /*index=5*/bf16[1024...) while((s32[]{:T(128)}, bf16[2,512,4096]{1,2,0:T(8,128)(2,1)}, ...), condition=%wide.region_13.14_spmd.clone, body=%wide.region_12.13_spmd.clone.sunk | while | flops 1109590656 | bytes 52686572 | solution.py:295
  683.0 8.1 broadcast_multiply_fusion.6
  691.2 5.8 fusion.176
  709.2 8.1 broadcast_multiply_fusion.6
  717.3 5.8 fusion.176
  725.4 11.3 copy.87
  736.8 6.8 fusion.81
  744.7 38.9 %while.54 = (s32[]{:T(128)}, f32[128,32,64]{0,2,1:T(8,128)}, s32[2]{0:T(128)S(1)}, bf16[1024,2048]{0,1:T(8,128)(2,1)}, s32[128]{0:T(128)S(1)}, /*index=5*/s32[10...) while((s32[]{:T(128)}, f32[128,32,64]{0,2,1:T(8,128)}, ...), condition=%wide.region_11.12_spmd.clone, body=%wide.region_10.11_spmd.clone.sunk | while | flops 820970112 | bytes 34778864 | solution.py:272
  755.4 8.8 fusion.194
  774.2 9.4 fusion.194
  784.7 23.6 reduce-scatter.15.cloned.1.call-done
  816.3 27.2 fusion.97
  847.8 30.6 %convolution_bitcast_fusion = f32[2048,10240]{1,0:T(8,128)} fusion(bf16[128,8192]{1,0:T(8,128)(2,1)} %get-tuple-element.649, bf16[128,2048]{1,0:T(8,128)(2,1)} %copy.83, bf16[1,128,2048]{2,1,0:T(8,128)(2,1)S(1)} %copy-done.6), kind=kOutput, calls=%fused_computation.83 | convolution fusion | flops 5373952000 | bytes 87031808 | tf_op jit(solution)/shard_map/dot_general | solution.py:319
  879.9 39.6 %fusion.111 = f32[2048,14336]{1,0:T(8,128)} fusion(bf16[1,128,2048]{2,1,0:T(8,128)(2,1)S(1)} %copy-done.2, f32[2048]{0:T(1024)S(1)} %copy-done.13, f32[2048]{0:T(1024)S(1)} %copy-done.11, f32[128]{0:T(128)S(1)} %copy-done.18, f32[128]{0:T(128)S(1)} %copy-done.16, bf16[128,8192]{1,0:T(8,128)(2,1)S(1)} %copy-done, bf16[128,2048]{1,0:T(8,128)(2,1)} %get-tuple-element.661, ...), kind=kOutput, calls=%fused_computation.167 | convolution fusion | flops 7532445696 | bytes 121652224 | tf_op jit(solution)/shard_map/dot_general | solution.py:316
  924.2 130.6 %pad_maximum_fusion = f32[2048,24576]{1,0:T(8,128)} fusion(f32[2048,10240]{1,0:T(8,128)} %convolution_bitcast_fusion, f32[2048,14336]{1,0:T(8,128)} %fusion.111), kind=kLoop, calls=%fused_computation.82 | loop fusion | flops 50331648 | bytes 402653184 | tf_op jit(solution)/shard_map/concatenate | solution.py:323
  1056.6 20.1 fusion.84
  1078.0 41.1 %reduce-scatter.21.cloned.1.call-done = f32[64,1]{1,0:T(8,128)} async-done(((f32[2048,1]{1,0:T(8,128)}), f32[64,1]{1,0:T(8,128)}) %reduce-scatter.21.cloned.1.call-update) | async-done | bytes 272
  1120.4 133.4 %reduce-scatter.23.cloned.1.call-done = f32[64,1]{1,0:T(8,128)} async-done(((f32[2048,1]{1,0:T(8,128)}), f32[64,1]{1,0:T(8,128)}) %reduce-scatter.23.cloned.1.call-update) | async-done | bytes 272
  1255.1 134.1 %reduce-scatter.19.cloned.1.call-done = f32[64,7]{1,0:T(8,128)} async-done(((f32[2048,7]{1,0:T(8,128)}), f32[64,7]{1,0:T(8,128)}) %reduce-scatter.19.cloned.1.call-update) | async-done | bytes 1808
  1390.6 1596.1 %reduce-scatter.17.cloned.1.call-done = f32[64,24576]{1,0:T(8,128)} async-done(((f32[2048,24576]{1,0:T(8,128)}), f32[64,24576]{1,0:T(8,128)}) %reduce-scatter.17.cloned.1.call-update) | async-done | bytes 6291472 | tf_op jit(solution)/shard_map/reduce_scatter | solution.py:322
  (207 shorter events, 126.3 us)
Async XLA Ops:
  7.2 95.7 %copy-start.1 = (bf16[1,128,2048]{2,1,0:T(8,128)(2,1)S(1)}, bf16[1,128,2048]{2,1,0:T(8,128)(2,1)}, u32[]{:S(2)}) copy-start(bf16[1,128,2048]{2,1,0:T(8,128)(2,1)} %param.17) | copy-start | bytes 1572868
  7.2 323.0 %all-gather.6.cloned.1.call-start = ((), (), s32[]{:S(2)}) async-start(), calls=%async_computation.6 | async-start | bytes 60555264 | tf_op jit(solution)/shard_map/all_gather | solution.py:141
  7.9 557.8 %all-gather.12.cloned.1.call-start = ((), (), s32[]{:S(2)}) async-start(), calls=%async_computation.9 | async-start | bytes 43253760 | tf_op jit(solution)/shard_map/all_gather | solution.py:225
  8.7 595.0 %all-gather.10.cloned.1.call-start = ((), (), s32[]{:S(2)}) async-start(), calls=%async_computation.8 | async-start | bytes 4718592 | tf_op jit(solution)/shard_map/all_gather | solution.py:171
  59.8 270.4 %copy-start.12 = (f32[2048]{0:T(1024)}, f32[2048]{0:T(1024)S(1)}, u32[]{:S(2)}) copy-start(f32[2048]{0:T(1024)S(1)} %add.217) | copy-start | bytes 24580
  59.8 270.4 %copy-start.10 = (f32[2048]{0:T(1024)}, f32[2048]{0:T(1024)S(1)}, u32[]{:S(2)}) copy-start(f32[2048]{0:T(1024)S(1)} %mul.358) | copy-start | bytes 24580
  103.0 227.2 %copy-start.15 = (f32[128]{0:T(128)}, f32[128]{0:T(128)S(1)}, u32[]{:S(2)}) copy-start(f32[128]{0:T(128)S(1)} %broadcast_multiply_fusion.4) | copy-start | bytes 1540
  103.3 226.9 %copy-start.17 = (f32[128]{0:T(128)}, f32[128]{0:T(128)S(1)}, u32[]{:S(2)}) copy-start(f32[128]{0:T(128)S(1)} %add_rsqrt_fusion) | copy-start | bytes 1540
  104.0 254.8 %copy-start.19 = (f32[128,16]{0,1:T(8,128)}, f32[128,16]{0,1:T(8,128)S(1)}, u32[]{:S(2)}) copy-start(f32[128,16]{0,1:T(8,128)S(1)} %get-tuple-element.670) | copy-start | bytes 24580
  357.1 3.9 copy-start.14
  358.4 207.3 %copy-start.5 = (bf16[1,128,2048]{2,1,0:T(8,128)(2,1)S(1)}, bf16[1,128,2048]{2,1,0:T(8,128)(2,1)}, u32[]{:S(2)}) copy-start(bf16[1,128,2048]{2,1,0:T(8,128)(2,1)} %param.25) | copy-start | bytes 1572868
  360.9 281.7 %all-gather.8.cloned.1.call-start = ((), (), s32[]{:S(2)}) async-start(), calls=%async_computation.7 | async-start | bytes 4718592 | tf_op jit(solution)/shard_map/all_gather | solution.py:172
  363.1 445.3 %reduce-scatter.15.cloned.1.call-start = ((), (), s32[]{:S(2)}) async-start(), calls=%async_computation.10 | async-start | bytes 9437184 | tf_op jit(solution)/shard_map/reduce_scatter | solution.py:296
  736.7 340.0 %reduce-scatter.25.cloned.1.call-start = ((), (), s32[]{:S(2)}) async-start(), calls=%async_computation.15 | async-start | bytes 1081344
  736.8 6.8 copy-start.8
  783.6 27.3 copy-start.20
  783.6 27.3 copy-start.21
  810.7 5.6 copy-start
  810.7 5.6 copy-start.2
  810.8 5.6 copy-start.11
  810.8 5.6 copy-start.16
  810.8 5.6 copy-start.18
  816.3 27.2 copy-start.6
  847.7 271.4 %reduce-scatter.21.cloned.1.call-start = ((), (), s32[]{:S(2)}) async-start(), calls=%async_computation.13 | async-start | bytes 1081344
  847.8 32.1 %copy-start.13 = (f32[2048]{0:T(1024)S(1)}, f32[2048]{0:T(1024)}, u32[]{:S(2)}) copy-start(f32[2048]{0:T(1024)} %copy-done.12) | copy-start | bytes 24580
  879.9 41.1 %copy-start.7 = (bf16[128,2048]{1,0:T(8,128)(2,1)S(1)}, bf16[128,2048]{1,0:T(8,128)(2,1)}, u32[]{:S(2)}) copy-start(bf16[128,2048]{1,0:T(8,128)(2,1)} %copy.89) | copy-start | bytes 1572868
  879.9 373.9 %reduce-scatter.23.cloned.1.call-start = ((), (), s32[]{:S(2)}) async-start(), calls=%async_computation.14 | async-start | bytes 1081344
  920.9 468.3 %reduce-scatter.19.cloned.1.call-start = ((), (), s32[]{:S(2)}) async-start(), calls=%async_computation.12 | async-start | bytes 1081344
  924.1 2062.6 %reduce-scatter.17.cloned.1.call-start = ((), (), s32[]{:S(2)}) async-start(), calls=%async_computation.11 | async-start | bytes 207618048 | tf_op jit(solution)/shard_map/reduce_scatter | solution.py:322
  1054.7 1.1 copy-start.3
  1054.8 1.8 copy-start.4
  1054.8 1.8 copy-start.9
  (1 other events, 0.7 us)
Sparse Core Ops, SparseCore 0:
  10.9 319.2 all-gather.5
  333.0 232.5 all-gather.11
  568.1 35.5 all-gather.9
  606.0 36.5 all-gather.7
  736.8 71.4 reduce-scatter.14
  847.9 136.5 reduce-scatter.24
  986.7 132.3 reduce-scatter.20
  1121.3 132.4 reduce-scatter.22
  1256.6 132.5 reduce-scatter.18
  1395.5 1591.1 reduce-scatter.16
where the time goes:
time: 3010 us; the launch traced here: 3000 us
  waiting for transfers between devices  2400 us (80%)
  matrix products  241 us (8%)
  other arithmetic  161 us (5%)
  local copies, waits for them, and re-layouts  90.6 us (3%)
  blocking collectives  88.1 us (3%)
    reduce_scatter x1, waiting for transfers between devices, on_device(): lax.psum_scatter(jnp.concatenate([in_term, out_term], 1), ('dp', 'ctx'),...  1600 us
    unnamed x14, waiting for transfers between devices  310 us
    all_gather x1, waiting for transfers between devices, on_device(): weight_piece = lax.all_gather(w_in_t, ('dp', 'ctx'), axis=1, tiled=True)  226 us
    all_gather x1, waiting for transfers between devices, on_device(): lax.all_gather((w_out_t, out_bias), ('dp', 'ctx'), axis=0, tiled=True)  202 us
    concatenate x1, other arithmetic, on_device(): jnp.concatenate([in_term, out_term], 1)  131 us
  transfers between devices with their start and end apart: 10, of which 9 were waited for; matrix products, arithmetic and copies ran while one was open for 12% of the time, Pallas kernels for 0%

commit v1 on v0

--- a/solution.py
+++ b/solution.py
@@ -115,7 +115,7 @@
     return (d_key.reshape(key_count, H * HD), d_value.reshape(key_count, H * HD))
 
 
-def on_device(
+def on_device_gathered(
     hidden_in, w_in_t, in_bias, ln_gain, ln_shift, w_out_t, out_bias, segment_ids, out_grad
 ):
     inputs = hidden_in[0].astype(jnp.float32)
@@ -352,6 +352,165 @@
     )
 
 
+AXES = ("dp", "ctx")
+
+
+def layer_norm_stats(inputs):
+    average = jnp.mean(inputs, -1, keepdims=True)
+    centred = inputs - average
+    inv_std = lax.rsqrt(jnp.mean(centred * centred, -1, keepdims=True) + epsilon)
+    return centred * inv_std, inv_std
+
+
+def exchange(blocks):
+    return lax.all_to_all(blocks, AXES, split_axis=0, concat_axis=0, tiled=True)
+
+
+def to_blocks(rows, parts, count, width):
+    depth = rows.shape[0]
+    return rows.reshape(depth, parts, count, width).transpose(2, 0, 1, 3).reshape(count, depth, parts * width)
+
+
+def from_blocks(blocks, parts, width):
+    count, depth, _ = blocks.shape
+    return blocks.reshape(count, depth, parts, width).transpose(1, 2, 0, 3).reshape(depth, parts * count * width)
+
+
+def attention(queries, keys, values, d_out, seg_all):
+    seq_len = seg_all.shape[1]
+    scaling = HD ** (-0.5)
+    index = jnp.arange(seq_len)
+    allowed = (seg_all[:, :, None] == seg_all[:, None, :]) & (index[:, None] >= index[None, :])[None]
+    scores = jnp.einsum("bqd,bkd->bqk", queries, keys, preferred_element_type=jnp.float32) * scaling
+    scores = jnp.where(allowed, scores, negative)
+    largest = jnp.max(scores, -1, keepdims=True)
+    weights = jnp.where(allowed, jnp.exp(scores - largest), 0.0)
+    weights = weights / jnp.sum(weights, -1, keepdims=True)
+    weights_low = weights.astype(jnp.bfloat16)
+    attended = jnp.einsum("bqk,bkd->bqd", weights_low, values, preferred_element_type=jnp.float32)
+    row_dots = jnp.sum(d_out.astype(jnp.float32) * attended, -1, keepdims=True)
+    d_weights = jnp.einsum("bqd,bkd->bqk", d_out, values, preferred_element_type=jnp.float32)
+    d_scores = (weights * (d_weights - row_dots)).astype(jnp.bfloat16)
+    d_query = jnp.einsum("bqk,bkd->bqd", d_scores, keys, preferred_element_type=jnp.float32) * scaling
+    d_key = jnp.einsum("bqk,bqd->bkd", d_scores, queries, preferred_element_type=jnp.float32) * scaling
+    d_value = jnp.einsum("bqk,bqd->bkd", weights_low, d_out, preferred_element_type=jnp.float32)
+    return attended, d_query, d_key, d_value
+
+
+def rotate_rows(rows, cosine, sine, direction):
+    half = ROT // 2
+    first, second = rows[:, :half], rows[:, half:ROT]
+    return jnp.concatenate(
+        [first * cosine - direction * second * sine, second * cosine + direction * first * sine, rows[:, ROT:]], 1
+    )
+
+
+def on_device(
+    hidden_in, w_in_t, in_bias, ln_gain, ln_shift, w_out_t, out_bias, segment_ids, out_grad
+):
+    devices = lax.axis_size("dp") * lax.axis_size("ctx")
+    me = lax.axis_index("dp") * lax.axis_size("ctx") + lax.axis_index("ctx")
+    tok_rows, model_width = hidden_in.shape[1:]
+    seq_len = segment_ids.shape[1]
+    tokens = devices * tok_rows
+    seqs = tokens // seq_len
+    own = model_width // devices
+    in_parts = in_bias.shape[0]
+    out_parts = w_out_t.shape[1] // model_width
+    w_in = exchange(to_blocks(w_in_t.T, in_parts, devices, own)).reshape(model_width, in_parts * own)
+    x_all = lax.all_gather(hidden_in[0], AXES, axis=0, tiled=True)
+    vectors = lax.all_gather(jnp.concatenate([ln_gain, ln_shift], 0), AXES, axis=1, tiled=True).astype(jnp.float32)
+    seg_all = lax.all_gather(segment_ids, "dp", axis=0, tiled=True)
+    w_out = exchange(to_blocks(w_out_t, out_parts, devices, own)).reshape(model_width, out_parts * own)
+    g_all = lax.all_gather(out_grad[0], AXES, axis=0, tiled=True)
+
+    index_all = jnp.arange(seq_len, dtype=jnp.int32)[None]
+    earlier = jnp.concatenate([seg_all[:, :1], seg_all[:, :-1]], 1)
+    begins = jnp.where((index_all == 0) | (seg_all != earlier), index_all, 0)
+    positions = (index_all - lax.cummax(begins, axis=1)).astype(jnp.float32).reshape(tokens)
+    half = ROT // 2
+    frequency = 10000.0 ** (-2.0 * jnp.arange(half, dtype=jnp.float32) / ROT)
+    angles = positions[:, None] * frequency[None, :]
+    cosine, sine = jnp.cos(angles), jnp.sin(angles)
+
+    hat_all, _ = layer_norm_stats(x_all.astype(jnp.float32))
+    normed = (hat_all * vectors[:1] + vectors[1:]).astype(jnp.bfloat16)
+    joint = jnp.dot(normed, w_in, preferred_element_type=jnp.float32)
+    joint = joint + in_bias.astype(jnp.float32).reshape(1, in_parts * own)
+    shape = (seqs, seq_len, HD)
+    queries = rotate_rows(joint[:, :own], cosine, sine, 1.0).astype(jnp.bfloat16)
+    keys = rotate_rows(joint[:, own : 2 * own], cosine, sine, 1.0).astype(jnp.bfloat16)
+    values = joint[:, 2 * own : 3 * own].astype(jnp.bfloat16)
+    pre_gelu = joint[:, 3 * own :]
+
+    d_joined = jnp.dot(g_all, w_out, preferred_element_type=jnp.float32)
+    d_attn = d_joined[:, :own].astype(jnp.bfloat16)
+    hidden, gelu_pull = jax.vjp(lambda t: jax.nn.gelu(t, approximate=True), pre_gelu)
+    d_pre = gelu_pull(d_joined[:, own:])[0]
+
+    attended, d_query, d_key, d_value = attention(
+        queries.reshape(shape), keys.reshape(shape), values.reshape(shape), d_attn.reshape(shape), seg_all
+    )
+    joined = jnp.concatenate([attended.reshape(tokens, own).astype(jnp.bfloat16), hidden.astype(jnp.bfloat16)], 1)
+
+    branch = lax.dot_general(joined, w_out, (((1,), (1,)), ((), ())), preferred_element_type=jnp.float32)
+    column = jnp.arange(model_width) // own
+    bias_row = jnp.where(column == me, jnp.tile(out_bias.astype(jnp.float32), devices), 0.0)
+    branch = (branch + bias_row[None]).astype(jnp.bfloat16)
+    branch_own = lax.psum_scatter(branch, AXES, scatter_dimension=0, tiled=True)
+    inputs = hidden_in[0].astype(jnp.float32)
+    result = (inputs + branch_own.astype(jnp.float32)).astype(jnp.bfloat16)
+
+    d_joint = jnp.concatenate(
+        [
+            rotate_rows(d_query.reshape(tokens, own), cosine, sine, -1.0),
+            rotate_rows(d_key.reshape(tokens, own), cosine, sine, -1.0),
+            d_value.reshape(tokens, own),
+            d_pre,
+        ],
+        1,
+    )
+    d_joint = d_joint.astype(jnp.bfloat16)
+    d_normed_part = lax.dot_general(
+        d_joint, w_in, (((1,), (1,)), ((), ())), preferred_element_type=jnp.float32
+    ).astype(jnp.bfloat16)
+    d_normed = lax.psum_scatter(d_normed_part, AXES, scatter_dimension=0, tiled=True).astype(jnp.float32)
+
+    grad_out_local = lax.dot_general(
+        g_all, joined, (((0,), (0,)), ((), ())), preferred_element_type=jnp.float32
+    ).astype(jnp.bfloat16)
+    grad_w_out = from_blocks(
+        exchange(grad_out_local.reshape(devices, own, out_parts * own)), out_parts, own
+    ).astype(jnp.float32)
+    grad_in_local = lax.dot_general(
+        normed, d_joint, (((0,), (0,)), ((), ())), preferred_element_type=jnp.float32
+    ).astype(jnp.bfloat16)
+    grad_w_in = from_blocks(
+        exchange(grad_in_local.reshape(devices, own, in_parts * own)), in_parts, own
+    ).astype(jnp.float32).T
+    grad_in_bias = jnp.sum(d_joint.astype(jnp.float32), 0).reshape(in_parts, own)
+    g_columns = lax.dynamic_slice_in_dim(g_all, me * own, own, 1)
+    grad_out_bias = jnp.sum(g_columns.astype(jnp.float32), 0)
+
+    hat, inv_std = layer_norm_stats(inputs)
+    pair = jnp.stack([jnp.sum(d_normed * hat, 0), jnp.sum(d_normed, 0)])
+    pair = lax.psum_scatter(pair, AXES, scatter_dimension=1, tiled=True)
+    d_hat = d_normed * vectors[:1]
+    d_input = inv_std * (
+        d_hat - jnp.mean(d_hat, -1, keepdims=True) - hat * jnp.mean(d_hat * hat, -1, keepdims=True)
+    ) + out_grad[0].astype(jnp.float32)
+    return (
+        result[None],
+        d_input[None],
+        grad_w_in,
+        grad_in_bias,
+        pair[:1],
+        pair[1:],
+        grad_w_out,
+        grad_out_bias,
+    )
+
+
 def solution(mesh):
     in_specs = (
         P("dp", "ctx", None),
@@ -374,6 +533,8 @@
         P(("dp", "ctx"), None),
         P(("dp", "ctx")),
     )
+    devices = mesh.shape["dp"] * mesh.shape["ctx"]
+    body = on_device if devices == H else on_device_gathered
     return jax.shard_map(
-        on_device, mesh=mesh, in_specs=in_specs, out_specs=out_specs, check_vma=False
-    )
+        body, mesh=mesh, in_specs=in_specs, out_specs=out_specs, check_vma=False
+    )

time: 3010 us -> 951 us (0.32)
  waiting for transfers between devices: 2400 us -> 533 us
  matrix products: 241 us -> 107 us
  other arithmetic: 161 us -> 56.6 us
  blocking collectives: 88.1 us -> 119 us
    reduce_scatter x2, waiting for transfers between devices: 1620 us -> 246 us  [the longest x1 195 us: on_device(): branch_own = lax.psum_scatter(branch, AXES, scatter_dimension=0, tiled=True)]
    all_gather x4 -> x2, waiting for transfers between devices: 469 us -> 35.5 us  [the longest x1 35.5 us: on_device(): g_all = lax.all_gather(out_grad[0], AXES, axis=0, tiled=True)]
    unnamed x14 -> x6, waiting for transfers between devices: 310 us -> 139 us
    concatenate x4 -> x1, other arithmetic: 132 us -> 2.87 us  [on_device(): jnp.concatenate([rotate_rows(d_query.reshape(tokens, own), cosine, sine,...]
    dot_general x19 -> x10, matrix products: 201 us -> 76.9 us  [the longest x1 14.6 us: on_device(): joint = jnp.dot(normed, w_in, preferred_element_type=jnp.float32)]
    all_to_all x0 -> x4, waiting for transfers between devices: none -> 113 us  [exchange(): return lax.all_to_all(blocks, AXES, split_axis=0, concat_axis=0, tiled=True)]
    all_gather x1 -> x2, blocking collectives: 42.6 us -> 119 us  [the longest x1 79.1 us: on_device(): seg_all = lax.all_gather(segment_ids, 'dp', axis=0, tiled=True)]
    unnamed x1 -> x0, blocking collectives: 45.4 us -> none
  transfers between devices with their start and end apart: 10 -> 9, of which waited for: 9 -> 7; matrix products, arithmetic and copies ran while one was open for 12% -> 18% of each run, Pallas kernels for 0% -> 0%
where the time goes in v1:
time: 951 us; the launch traced here: 942 us
  waiting for transfers between devices  533 us (56%)
  blocking collectives  119 us (13%)
  matrix products  107 us (11%)
  local copies, waits for them, and re-layouts  87.6 us (9%)
  other arithmetic  56.6 us (6%)
  starting transfers between devices  24.8 us (3%)
  between operations  14.7 us (2%)
    reduce_scatter x1, waiting for transfers between devices, on_device(): branch_own = lax.psum_scatter(branch, AXES, scatter_dimension=0, tiled=True)  195 us
    unnamed x6, waiting for transfers between devices  139 us
    all_to_all x4, waiting for transfers between devices, exchange(): return lax.all_to_all(blocks, AXES, split_axis=0, concat_axis=0, tiled=True)  113 us
    all_gather x1, blocking collectives, on_device(): seg_all = lax.all_gather(segment_ids, 'dp', axis=0, tiled=True)  79.1 us
    reduce_scatter x1, waiting for transfers between devices, on_device(): lax.psum_scatter(d_normed_part, AXES, scatter_dimension=0, tiled=True)  50.6 us
    all_gather x1, blocking collectives, on_device(): lax.all_gather(jnp.concatenate([ln_gain, ln_shift], 0), AXES, axis=1, til...  39.5 us
    all_gather x1, waiting for transfers between devices, on_device(): g_all = lax.all_gather(out_grad[0], AXES, axis=0, tiled=True)  35.5 us
    reshape x6, local copies, waits for them, and re-layouts, to_blocks(): rows.reshape(depth, parts, count, width).transpose(2, 0, 1, 3)  28.2 us
  transfers between devices with their start and end apart: 9, of which 7 were waited for; matrix products, arithmetic and copies ran while one was open for 18% of the time, Pallas kernels for 0%

profile of v1, /device:TPU:0, one launch (start us, length us, event | category | flops | bytes accessed | tf_op | source)
XLA Modules:
  0.0 942.4 jit_solution(9228138475681468545)
XLA Ops:
  8.7 6.0 reshape.195
  14.6 5.7 copy.233
  20.3 6.5 reshape.196
  26.9 7.4 all-to-all-start
  34.3 79.1 %all-gather.2 = s32[4,1,1024]{2,1,0:T(1,128)S(1)} all-gather(s32[1,1,1024]{2,1,0:T(1,128)S(1)} %bitcast.230), channel_id=1, replica_groups=mesh['dp'=4,'ctx'=8] {'dp'}, dimensions={0}, use_global_device_ids=true | all-gather | bytes 20480 | tf_op jit(solution)/shard_map/all_gather | solution.py:423
  115.2 39.5 %all-gather.3 = bf16[32,64,2]{1,2,0:T(2,128)(2,1)S(1)} all-gather(bf16[1,64,2]{1,2,0:T(2,128)(2,1)S(1)} %maximum_bitcast_fusion), channel_id=1, replica_groups=mesh['dp'=4,'ctx'=8] {'dp','ctx'}, dimensions={0}, use_global_device_ids=true | all-gather | bytes 8448 | tf_op jit(solution)/shard_map/all_gather | solution.py:422
  166.3 7.2 convert_reduce_fusion
  177.2 6.5 fusion.4
  183.7 9.8 %fusion.7 = bf16[4096,2048]{1,0:T(8,128)(2,1)} fusion(bf16[1,4096,2048]{2,1,0:T(8,128)(2,1)S(1)} %copy-done, f32[2048]{0:T(1024)S(1)} %bitcast.226, f32[2048]{0:T(1024)S(1)} %bitcast.217, f32[4096]{0:T(1024)S(1)} %add_rsqrt_fusion, f32[4096]{0:T(1024)S(1)} %broadcast_multiply_fusion), kind=kLoop, calls=%fused_computation.9 | loop fusion | flops 50331648 | bytes 33603584 | tf_op jit(solution)/shard_map/convert_element_type | solution.py:437
  196.5 14.6 %fusion.115 = (bf16[4096,448]{0,1:T(8,128)(2,1)}, f32[4096,448]{0,1:T(8,128)}) fusion(f32[448]{0:T(512)S(1)} %reshape.211, bf16[4096,2048]{1,0:T(8,128)(2,1)} %fusion.7, bf16[2048,448]{1,0:T(8,128)(2,1)} %bitcast.10), kind=kOutput, calls=%fused_computation.173 | convolution fusion | flops 7519862784 | bytes 29624064 | tf_op jit(solution)/shard_map/dot_general | solution.py:438
  213.2 45.1 %all-to-all-done.1 = bf16[32,64,320]{2,1,0:T(8,128)(2,1)S(1)} async-done(((bf16[32,64,320]{2,1,0:T(8,128)(2,1)}), bf16[32,64,320]{2,1,0:T(8,128)(2,1)S(1)}, u32[]{:S(2)}, u32[]{:S(2)}) %all-to-all-start.1) | async-done | bytes 1310752 | tf_op jit(solution)/shard_map/all_to_all | solution.py:366
  258.3 35.5 %all-gather.9.cloned.1.call-done = bf16[1,4096,2048]{2,1,0:T(8,128)(2,1)} async-done(((bf16[1,128,2048]{2,1,0:T(8,128)(2,1)}), bf16[1,4096,2048]{2,1,0:T(8,128)(2,1)}) %all-gather.9.cloned.1.call-update) | async-done | bytes 16777232 | tf_op jit(solution)/shard_map/all_gather | solution.py:425
  293.8 9.3 fusion.10
  307.9 16.8 %fusion.116 = (f32[4,1024]{1,0:T(4,128)S(1)}, f32[4,1024,1024]{1,2,0:T(8,128)}) fusion(s32[4,1024]{1,0:T(4,128)S(1)} %bitcast.223, pred[1024,1024]{0,1:T(8,128)(4,1)} %iota_compare_fusion, bf16[4,1024,64]{1,2,0:T(8,128)(2,1)S(1)} %get-tuple-element.31, bf16[4,1024,64]{1,2,0:T(8,128)(2,1)S(1)} %get-tuple-element.30), kind=kOutput, calls=%fused_computation.174 | convolution fusion | flops 574620672 | bytes 18907136 | tf_op jit(solution)/shard_map/sub | solution.py:387
  324.8 6.9 fusion.18
  336.0 7.3 multiply_convert_fusion
  357.2 14.1 %convolution_convert_fusion = bf16[4096,2048]{1,0:T(8,128)(2,1)} fusion(bf16[4096,448]{0,1:T(8,128)(2,1)S(1)} %fusion.34, bf16[2048,448]{1,0:T(8,128)(2,1)} %bitcast.10), kind=kOutput, calls=%fused_computation.19 | convolution fusion | flops 7524581376 | bytes 22282240 | tf_op jit(solution)/shard_map/dot_general | solution.py:474
  375.8 14.0 %add_convert_fusion = bf16[4096,2048]{1,0:T(8,128)(2,1)} fusion(f32[2048]{0:T(1024)S(1)} %fusion.107, bf16[2048,320]{1,0:T(8,128)(2,1)} %bitcast.208, bf16[4096,256]{0,1:T(8,128)(2,1)S(1)} %multiply_convert_fusion.1, bf16[4096,64]{0,1:T(8,128)(2,1)S(1)} %bitcast.215), kind=kOutput, calls=%fused_computation.10 | convolution fusion | flops 5390729216 | bytes 20717568 | tf_op jit(solution)/shard_map/dot_general | solution.py:456
  389.8 9.2 fusion.29
  404.2 13.4 %convolution_convert_fusion.1 = bf16[2048,448]{0,1:T(8,128)(2,1)} fusion(bf16[4096,448]{0,1:T(8,128)(2,1)} %copy-done.4, bf16[4096,2048]{1,0:T(8,128)(2,1)} %fusion.7), kind=kOutput, calls=%fused_computation.42 | convolution fusion | flops 7517110272 | bytes 22282240 | tf_op jit(solution)/shard_map/dot_general | solution.py:485
  421.5 28.6 %all-to-all-done.3 = bf16[32,64,320]{2,1,0:T(8,128)(2,1)S(1)} async-done(((bf16[32,64,320]{2,1,0:T(8,128)(2,1)}), bf16[32,64,320]{2,1,0:T(8,128)(2,1)S(1)}, u32[]{:S(2)}, u32[]{:S(2)}) %all-to-all-start.3) | async-done | bytes 1310752 | tf_op jit(solution)/shard_map/all_to_all | solution.py:366
  451.2 10.4 %all-to-all-start.2 = ((bf16[32,64,448]{2,1,0:T(8,128)(2,1)}), bf16[32,64,448]{2,1,0:T(8,128)(2,1)S(1)}, u32[]{:S(2)}, u32[]{:S(2)}) async-start(bf16[32,64,448]{2,1,0:T(8,128)(2,1)} %bitcast.189), calls=%async_computation.4 | async-start | bytes 4194304 | tf_op jit(solution)/shard_map/all_to_all | solution.py:366
  468.1 4.3 copy.175
  472.3 6.0 copy.176
  478.4 5.4 reshape.212
  483.8 38.8 %all-to-all-done.2 = bf16[32,64,448]{2,1,0:T(8,128)(2,1)S(1)} async-done(((bf16[32,64,448]{2,1,0:T(8,128)(2,1)}), bf16[32,64,448]{2,1,0:T(8,128)(2,1)S(1)}, u32[]{:S(2)}, u32[]{:S(2)}) %all-to-all-start.2) | async-done | bytes 1835040 | tf_op jit(solution)/shard_map/all_to_all | solution.py:366
  522.6 4.4 reshape.215
  527.0 10.7 %copy.173 = f32[64,7,32,64]{3,2,1,0:T(8,128)} copy(f32[64,7,32,64]{3,1,0,2:T(8,128)} %bitcast.183) | data formatting | bytes 7340032 | tf_op jit(solution)/shard_map/transpose | solution.py:490
  537.7 6.5 reshape.213
  544.2 50.6 %reduce-scatter.8.cloned.1.call-done = bf16[128,2048]{1,0:T(8,128)(2,1)} async-done(((bf16[4096,2048]{1,0:T(8,128)(2,1)}), bf16[128,2048]{1,0:T(8,128)(2,1)}) %reduce-scatter.8.cloned.1.call-update) | async-done | bytes 524304 | tf_op jit(solution)/shard_map/reduce_scatter | solution.py:477
  597.7 195.2 %reduce-scatter.6.cloned.1.call-done = bf16[128,2048]{1,0:T(8,128)(2,1)} async-done(((bf16[4096,2048]{1,0:T(8,128)(2,1)}), bf16[128,2048]{1,0:T(8,128)(2,1)}) %reduce-scatter.6.cloned.1.call-update) | async-done | bytes 524304 | tf_op jit(solution)/shard_map/reduce_scatter | solution.py:460
  795.9 137.5 %reduce-scatter.10.cloned.1.call-done = f32[64,2]{1,0:T(8,128)} async-done(((f32[2048,2]{1,0:T(8,128)}), f32[64,2]{1,0:T(8,128)}) %reduce-scatter.10.cloned.1.call-update) | async-done | bytes 528
  (125 shorter events, 75.3 us)
Async XLA Ops:
  7.2 159.1 %all-gather.7.cloned.1.call-start = ((), (), s32[]{:S(2)}) async-start(), calls=%async_computation.9 | async-start | bytes 17301504 | tf_op jit(solution)/shard_map/all_gather | solution.py:421
  7.9 285.9 %all-gather.9.cloned.1.call-start = ((), (), s32[]{:S(2)}) async-start(), calls=%async_computation.10 | async-start | bytes 17301504 | tf_op jit(solution)/shard_map/all_gather | solution.py:425
  20.3 13.9 %copy-start.12 = (bf16[7,64]{1,0:T(8,128)(2,1)S(1)}, bf16[7,64]{1,0:T(8,128)(2,1)}, u32[]{:S(2)}) copy-start(bf16[7,64]{1,0:T(8,128)(2,1)} %param.11) | copy-start | bytes 2692
  20.3 14.0 %copy-start.11 = (s32[1,1024]{1,0:T(1,128)S(1)}, s32[1,1024]{1,0:T(1,128)}, u32[]{:S(2)}) copy-start(s32[1,1024]{1,0:T(1,128)} %param.16) | copy-start | bytes 12292
  20.3 94.8 %copy-start.14 = (bf16[1,64]{1,0:T(2,128)(2,1)S(1)}, bf16[1,64]{1,0:T(2,128)(2,1)}, u32[]{:S(2)}) copy-start(bf16[1,64]{1,0:T(2,128)(2,1)} %param.13) | copy-start | bytes 388
  20.3 94.8 %copy-start.15 = (bf16[1,64]{1,0:T(2,128)(2,1)S(1)}, bf16[1,64]{1,0:T(2,128)(2,1)}, u32[]{:S(2)}) copy-start(bf16[1,64]{1,0:T(2,128)(2,1)} %param.12) | copy-start | bytes 388
  20.3 134.5 %copy-start.7 = (bf16[64,10240]{1,0:T(8,128)(2,1)S(1)}, bf16[64,10240]{1,0:T(8,128)(2,1)}, u32[]{:S(2)}) copy-start(bf16[64,10240]{1,0:T(8,128)(2,1)} %param.14) | copy-start | bytes 3932164
  26.9 166.7 %all-to-all-start = ((bf16[32,64,448]{2,1,0:T(8,128)(2,1)}), bf16[32,64,448]{2,1,0:T(8,128)(2,1)}, u32[]{:S(2)}, u32[]{:S(2)}) async-start(bf16[32,64,448]{2,1,0:T(8,128)(2,1)} %reshape.196), calls=%async_computation | async-start | bytes 4194304 | tf_op jit(solution)/shard_map/all_to_all | solution.py:366
  166.2 17.5 %copy-start.9 = (f32[1,2048]{1,0:T(1,128)}, f32[1,2048]{1,0:T(1,128)S(1)}, u32[]{:S(2)}) copy-start(f32[1,2048]{1,0:T(1,128)S(1)} %get-tuple-element.24) | copy-start | bytes 24580
  166.3 10.9 %copy-start = (bf16[1,4096,2048]{2,1,0:T(8,128)(2,1)S(1)}, bf16[1,4096,2048]{2,1,0:T(8,128)(2,1)}, u32[]{:S(2)}) copy-start(bf16[1,4096,2048]{2,1,0:T(8,128)(2,1)} %all-gather.7.cloned.1.call-done) | copy-start | bytes 50331652
  193.5 64.8 %all-to-all-start.1 = ((bf16[32,64,320]{2,1,0:T(8,128)(2,1)}), bf16[32,64,320]{2,1,0:T(8,128)(2,1)S(1)}, u32[]{:S(2)}, u32[]{:S(2)}) async-start(bf16[32,64,320]{2,1,0:T(8,128)(2,1)} %copy.160), calls=%async_computation.1 | async-start | bytes 3145728 | tf_op jit(solution)/shard_map/all_to_all | solution.py:366
  196.2 398.5 %reduce-scatter.8.cloned.1.call-start = ((), (), s32[]{:S(2)}) async-start(), calls=%async_computation.8 | async-start | bytes 17301504 | tf_op jit(solution)/shard_map/reduce_scatter | solution.py:477
  258.3 44.8 %copy-start.6 = (bf16[32,64,320]{2,1,0:T(8,128)(2,1)}, bf16[32,64,320]{2,1,0:T(8,128)(2,1)S(1)}, u32[]{:S(2)}) copy-start(bf16[32,64,320]{2,1,0:T(8,128)(2,1)S(1)} %all-to-all-done.1) | copy-start | bytes 3932164
  303.1 2.3 copy-start.3
  343.3 9.2 slice-start.2
  346.0 6.5 slice-start
  346.0 6.5 slice-start.3
  347.6 4.9 slice-start.1
  355.4 1.8 copy-start.4
  371.3 0.7 copy-start.13
  371.4 421.6 %reduce-scatter.6.cloned.1.call-start = ((), (), s32[]{:S(2)}) async-start(), calls=%async_computation.7 | async-start | bytes 17301504 | tf_op jit(solution)/shard_map/reduce_scatter | solution.py:460
  372.1 3.7 copy-start.8
  400.6 49.5 %all-to-all-start.3 = ((bf16[32,64,320]{2,1,0:T(8,128)(2,1)}), bf16[32,64,320]{2,1,0:T(8,128)(2,1)S(1)}, u32[]{:S(2)}, u32[]{:S(2)}) async-start(bf16[32,64,320]{2,1,0:T(8,128)(2,1)} %bitcast.25), calls=%async_computation.5 | async-start | bytes 3145728 | tf_op jit(solution)/shard_map/all_to_all | solution.py:366
  417.6 44.3 %copy-start.1 = (bf16[1,128,2048]{2,1,0:T(8,128)(2,1)S(1)}, bf16[1,128,2048]{2,1,0:T(8,128)(2,1)}, u32[]{:S(2)}) copy-start(bf16[1,128,2048]{2,1,0:T(8,128)(2,1)} %param.9) | copy-start | bytes 1572868
  450.1 1.1 copy-start.2
  451.2 71.4 %all-to-all-start.2 = ((bf16[32,64,448]{2,1,0:T(8,128)(2,1)}), bf16[32,64,448]{2,1,0:T(8,128)(2,1)S(1)}, u32[]{:S(2)}, u32[]{:S(2)}) async-start(bf16[32,64,448]{2,1,0:T(8,128)(2,1)} %bitcast.189), calls=%async_computation.4 | async-start | bytes 4194304 | tf_op jit(solution)/shard_map/all_to_all | solution.py:366
  461.6 471.8 %reduce-scatter.10.cloned.1.call-start = ((), (), s32[]{:S(2)}) async-start(), calls=%async_computation.11 | async-start | bytes 1081344
  537.7 57.1 %copy-start.10 = (f32[1,2048]{1,0:T(1,128)S(1)}, f32[1,2048]{1,0:T(1,128)}, u32[]{:S(2)}) copy-start(f32[1,2048]{1,0:T(1,128)} %copy-done.9) | copy-start | bytes 24580
  537.7 255.3 %copy-start.5 = (bf16[1,128,2048]{2,1,0:T(8,128)(2,1)S(1)}, bf16[1,128,2048]{2,1,0:T(8,128)(2,1)}, u32[]{:S(2)}) copy-start(bf16[1,128,2048]{2,1,0:T(8,128)(2,1)} %param.17) | copy-start | bytes 1572868
Sparse Core Ops, SparseCore 0:
  10.8 145.6 all-gather.6
  159.4 134.3 all-gather.8
  371.5 223.2 reduce-scatter.7
  596.9 195.9 reduce-scatter.5
  795.0 138.2 reduce-scatter.9

commit v2 on v1

--- a/solution.py
+++ b/solution.py
@@ -1,8 +1,11 @@
+import functools
 import math
 
 import jax
 import jax.numpy as jnp
 from jax import lax
+from jax.experimental import pallas as pl
+from jax.experimental.pallas import tpu as pltpu
 from jax.sharding import PartitionSpec as P
 
 H = 32
@@ -353,6 +356,342 @@
 
 
 AXES = ("dp", "ctx")
+MESH = pl.DeviceIdType.MESH
+class Place:
+    def __init__(self, depth):
+        self.depth = depth
+        self.z = lax.axis_index("dp")
+        self.c = lax.axis_index("ctx")
+        y, x, self.core = self.c // 4, (self.c // 2) % 2, self.c % 2
+        self.first_stride = jnp.where(self.core == 0, 2, 4)
+        self.last_stride = jnp.where(self.core == 0, 4, 2)
+        self.f = jnp.where(self.core == 0, x, y)
+        self.l = jnp.where(self.core == 0, y, x)
+
+    def ctx(self, f, l, core):
+        return f * self.first_stride + l * self.last_stride + core
+
+    def shard(self, z, f, l, core):
+        return z * 8 + self.ctx(f, l, core)
+
+    def first(self):
+        return {"dp": self.z, "ctx": self.ctx(1 - self.f, self.l, self.core)}
+
+    def last(self):
+        return {"dp": self.z, "ctx": self.ctx(self.f, 1 - self.l, self.core)}
+
+    def sibling(self):
+        return {"dp": self.z, "ctx": self.ctx(self.f, self.l, 1 - self.core)}
+
+    def above(self):
+        return {"dp": self.z + 1, "ctx": self.c}
+
+    def below(self):
+        return {"dp": self.z - 1, "ctx": self.c}
+
+    def greet(self):
+        barrier = pltpu.get_barrier_semaphore()
+        for device in (self.first(), self.last(), self.sibling()):
+            pl.semaphore_signal(barrier, inc=1, device_id=device, device_id_type=MESH)
+
+        @pl.when(self.z > 0)
+        def _():
+            pl.semaphore_signal(barrier, inc=1, device_id=self.below(), device_id_type=MESH)
+
+        @pl.when(self.z < self.depth - 1)
+        def _():
+            pl.semaphore_signal(barrier, inc=1, device_id=self.above(), device_id_type=MESH)
+
+        ends = jnp.where(self.z > 0, 1, 0) + jnp.where(self.z < self.depth - 1, 1, 0)
+        pl.semaphore_wait(barrier, 3 + ends)
+
+
+def push(source, target, send, receive, device):
+    return pltpu.make_async_remote_copy(
+        src_ref=source, dst_ref=target, send_sem=send, recv_sem=receive, device_id=device, device_id_type=MESH
+    )
+
+
+def gather_kernel(depth, rows, own_ref, all_ref, local, sends, arrivals):
+    me = Place(depth)
+    last = depth - 1
+
+    def block(shard):
+        return all_ref.at[pl.ds(pl.multiple_of(shard * rows, rows), rows)]
+
+    def send(source, shard, slot, device):
+        push(source, block(shard), sends.at[slot], arrivals.at[shard], device).start()
+
+    def drained(slot):
+        push(own_ref, block(0), sends.at[slot], arrivals.at[0], me.sibling()).wait_send()
+
+    def arrived(shard):
+        push(own_ref, block(shard), sends.at[0], arrivals.at[shard], me.sibling()).wait_recv()
+
+    me.greet()
+    mine = me.shard(me.z, me.f, me.l, me.core)
+    keep = pltpu.make_async_copy(own_ref, block(mine), local)
+    send(own_ref, mine, 0, me.first())
+
+    def spread(source, shard, base):
+        @pl.when(me.z < last)
+        def _():
+            send(source, shard, base, me.above())
+
+        @pl.when(me.z > 0)
+        def _():
+            send(source, shard, base + 1, me.below())
+
+        send(source, shard, base + 2, me.last())
+        send(source, shard, base + 3, me.sibling())
+
+    spread(own_ref, mine, 1)
+    keep.start()
+    other = me.shard(me.z, 1 - me.f, me.l, me.core)
+    arrived(other)
+    spread(block(other), other, 5)
+
+    def level(step):
+        near = []
+        for z in range(depth):
+            order = sorted([q for q in range(depth) if q != z], key=lambda q: (abs(q - z), q))
+            near.append(order)
+        value = jnp.int32(0)
+        for z in range(depth):
+            value = jnp.where(me.z == z, near[z][step], value)
+        return value
+
+    def relay(shard, from_z, base):
+        arrived(shard)
+
+        @pl.when((from_z < me.z) & (me.z < last))
+        def _():
+            send(block(shard), shard, base, me.above())
+
+        @pl.when((from_z > me.z) & (me.z > 0))
+        def _():
+            send(block(shard), shard, base, me.below())
+
+        send(block(shard), shard, base + 1, me.last())
+        send(block(shard), shard, base + 2, me.sibling())
+
+    def cross(z, f, slot):
+        shard = me.shard(z, f, 1 - me.l, me.core)
+        arrived(shard)
+        send(block(shard), shard, slot, me.sibling())
+
+    base = 9
+    cross(me.z, me.f, base)
+    base += 1
+    pending = (me.z, 1 - me.f)
+    for step in range(last):
+        z = level(step)
+        for f in (me.f, 1 - me.f):
+            relay(me.shard(z, f, me.l, me.core), z, base)
+            base += 3
+            cross(*pending, base)
+            base += 1
+            pending = (z, f)
+    cross(*pending, base)
+    base += 1
+    for z in range(depth):
+        for f in range(2):
+            for l in range(2):
+                arrived(me.shard(z, f, l, 1 - me.core))
+    keep.wait()
+    drained(0)
+    for start in (1, 5):
+
+        @pl.when(me.z < last)
+        def _():
+            drained(start)
+
+        @pl.when(me.z > 0)
+        def _():
+            drained(start + 1)
+
+        drained(start + 2)
+        drained(start + 3)
+    slot = 9
+    drained(slot)
+    slot += 1
+    for step in range(last):
+        z = level(step)
+        for _ in range(2):
+
+            @pl.when(((z < me.z) & (me.z < last)) | ((z > me.z) & (me.z > 0)))
+            def _():
+                drained(slot)
+
+            drained(slot + 1)
+            drained(slot + 2)
+            drained(slot + 3)
+            slot += 4
+    drained(slot)
+
+
+def gather_all(own, depth, collective_id):
+    rows, width = own.shape
+    devices = depth * 8
+    slots = 9 + 1 + 8 * (depth - 1) + 1
+    return pl.pallas_call(
+        functools.partial(gather_kernel, depth, rows),
+        out_shape=jax.ShapeDtypeStruct((devices * rows, width), own.dtype),
+        in_specs=[pl.BlockSpec(memory_space=pl.ANY)],
+        out_specs=pl.BlockSpec(memory_space=pl.ANY),
+        scratch_shapes=[
+            pltpu.SemaphoreType.DMA(()),
+            pltpu.SemaphoreType.DMA((slots,)),
+            pltpu.SemaphoreType.DMA((devices,)),
+        ],
+        compiler_params=pltpu.CompilerParams(collective_id=collective_id, has_side_effects=True),
+    )(own)
+
+
+def add_into(target, source, rows, step):
+    @pl.loop(0, rows // step)
+    def _(i):
+        part = pl.ds(pl.multiple_of(i * step, step), step)
+        target[part, :] = (target[part, :].astype(jnp.float32) + source[part, :].astype(jnp.float32)).astype(
+            target.dtype
+        )
+
+
+def scatter_kernel(depth, rows, part_ref, out_ref, sums, from_sib, from_last, from_below, from_above, from_first,
+                   loads, send_sib, send_last, send_line, send_first, got_sib, got_last, got_below, got_above, got_first):
+    me = Place(depth)
+    last = depth - 1
+    step = min(rows, 16)
+
+    def source(z, f, l, core):
+        return part_ref.at[pl.ds(pl.multiple_of(me.shard(z, f, l, core) * rows, rows), rows)]
+
+    def at(z, f, l):
+        return z * 4 + f * 2 + l
+
+    def order(i):
+        value = jnp.int32(0)
+        for z in range(depth):
+            far = [q for q in range(depth - 1, z, -1)] + [q for q in range(z)] if 2 * z < depth else [q for q in range(z)] + [q for q in range(depth - 1, z, -1)]
+            value = jnp.where(me.z == z, (far + [z])[i], value)
+        return value
+
+    me.greet()
+    pairs = [(f, l) for l in (1 - me.l, me.l) for f in (1 - me.f, me.f)]
+    for i in range(depth):
+        z = order(i)
+        for f in (1 - me.f, me.f):
+            for l in (1 - me.l, me.l):
+                push(source(z, f, l, 1 - me.core), from_sib.at[at(z, l, f)], send_sib.at[at(z, f, l)], got_sib.at[at(z, l, f)], me.sibling()).start()
+        for f, l in pairs:
+            pltpu.make_async_copy(source(z, f, l, me.core), sums.at[at(z, f, l)], loads.at[at(z, f, l)]).start()
+
+    def chip(i):
+        z = order(i)
+        for n, (f, l) in enumerate(pairs):
+            k = at(z, f, l)
+            pltpu.make_async_copy(source(z, f, l, me.core), sums.at[k], loads.at[k]).wait()
+            push(source(z, f, l, me.core), from_sib.at[k], send_sib.at[k], got_sib.at[k], me.sibling()).wait_recv()
+            add_into(sums.at[k], from_sib.at[k], rows, step)
+            if n in (1, 2):
+                f0 = pairs[n - 1][0]
+                push(sums.at[at(z, f0, 1 - me.l)], from_last.at[z * 2 + f0], send_last.at[z * 2 + f0], got_last.at[z * 2 + f0], me.last()).start()
+
+    def up(z, f):
+        return push(sums.at[at(z, f, me.l)], from_below.at[z * 2 + f], send_line.at[z * 2 + f], got_below.at[z * 2 + f], me.above())
+
+    def down(z, f):
+        return push(sums.at[at(z, f, me.l)], from_above.at[z * 2 + f], send_line.at[z * 2 + f], got_above.at[z * 2 + f], me.below())
+
+    def plane(i):
+        z = order(i)
+        for f in (1 - me.f, me.f):
+            k = at(z, f, me.l)
+            push(sums.at[k], from_last.at[z * 2 + f], send_last.at[z * 2 + f], got_last.at[z * 2 + f], me.last()).wait_recv()
+            add_into(sums.at[k], from_last.at[z * 2 + f], rows, step)
+        for f in (1 - me.f, me.f):
+            k = at(z, f, me.l)
+            if i < last:
+
+                @pl.when((z > me.z) & (me.z > 0))
+                def _():
+                    up(z, f).wait_recv()
+                    add_into(sums.at[k], from_below.at[z * 2 + f], rows, step)
+
+                @pl.when((z < me.z) & (me.z < last))
+                def _():
+                    down(z, f).wait_recv()
+                    add_into(sums.at[k], from_above.at[z * 2 + f], rows, step)
+
+                @pl.when(z > me.z)
+                def _():
+                    up(z, f).start()
+
+                @pl.when(z < me.z)
+                def _():
+                    down(z, f).start()
+            else:
+
+                @pl.when(me.z > 0)
+                def _():
+                    up(z, f).wait_recv()
+                    add_into(sums.at[k], from_below.at[z * 2 + f], rows, step)
+
+                @pl.when(me.z < last)
+                def _():
+                    down(z, f).wait_recv()
+                    add_into(sums.at[k], from_above.at[z * 2 + f], rows, step)
+
+    chip(0)
+    for i in range(1, depth):
+        chip(i)
+        plane(i - 1)
+    plane(last)
+    give = push(sums.at[at(me.z, 1 - me.f, me.l)], from_first, send_first, got_first, me.first())
+    give.start()
+    give.wait_recv()
+    mine = sums.at[at(me.z, me.f, me.l)]
+
+    @pl.loop(0, rows // step)
+    def _(i):
+        part = pl.ds(pl.multiple_of(i * step, step), step)
+        out_ref[part, :] = (mine[part, :].astype(jnp.float32) + from_first[part, :].astype(jnp.float32)).astype(out_ref.dtype)
+
+    give.wait_send()
+    for i in range(depth):
+        z = order(i)
+        for f, l in pairs:
+            k = at(z, f, l)
+            push(source(z, f, l, 1 - me.core), from_sib.at[k], send_sib.at[k], got_sib.at[k], me.sibling()).wait_send()
+        for f in (1 - me.f, me.f):
+            push(sums.at[at(z, f, 1 - me.l)], from_last.at[z * 2 + f], send_last.at[z * 2 + f], got_last.at[z * 2 + f], me.last()).wait_send()
+            if i < last:
+                up(z, f).wait_send()
+
+
+def scatter_sum(part, depth, collective_id, out_dtype):
+    tokens, width = part.shape
+    devices = depth * 8
+    rows = tokens // devices
+    shard = (rows, width)
+    dma = pltpu.SemaphoreType.DMA
+    return pl.pallas_call(
+        functools.partial(scatter_kernel, depth, rows),
+        out_shape=jax.ShapeDtypeStruct(shard, out_dtype),
+        in_specs=[pl.BlockSpec(memory_space=pl.ANY)],
+        out_specs=pl.BlockSpec(memory_space=pltpu.VMEM),
+        scratch_shapes=[
+            pltpu.VMEM((depth * 4, *shard), part.dtype),
+            pltpu.VMEM((depth * 4, *shard), part.dtype),
+            pltpu.VMEM((depth * 2, *shard), part.dtype),
+            pltpu.VMEM((depth * 2, *shard), part.dtype),
+            pltpu.VMEM((depth * 2, *shard), part.dtype),
+            pltpu.VMEM(shard, part.dtype),
+            dma((depth * 4,)), dma((depth * 4,)), dma((depth * 2,)), dma((depth * 2,)), dma(()),
+            dma((depth * 4,)), dma((depth * 2,)), dma((depth * 2,)), dma((depth * 2,)), dma(()),
+        ],
+        compiler_params=pltpu.CompilerParams(collective_id=collective_id, has_side_effects=True, vmem_limit_bytes=60 << 20),
+    )(part)
 
 
 def layer_norm_stats(inputs):
@@ -408,20 +747,32 @@
 def on_device(
     hidden_in, w_in_t, in_bias, ln_gain, ln_shift, w_out_t, out_bias, segment_ids, out_grad
 ):
-    devices = lax.axis_size("dp") * lax.axis_size("ctx")
-    me = lax.axis_index("dp") * lax.axis_size("ctx") + lax.axis_index("ctx")
+    depth = lax.axis_size("dp")
+    devices = depth * lax.axis_size("ctx")
+    ctx = lax.axis_index("ctx")
+    me = lax.axis_index("dp") * lax.axis_size("ctx") + ctx
     tok_rows, model_width = hidden_in.shape[1:]
     seq_len = segment_ids.shape[1]
     tokens = devices * tok_rows
     seqs = tokens // seq_len
     own = model_width // devices
     in_parts = in_bias.shape[0]
+    in_width = in_parts * own
     out_parts = w_out_t.shape[1] // model_width
-    w_in = exchange(to_blocks(w_in_t.T, in_parts, devices, own)).reshape(model_width, in_parts * own)
-    x_all = lax.all_gather(hidden_in[0], AXES, axis=0, tiled=True)
-    vectors = lax.all_gather(jnp.concatenate([ln_gain, ln_shift], 0), AXES, axis=1, tiled=True).astype(jnp.float32)
-    seg_all = lax.all_gather(segment_ids, "dp", axis=0, tiled=True)
-    w_out = exchange(to_blocks(w_out_t, out_parts, devices, own)).reshape(model_width, out_parts * own)
+    out_width = out_parts * own
+    own_seg = lax.dynamic_slice_in_dim(segment_ids[0], ctx * tok_rows, tok_rows)
+    extra = jnp.concatenate(
+        [ln_gain.T, ln_shift.T, own_seg.astype(jnp.bfloat16).reshape(own, tok_rows // own)], 1
+    )
+    extra = jnp.broadcast_to(extra[None], (devices, *extra.shape))
+    in_blocks = jnp.concatenate([to_blocks(w_in_t.T, in_parts, devices, own), extra], 2)
+    in_got = exchange(in_blocks)
+    w_in = in_got[:, :, :in_width].reshape(model_width, in_width)
+    gain = in_got[:, :, in_width].reshape(1, model_width).astype(jnp.float32)
+    shift = in_got[:, :, in_width + 1].reshape(1, model_width).astype(jnp.float32)
+    seg_all = in_got[:, :, in_width + 2 :].astype(jnp.int32).reshape(seqs, seq_len)
+    w_out = exchange(to_blocks(w_out_t, out_parts, devices, own)).reshape(model_width, out_width)
+    x_all = gather_all(hidden_in[0], depth, 0)
     g_all = lax.all_gather(out_grad[0], AXES, axis=0, tiled=True)
 
     index_all = jnp.arange(seq_len, dtype=jnp.int32)[None]
@@ -434,9 +785,9 @@
     cosine, sine = jnp.cos(angles), jnp.sin(angles)
 
     hat_all, _ = layer_norm_stats(x_all.astype(jnp.float32))
-    normed = (hat_all * vectors[:1] + vectors[1:]).astype(jnp.bfloat16)
+    normed = (hat_all * gain + shift).astype(jnp.bfloat16)
     joint = jnp.dot(normed, w_in, preferred_element_type=jnp.float32)
-    joint = joint + in_bias.astype(jnp.float32).reshape(1, in_parts * own)
+    joint = joint + in_bias.astype(jnp.float32).reshape(1, in_width)
     shape = (seqs, seq_len, HD)
     queries = rotate_rows(joint[:, :own], cosine, sine, 1.0).astype(jnp.bfloat16)
     keys = rotate_rows(joint[:, own : 2 * own], cosine, sine, 1.0).astype(jnp.bfloat16)
@@ -474,28 +825,35 @@
     d_normed_part = lax.dot_general(
         d_joint, w_in, (((1,), (1,)), ((), ())), preferred_element_type=jnp.float32
     ).astype(jnp.bfloat16)
-    d_normed = lax.psum_scatter(d_normed_part, AXES, scatter_dimension=0, tiled=True).astype(jnp.float32)
 
     grad_out_local = lax.dot_general(
         g_all, joined, (((0,), (0,)), ((), ())), preferred_element_type=jnp.float32
     ).astype(jnp.bfloat16)
-    grad_w_out = from_blocks(
-        exchange(grad_out_local.reshape(devices, own, out_parts * own)), out_parts, own
-    ).astype(jnp.float32)
+    grad_w_out = from_blocks(exchange(grad_out_local.reshape(devices, own, out_width)), out_parts, own).astype(
+        jnp.float32
+    )
     grad_in_local = lax.dot_general(
         normed, d_joint, (((0,), (0,)), ((), ())), preferred_element_type=jnp.float32
-    ).astype(jnp.bfloat16)
-    grad_w_in = from_blocks(
-        exchange(grad_in_local.reshape(devices, own, in_parts * own)), in_parts, own
-    ).astype(jnp.float32).T
-    grad_in_bias = jnp.sum(d_joint.astype(jnp.float32), 0).reshape(in_parts, own)
+    )
+    joint_sums = jnp.sum(d_joint.astype(jnp.float32), 0)
+    grad_in_bias = joint_sums.reshape(in_parts, own)
+    weight_in = w_in.astype(jnp.float32)
+    shift_part = jnp.sum(weight_in * joint_sums[None], 1)
+    gain_part = (jnp.sum(weight_in * grad_in_local, 1) - shift[0] * shift_part) / gain[0]
+    back = jnp.concatenate(
+        [grad_in_local.astype(jnp.bfloat16), gain_part[:, None].astype(jnp.bfloat16), shift_part[:, None].astype(jnp.bfloat16)], 1
+    )
+    back = exchange(back.reshape(devices, own, in_width + 2))
+    grad_w_in = from_blocks(back[:, :, :in_width], in_parts, own).astype(jnp.float32).T
+    grad_gain, grad_shift = [
+        jnp.sum(back[:, :, in_width + i].astype(jnp.float32), 0, keepdims=True) for i in range(2)
+    ]
     g_columns = lax.dynamic_slice_in_dim(g_all, me * own, own, 1)
     grad_out_bias = jnp.sum(g_columns.astype(jnp.float32), 0)
 
+    d_normed = scatter_sum(d_normed_part, depth, 1, jnp.float32)
     hat, inv_std = layer_norm_stats(inputs)
-    pair = jnp.stack([jnp.sum(d_normed * hat, 0), jnp.sum(d_normed, 0)])
-    pair = lax.psum_scatter(pair, AXES, scatter_dimension=1, tiled=True)
-    d_hat = d_normed * vectors[:1]
+    d_hat = d_normed * gain
     d_input = inv_std * (
         d_hat - jnp.mean(d_hat, -1, keepdims=True) - hat * jnp.mean(d_hat * hat, -1, keepdims=True)
     ) + out_grad[0].astype(jnp.float32)
@@ -504,8 +862,8 @@
         d_input[None],
         grad_w_in,
         grad_in_bias,
-        pair[:1],
-        pair[1:],
+        grad_gain,
+        grad_shift,
         grad_w_out,
         grad_out_bias,
     )
@@ -533,8 +891,8 @@
         P(("dp", "ctx"), None),
         P(("dp", "ctx")),
     )
-    devices = mesh.shape["dp"] * mesh.shape["ctx"]
-    body = on_device if devices == H else on_device_gathered
+    tensor_parallel = mesh.shape["ctx"] == 8 and mesh.shape["dp"] * 8 == H
+    body = on_device if tensor_parallel else on_device_gathered
     return jax.shard_map(
         body, mesh=mesh, in_specs=in_specs, out_specs=out_specs, check_vma=False
     )

time: 951 us -> 699 us (0.74)
  the two profiles are of different devices: /device:TPU:0 before, /device:TPU:17 now
where the time goes in v2:
time: 699 us; the launch traced here: 691 us
  Pallas kernels  326 us (47%)
  matrix products  117 us (17%)
  local copies, waits for them, and re-layouts  101 us (14%)
  other arithmetic  84.4 us (12%)
  starting transfers between devices  39.7 us (6%)
  between operations  14.7 us (2%)
  waiting for transfers between devices  8.39 us (1%)
    pallas_call x1, Pallas kernels, scatter_sum(): pl.pallas_call(functools.partial(scatter_kernel, depth, rows), out_shape=...  168 us
    pallas_call x1, Pallas kernels, gather_all(): pl.pallas_call(functools.partial(gather_kernel, depth, rows), out_shape=j...  158 us
    all_to_all x4, starting transfers between devices, exchange(): return lax.all_to_all(blocks, AXES, split_axis=0, concat_axis=0, tiled=True)  39.1 us
    reshape x6, local copies, waits for them, and re-layouts, to_blocks(): rows.reshape(depth, parts, count, width).transpose(2, 0, 1, 3)  29.6 us
    transpose x3, local copies, waits for them, and re-layouts, on_device(): from_blocks(back[:, :, :in_width], in_parts, own).astype(jnp.float32)  24.3 us
    sub x1, matrix products, attention(): weights = jnp.where(allowed, jnp.exp(scores - largest), 0.0)  16.8 us
    convert_element_type x1, other arithmetic, on_device(): normed = (hat_all * gain + shift).astype(jnp.bfloat16)  16.4 us
    convert_element_type x3, local copies, waits for them, and re-layouts, on_device(): from_blocks(exchange(grad_out_local.reshape(devices, own, out_width)), ou...  15.7 us
  transfers between devices with their start and end apart: 6, of which 1 were waited for; matrix products, arithmetic and copies ran while one was open for 39% of the time, Pallas kernels for 47%

profile of v2, /device:TPU:17, one launch (start us, length us, event | category | flops | bytes accessed | tf_op | source)
XLA Modules:
  0.0 690.6 jit_solution(18075281874289348246)
XLA Ops:
  10.3 6.0 reshape.266
  16.2 5.6 copy.348
  21.8 5.3 reshape.267
  29.1 6.1 all-to-all-start
  39.1 4.9 copy.277
  48.2 158.0 %shard_map.152 = bf16[4096,2048]{1,0:T(8,128)(2,1)} custom-call(bf16[128,2048]{1,0:T(8,128)(2,1)} %bitcast.144), custom_call_target="tpu_custom_call" | custom-call | tf_op jit(solution)/shard_map/pallas_call | solution.py:537
  207.6 7.1 %convert_reduce_fusion = f32[4096]{0:T(1024)S(1)} fusion(bf16[4096,2048]{1,0:T(8,128)(2,1)} %shard_map.152), kind=kLoop, calls=%fused_computation.2 | loop fusion | flops 16773120 | bytes 16793600 | tf_op jit(solution)/shard_map/reduce_sum | solution.py:698
  218.2 6.5 fusion.3
  224.8 17.9 %all-to-all-start.1 = ((bf16[32,64,320]{2,1,0:T(8,128)(2,1)}), bf16[32,64,320]{2,1,0:T(8,128)(2,1)}, u32[]{:S(2)}, u32[]{:S(2)}) async-start(bf16[32,64,320]{2,1,0:T(8,128)(2,1)} %copy.278), calls=%async_computation.1 | async-start | bytes 3145728 | tf_op jit(solution)/shard_map/all_to_all | solution.py:705
  247.8 16.4 %fusion.6 = bf16[4096,2048]{1,0:T(8,128)(2,1)} fusion(bf16[4096,2048]{1,0:T(8,128)(2,1)} %shard_map.152, f32[2048]{0:T(1024)S(1)} %reshape.282, f32[2048]{0:T(1024)S(1)} %reshape.281, f32[4096]{0:T(1024)S(1)} %add_rsqrt_fusion, f32[4096]{0:T(1024)S(1)} %broadcast_multiply_fusion), kind=kLoop, calls=%fused_computation.8 | loop fusion | flops 50331648 | bytes 33603584 | tf_op jit(solution)/shard_map/convert_element_type | solution.py:788
  264.2 13.9 %fusion.112 = (bf16[4096,448]{0,1:T(8,128)(2,1)}, f32[4096,448]{0,1:T(8,128)}) fusion(f32[448]{0:T(512)S(1)} %reshape.283, bf16[4096,2048]{1,0:T(8,128)(2,1)} %fusion.6, bf16[2048,448]{1,0:T(8,128)(2,1)S(1)} %bitcast.139), kind=kOutput, calls=%fused_computation.177 | convolution fusion | flops 7519862784 | bytes 29624064 | tf_op jit(solution)/shard_map/dot_general | solution.py:789
  286.1 4.8 multiply_convert_fusion.1
  290.9 16.8 %fusion.113 = (f32[4,1024]{1,0:T(4,128)S(1)}, f32[4,1024,1024]{1,2,0:T(8,128)}) fusion(s32[4,1024]{1,0:T(4,128)S(1)} %eq.36, pred[1024,1024]{0,1:T(8,128)(4,1)} %iota_compare_fusion, bf16[4,1024,64]{1,2,0:T(8,128)(2,1)} %get-tuple-element.31, bf16[4,1024,64]{1,2,0:T(8,128)(2,1)} %get-tuple-element.30), kind=kOutput, calls=%fused_computation.178 | convolution fusion | flops 574620672 | bytes 18907136 | tf_op jit(solution)/shard_map/sub | solution.py:726
  307.8 9.2 %fusion.17 = bf16[4,1024,1024]{1,2,0:T(8,128)(2,1)} fusion(f32[4,1024,1024]{1,2,0:T(8,128)} %get-tuple-element.29, f32[4,1024]{1,0:T(4,128)S(1)} %get-tuple-element.28), kind=kLoop, calls=%fused_computation.27 | loop fusion | flops 8388608 | bytes 25182208 | tf_op jit(solution)/shard_map/convert_element_type | solution.py:728
  317.0 11.4 %fusion.9 = f32[4096,320]{0,1:T(8,128)} fusion(bf16[2048,320]{1,0:T(8,128)(2,1)} %bitcast.9, bf16[1,4096,2048]{2,1,0:T(8,128)(2,1)} %all-gather.3.cloned.1.call-done), kind=kOutput, calls=%fused_computation.12 | convolution fusion | flops 5368709120 | bytes 23330816 | tf_op jit(solution)/shard_map/dot_general | solution.py:797
  332.1 14.4 %add_convert_fusion = bf16[4096,2048]{1,0:T(8,128)(2,1)} fusion(f32[2048]{0:T(1024)S(1)} %fusion.104, bf16[2048,320]{1,0:T(8,128)(2,1)} %bitcast.9, bf16[4096,256]{0,1:T(8,128)(2,1)} %multiply_convert_fusion.1, bf16[4096,64]{0,1:T(8,128)(2,1)S(1)} %bitcast.168), kind=kOutput, calls=%fused_computation.9 | convolution fusion | flops 5390729216 | bytes 20717568 | tf_op jit(solution)/shard_map/dot_general | solution.py:807
  348.8 6.0 fusion.38
  355.7 7.2 %multiply_convert_fusion = bf16[4,1024,1024]{1,2,0:T(8,128)(2,1)S(1)} fusion(f32[4,1024]{1,0:T(4,128)S(1)} %get-tuple-element.22, f32[4,1024,1024]{1,2,0:T(8,128)} %get-tuple-element.29, f32[4,1024]{1,0:T(4,128)S(1)} %get-tuple-element.28, bf16[8,4,8,1024]{3,2,1,0:T(8,128)(2,1)S(1)} %bitcast.159, bf16[8,4,8,1024]{3,2,1,0:T(8,128)(2,1)S(1)} %bitcast.156), kind=kOutput, calls=%fused_computation.14 | convolution fusion | flops 553648128 | bytes 26247168 | tf_op jit(solution)/shard_map/bqd,bkd->bqk/dot_general | solution.py:731
  370.5 11.0 %fusion.28 = bf16[2048,320]{0,1:T(8,128)(2,1)} fusion(bf16[1,4096,2048]{2,1,0:T(8,128)(2,1)} %all-gather.3.cloned.1.call-done, bf16[4096,256]{0,1:T(8,128)(2,1)S(1)} %copy-done.5, bf16[4096,64]{0,1:T(8,128)(2,1)S(1)} %bitcast.169), kind=kOutput, calls=%fused_computation.45 | convolution fusion | flops 5374607360 | bytes 20709376 | tf_op jit(solution)/shard_map/dot_general | solution.py:829
  384.1 6.0 all-to-all-start.3
  398.7 5.3 fusion.33
  404.0 13.6 %fusion.109 = (bf16[2048,448]{0,1:T(8,128)(2,1)}, f32[2048]{0:T(1024)S(1)}) fusion(bf16[2048,448]{0,1:T(8,128)(2,1)S(1)} %copy-done.7, bf16[4096,448]{0,1:T(8,128)(2,1)S(1)} %fusion.33, bf16[4096,2048]{1,0:T(8,128)(2,1)} %fusion.6), kind=kOutput, calls=%fused_computation.174 | convolution fusion | flops 7519860736 | bytes 24125440 | tf_op jit(solution)/shard_map/dot_general | solution.py:835
  430.1 7.7 %all-to-all-done.3 = bf16[32,64,320]{2,1,0:T(8,128)(2,1)} async-done(((bf16[32,64,320]{2,1,0:T(8,128)(2,1)}), bf16[32,64,320]{2,1,0:T(8,128)(2,1)}, u32[]{:S(2)}, u32[]{:S(2)}) %all-to-all-start.3) | async-done | bytes 1310752 | tf_op jit(solution)/shard_map/all_to_all | solution.py:705
  437.7 9.1 %all-to-all-start.2 = ((bf16[32,64,450]{2,1,0:T(8,128)(2,1)}), bf16[32,64,450]{2,1,0:T(8,128)(2,1)}, u32[]{:S(2)}, u32[]{:S(2)}) async-start(bf16[32,64,450]{2,1,0:T(8,128)(2,1)} %pad_maximum_fusion.2), calls=%async_computation.3 | async-start | bytes 4194304 | tf_op jit(solution)/shard_map/all_to_all | solution.py:705
  448.0 14.6 %convolution_convert_fusion.part_ref = bf16[4096,2048]{1,0:T(8,128)(2,1)} fusion(bf16[4096,448]{0,1:T(8,128)(2,1)} %copy-done.4, bf16[2048,448]{1,0:T(8,128)(2,1)S(1)} %bitcast.141), kind=kOutput, calls=%fused_computation.18 | convolution fusion | flops 7524581376 | bytes 22282240 | tf_op jit(solution)/shard_map/dot_general | solution.py:825
  462.6 167.7 %shard_map.153 = f32[128,2048]{1,0:T(8,128)} custom-call(bf16[4096,2048]{1,0:T(8,128)(2,1)} %convolution_convert_fusion.part_ref), custom_call_target="tpu_custom_call" | custom-call | tf_op jit(solution)/shard_map/pallas_call | solution.py:678
  634.3 4.3 copy.296
  638.6 6.0 copy.297
  644.6 5.4 reshape.284
  654.2 7.2 %reshape.287 = f32[32,64,7,64]{3,2,1,0:T(8,128)} reshape(f32[32,64,448]{2,1,0:T(8,128)} %slice_convert_fusion) | data formatting | bytes 7340032 | tf_op jit(solution)/shard_map/transpose | solution.py:847
  661.3 10.6 %copy.294 = f32[64,7,32,64]{3,2,1,0:T(8,128)} copy(f32[64,7,32,64]{3,1,0,2:T(8,128)} %bitcast.138) | data formatting | bytes 7340032 | tf_op jit(solution)/shard_map/transpose | solution.py:847
  672.0 6.5 reshape.285
  (132 shorter events, 83.4 us)
Async XLA Ops:
  7.2 309.8 %all-gather.3.cloned.1.call-start = ((), (), s32[]{:S(2)}) async-start(), calls=%async_computation.6 | async-start | bytes 17301504 | tf_op jit(solution)/shard_map/all_gather | solution.py:776
  27.3 7.9 %copy-start.17 = (bf16[7,64]{1,0:T(8,128)(2,1)S(1)}, bf16[7,64]{1,0:T(8,128)(2,1)}, u32[]{:S(2)}) copy-start(bf16[7,64]{1,0:T(8,128)(2,1)} %param.11) | copy-start | bytes 2692
  27.3 8.0 %copy-start.18 = (bf16[64]{0:T(256)(128)(2,1)S(1)}, bf16[64]{0:T(256)(128)(2,1)}, u32[]{:S(2)}) copy-start(bf16[64]{0:T(256)(128)(2,1)} %param.15) | copy-start | bytes 388
  27.3 8.1 %copy-start.8 = (bf16[64,10240]{1,0:T(8,128)(2,1)S(1)}, bf16[64,10240]{1,0:T(8,128)(2,1)}, u32[]{:S(2)}) copy-start(bf16[64,10240]{1,0:T(8,128)(2,1)} %param.14) | copy-start | bytes 3932164
  29.1 195.7 %all-to-all-start = ((bf16[32,64,452]{2,1,0:T(8,128)(2,1)}), bf16[32,64,452]{2,1,0:T(8,128)(2,1)S(1)}, u32[]{:S(2)}, u32[]{:S(2)}) async-start(bf16[32,64,452]{2,1,0:T(8,128)(2,1)} %pad_maximum_fusion.1), calls=%async_computation | async-start | bytes 4194304 | tf_op jit(solution)/shard_map/all_to_all | solution.py:705
  207.6 10.7 %copy-start = (bf16[4096,2048]{1,0:T(8,128)(2,1)S(1)}, bf16[4096,2048]{1,0:T(8,128)(2,1)}, u32[]{:S(2)}) copy-start(bf16[4096,2048]{1,0:T(8,128)(2,1)} %shard_map.152) | copy-start | bytes 50331652
  224.8 92.2 %all-to-all-start.1 = ((bf16[32,64,320]{2,1,0:T(8,128)(2,1)}), bf16[32,64,320]{2,1,0:T(8,128)(2,1)}, u32[]{:S(2)}, u32[]{:S(2)}) async-start(bf16[32,64,320]{2,1,0:T(8,128)(2,1)} %copy.278), calls=%async_computation.1 | async-start | bytes 3145728 | tf_op jit(solution)/shard_map/all_to_all | solution.py:705
  242.7 438.1 %reduce-scatter.2.cloned.1.call-start = ((), (), s32[]{:S(2)}) async-start(), calls=%async_computation.5 | async-start | bytes 17301504 | tf_op jit(solution)/shard_map/reduce_scatter | solution.py:811
  247.3 16.9 %copy-start.13 = (bf16[32,64,1]{1,0,2:T(8,128)(2,1)}, bf16[32,64,1]{1,0,2:T(8,128)(2,1)S(1)}, u32[]{:S(2)}) copy-start(bf16[32,64,1]{1,0,2:T(8,128)(2,1)S(1)} %copy.304) | copy-start | bytes 12292
  247.4 16.8 %copy-start.11 = (f32[2048]{0:T(1024)}, f32[2048]{0:T(1024)S(1)}, u32[]{:S(2)}) copy-start(f32[2048]{0:T(1024)S(1)} %reshape.281) | copy-start | bytes 24580
  247.7 16.5 %copy-start.15 = (bf16[32,64,1]{1,0,2:T(8,128)(2,1)}, bf16[32,64,1]{1,0,2:T(8,128)(2,1)S(1)}, u32[]{:S(2)}) copy-start(bf16[32,64,1]{1,0,2:T(8,128)(2,1)S(1)} %copy.305) | copy-start | bytes 12292
  317.0 12.7 %copy-start.1 = (bf16[4,1024,1024]{1,2,0:T(8,128)(2,1)S(1)}, bf16[4,1024,1024]{1,2,0:T(8,128)(2,1)}, u32[]{:S(2)}) copy-start(bf16[4,1024,1024]{1,2,0:T(8,128)(2,1)} %fusion.17) | copy-start | bytes 25165828
  331.3 0.8 copy-start.9
  366.6 3.9 copy-start.5
  366.6 3.9 copy-start.10
  384.1 53.7 %all-to-all-start.3 = ((bf16[32,64,320]{2,1,0:T(8,128)(2,1)}), bf16[32,64,320]{2,1,0:T(8,128)(2,1)}, u32[]{:S(2)}, u32[]{:S(2)}) async-start(bf16[32,64,320]{2,1,0:T(8,128)(2,1)} %bitcast.147), calls=%async_computation.4 | async-start | bytes 3145728 | tf_op jit(solution)/shard_map/all_to_all | solution.py:705
  398.7 5.3 copy-start.7
  404.0 13.6 %copy-start.4 = (bf16[4096,448]{0,1:T(8,128)(2,1)}, bf16[4096,448]{0,1:T(8,128)(2,1)S(1)}, u32[]{:S(2)}) copy-start(bf16[4096,448]{0,1:T(8,128)(2,1)S(1)} %fusion.33) | copy-start | bytes 11010052
  417.7 7.0 %copy-start.14 = (bf16[32,64,1]{1,0,2:T(8,128)(2,1)S(1)}, bf16[32,64,1]{1,0,2:T(8,128)(2,1)}, u32[]{:S(2)}) copy-start(bf16[32,64,1]{1,0,2:T(8,128)(2,1)} %copy-done.13) | copy-start | bytes 12292
  417.7 7.1 %copy-start.16 = (bf16[32,64,1]{1,0,2:T(8,128)(2,1)S(1)}, bf16[32,64,1]{1,0,2:T(8,128)(2,1)}, u32[]{:S(2)}) copy-start(bf16[32,64,1]{1,0,2:T(8,128)(2,1)} %copy-done.15) | copy-start | bytes 12292
  426.2 20.6 %copy-start.2 = (bf16[1,128,2048]{2,1,0:T(8,128)(2,1)S(1)}, bf16[1,128,2048]{2,1,0:T(8,128)(2,1)}, u32[]{:S(2)}) copy-start(bf16[1,128,2048]{2,1,0:T(8,128)(2,1)} %param.9) | copy-start | bytes 1572868
  437.7 212.3 %all-to-all-start.2 = ((bf16[32,64,450]{2,1,0:T(8,128)(2,1)}), bf16[32,64,450]{2,1,0:T(8,128)(2,1)}, u32[]{:S(2)}, u32[]{:S(2)}) async-start(bf16[32,64,450]{2,1,0:T(8,128)(2,1)} %pad_maximum_fusion.2), calls=%async_computation.3 | async-start | bytes 4194304 | tf_op jit(solution)/shard_map/all_to_all | solution.py:705
  462.6 170.1 %copy-start.12 = (f32[2048]{0:T(1024)S(1)}, f32[2048]{0:T(1024)}, u32[]{:S(2)}) copy-start(f32[2048]{0:T(1024)} %copy-done.11) | copy-start | bytes 24580
  671.9 8.9 %copy-start.3 = (f32[128,2048]{1,0:T(8,128)S(1)}, f32[128,2048]{1,0:T(8,128)}, u32[]{:S(2)}) copy-start(f32[128,2048]{1,0:T(8,128)} %shard_map.153) | copy-start | bytes 3145732
  671.9 8.9 %copy-start.6 = (bf16[1,128,2048]{2,1,0:T(8,128)(2,1)S(1)}, bf16[1,128,2048]{2,1,0:T(8,128)(2,1)}, u32[]{:S(2)}) copy-start(bf16[1,128,2048]{2,1,0:T(8,128)(2,1)} %param.17) | copy-start | bytes 1572868
Sparse Core Ops, SparseCore 0:
  10.8 161.5 all-gather.2
  346.6 275.8 reduce-scatter.1

commit v3 on v0

--- a/solution.py
+++ b/solution.py
@@ -1,8 +1,11 @@
+import functools
 import math
 
 import jax
 import jax.numpy as jnp
 from jax import lax
+from jax.experimental import pallas as pl
+from jax.experimental.pallas import tpu as pltpu
 from jax.sharding import PartitionSpec as P
 
 H = 32
@@ -115,7 +118,7 @@
     return (d_key.reshape(key_count, H * HD), d_value.reshape(key_count, H * HD))
 
 
-def on_device(
+def on_device_gathered(
     hidden_in, w_in_t, in_bias, ln_gain, ln_shift, w_out_t, out_bias, segment_ids, out_grad
 ):
     inputs = hidden_in[0].astype(jnp.float32)
@@ -352,6 +355,762 @@
     )
 
 
+AXES = ("dp", "ctx")
+MESH = pl.DeviceIdType.MESH
+class Place:
+    def __init__(self, depth):
+        self.depth = depth
+        self.top = depth - 1
+        self.z = lax.axis_index("dp")
+        self.c = lax.axis_index("ctx")
+        y, x, self.core = self.c // 4, (self.c // 2) % 2, self.c % 2
+        self.first_stride = jnp.where(self.core == 0, 2, 4)
+        self.last_stride = jnp.where(self.core == 0, 4, 2)
+        self.f = jnp.where(self.core == 0, x, y)
+        self.l = jnp.where(self.core == 0, y, x)
+
+    def ctx(self, f, l, core):
+        return f * self.first_stride + l * self.last_stride + core
+
+    def shard(self, z, f, l, core=None):
+        return z * 8 + self.ctx(f, l, self.core if core is None else core)
+
+    def first(self):
+        return {"dp": self.z, "ctx": self.ctx(1 - self.f, self.l, self.core)}
+
+    def last(self):
+        return {"dp": self.z, "ctx": self.ctx(self.f, 1 - self.l, self.core)}
+
+    def sibling(self):
+        return {"dp": self.z, "ctx": self.ctx(self.f, self.l, 1 - self.core)}
+
+    def above(self):
+        return {"dp": self.z + 1, "ctx": self.c}
+
+    def below(self):
+        return {"dp": self.z - 1, "ctx": self.c}
+
+    def greet(self):
+        barrier = pltpu.get_barrier_semaphore()
+        for device in (self.first(), self.last(), self.sibling()):
+            pl.semaphore_signal(barrier, inc=1, device_id=device, device_id_type=MESH)
+
+        @pl.when(self.z > 0)
+        def _():
+            pl.semaphore_signal(barrier, inc=1, device_id=self.below(), device_id_type=MESH)
+
+        @pl.when(self.z < self.top)
+        def _():
+            pl.semaphore_signal(barrier, inc=1, device_id=self.above(), device_id_type=MESH)
+
+        ends = jnp.where(self.z > 0, 1, 0) + jnp.where(self.z < self.top, 1, 0)
+        pl.semaphore_wait(barrier, 3 + ends)
+
+    def choose(self, rule):
+        value = jnp.int32(0)
+        for z in range(self.depth):
+            value = jnp.where(self.z == z, rule(z), value)
+        return value
+
+    def near(self, step):
+        return self.choose(lambda z: sorted([q for q in range(self.depth) if q != z], key=lambda q: (abs(q - z), q))[step])
+
+    def far(self, step):
+        def rule(z):
+            ups, downs = list(range(self.top, z, -1)), list(range(z))
+            return ((ups + downs if 2 * z < self.depth else downs + ups) + [z])[step]
+
+        return self.choose(rule)
+
+
+def push(source, target, send, receive, device):
+    return pltpu.make_async_remote_copy(
+        src_ref=source, dst_ref=target, send_sem=send, recv_sem=receive, device_id=device, device_id_type=MESH
+    )
+
+
+class Gather:
+    def __init__(self, depth, rows, own_ref, all_ref, local, sends, arrivals):
+        self.me, self.rows = Place(depth), rows
+        self.own_ref, self.all_ref, self.sends, self.arrivals = own_ref, all_ref, sends, arrivals
+        me = self.me
+        self.keep = pltpu.make_async_copy(own_ref, self.block(me.shard(me.z, me.f, me.l)), local)
+        self.used, self.drains = 0, []
+        zs = [me.z] + [me.near(step) for step in range(depth - 1)]
+        self.steps = [self.begin]
+        crossings = [(z, f) for z in zs for f in (me.f, 1 - me.f)]
+        relays = []
+        for z in zs:
+            if z is not me.z:
+                relays.append(functools.partial(self.along_line, z))
+            relays.append(functools.partial(self.along_first, z))
+        for n, relay in enumerate(relays):
+            self.steps += [relay, functools.partial(self.cross, *crossings[n])]
+        self.steps.append(functools.partial(self.cross, *crossings[-1]))
+
+    def block(self, shard):
+        return self.all_ref.at[pl.ds(pl.multiple_of(shard * self.rows, self.rows), self.rows)]
+
+    def send(self, source, shard, device, when=None):
+        slot = self.used
+        self.used += 1
+
+        def start():
+            push(source, self.block(shard), self.sends.at[slot], self.arrivals.at[shard], device).start()
+
+        def drain():
+            push(self.own_ref, self.block(0), self.sends.at[slot], self.arrivals.at[0], self.me.sibling()).wait_send()
+
+        if when is None:
+            start()
+            self.drains.append(drain)
+        else:
+            pl.when(when())(start)
+            self.drains.append(lambda: pl.when(when())(drain))
+
+    def arrived(self, shard):
+        push(self.own_ref, self.block(shard), self.sends.at[0], self.arrivals.at[shard], self.me.sibling()).wait_recv()
+
+    def begin(self):
+        me = self.me
+        shard = me.shard(me.z, me.f, me.l)
+        self.send(self.own_ref, shard, me.above(), lambda: me.z < me.top)
+        self.send(self.own_ref, shard, me.below(), lambda: me.z > 0)
+        self.send(self.own_ref, shard, me.first())
+        self.send(self.own_ref, shard, me.last())
+        self.send(self.own_ref, shard, me.sibling())
+        self.keep.start()
+
+    def along_line(self, z):
+        me = self.me
+        shard = me.shard(z, me.f, me.l)
+        self.arrived(shard)
+        self.send(self.block(shard), shard, me.above(), lambda: (z < me.z) & (me.z < me.top))
+        self.send(self.block(shard), shard, me.below(), lambda: (z > me.z) & (me.z > 0))
+        self.send(self.block(shard), shard, me.first())
+        self.send(self.block(shard), shard, me.last())
+        self.send(self.block(shard), shard, me.sibling())
+
+    def along_first(self, z):
+        me = self.me
+        shard = me.shard(z, 1 - me.f, me.l)
+        self.arrived(shard)
+        self.send(self.block(shard), shard, me.last())
+        self.send(self.block(shard), shard, me.sibling())
+
+    def cross(self, z, f):
+        me = self.me
+        shard = me.shard(z, f, 1 - me.l)
+        self.arrived(shard)
+        self.send(self.block(shard), shard, me.sibling())
+
+    def finish(self):
+        me = self.me
+        for z in range(me.depth):
+            for f in range(2):
+                for l in range(2):
+                    self.arrived(me.shard(z, f, l, 1 - me.core))
+        self.keep.wait()
+        for drain in self.drains:
+            drain()
+
+    @staticmethod
+    def scratch(depth):
+        return [
+            pltpu.SemaphoreType.DMA(()),
+            pltpu.SemaphoreType.DMA((5 + 5 * (depth - 1) + 2 * depth + 2 * depth,)),
+            pltpu.SemaphoreType.DMA((depth * 8,)),
+        ]
+
+
+def gather_kernel(depth, rows, own_ref, all_ref, *scratch):
+    gather = Gather(depth, rows, own_ref, all_ref, *scratch)
+    gather.me.greet()
+    for step in gather.steps:
+        step()
+    gather.finish()
+
+
+def gather_all(own, depth, collective_id):
+    rows, width = own.shape
+    return pl.pallas_call(
+        functools.partial(gather_kernel, depth, rows),
+        out_shape=jax.ShapeDtypeStruct((depth * 8 * rows, width), own.dtype),
+        in_specs=[pl.BlockSpec(memory_space=pl.ANY)],
+        out_specs=pl.BlockSpec(memory_space=pl.ANY),
+        scratch_shapes=Gather.scratch(depth),
+        compiler_params=pltpu.CompilerParams(collective_id=collective_id, has_side_effects=True),
+    )(own)
+
+
+class Scatter:
+    def __init__(self, depth, rows, part_ref, out_ref, sums, from_sib, from_last, from_first, from_below, from_above,
+                 loads, send_sib, send_last, send_first, send_line, got_sib, got_last, got_first, got_below, got_above):
+        self.me, self.rows, self.step = Place(depth), rows, min(rows, 16)
+        self.part_ref, self.out_ref, self.sums, self.loads = part_ref, out_ref, sums, loads
+        self.sib, self.last, self.first = (from_sib, send_sib, got_sib), (from_last, send_last, got_last), (from_first, send_first, got_first)
+        self.up, self.down = (from_below, send_line, got_below), (from_above, send_line, got_above)
+        me = self.me
+        self.zs = [me.far(i) for i in range(depth)]
+        chip = [functools.partial(self.chip, z) for z in self.zs]
+        plane = [functools.partial(self.plane, z) for z in self.zs]
+        line = [functools.partial(self.line, z) for z in self.zs[:-1]] + [self.final]
+        self.steps = [self.begin, chip[0]]
+        for i in range(1, depth + 2):
+            if i < depth:
+                self.steps.append(chip[i])
+            if i <= depth:
+                self.steps.append(plane[i - 1])
+            if i >= 2:
+                self.steps.append(line[i - 2])
+
+    def source(self, z, f, l, core):
+        me = self.me
+        return self.part_ref.at[pl.ds(pl.multiple_of(me.shard(z, f, l, core) * self.rows, self.rows), self.rows)]
+
+    def at(self, z, f, l):
+        return z * 4 + f * 2 + l
+
+    def add(self, target, source):
+        @pl.loop(0, self.rows // self.step)
+        def _(i):
+            part = pl.ds(pl.multiple_of(i * self.step, self.step), self.step)
+            target[part, :] = (target[part, :].astype(jnp.float32) + source[part, :].astype(jnp.float32)).astype(target.dtype)
+
+    def copy(self, stage, source, slot, device, send_slot=None):
+        landing, send, got = stage
+        return push(source, landing.at[slot], send.at[slot if send_slot is None else send_slot], got.at[slot], device)
+
+    def to_sibling(self, z, f, l):
+        return self.copy(self.sib, self.source(z, f, l, 1 - self.me.core), self.at(z, l, f), self.me.sibling())
+
+    def to_last(self, z, f):
+        me = self.me
+        return self.copy(self.last, self.sums.at[self.at(z, f, 1 - me.l)], z * 2 + f, me.last())
+
+    def to_first(self, z):
+        me = self.me
+        return self.copy(self.first, self.sums.at[self.at(z, 1 - me.f, me.l)], z, me.first())
+
+    def mine(self, z):
+        return self.sums.at[self.at(z, self.me.f, self.me.l)]
+
+    def load(self, z, f, l):
+        k = self.at(z, f, l)
+        return pltpu.make_async_copy(self.source(z, f, l, self.me.core), self.sums.at[k], self.loads.at[k])
+
+    def pairs(self):
+        me = self.me
+        return [(f, l) for l in (1 - me.l, me.l) for f in (1 - me.f, me.f)]
+
+    def begin(self):
+        me = self.me
+        for z in self.zs:
+            for f in (1 - me.f, me.f):
+                for l in (1 - me.l, me.l):
+                    self.to_sibling(z, f, l).start()
+            for f, l in self.pairs():
+                self.load(z, f, l).start()
+
+    def chip(self, z):
+        me = self.me
+        for n, (f, l) in enumerate(self.pairs()):
+            k = self.at(z, f, l)
+            self.load(z, f, l).wait()
+            self.copy(self.sib, self.sums.at[k], k, me.sibling()).wait_recv()
+            self.add(self.sums.at[k], self.sib[0].at[k])
+            if n in (1, 2):
+                self.to_last(z, self.pairs()[n - 1][0]).start()
+
+    def plane(self, z):
+        me = self.me
+        for f in (1 - me.f, me.f):
+            k = self.at(z, f, me.l)
+            self.to_last(z, f).wait_recv()
+            self.add(self.sums.at[k], self.last[0].at[z * 2 + f])
+        self.to_first(z).start()
+
+    def line(self, z):
+        me = self.me
+        self.to_first(z).wait_recv()
+        self.add(self.mine(z), self.first[0].at[z])
+        upward, downward = self.copy(self.up, self.mine(z), z, me.above()), self.copy(self.down, self.mine(z), z, me.below())
+
+        @pl.when((z > me.z) & (me.z > 0))
+        def _():
+            upward.wait_recv()
+            self.add(self.mine(z), self.up[0].at[z])
+
+        @pl.when((z < me.z) & (me.z < me.top))
+        def _():
+            downward.wait_recv()
+            self.add(self.mine(z), self.down[0].at[z])
+
+        @pl.when(z > me.z)
+        def _():
+            upward.start()
+
+        @pl.when(z < me.z)
+        def _():
+            downward.start()
+
+    def final(self):
+        me = self.me
+        z = me.z
+        self.to_first(z).wait_recv()
+        self.add(self.mine(z), self.first[0].at[z])
+
+        @pl.when(z > 0)
+        def _():
+            self.copy(self.up, self.mine(z), z, me.above()).wait_recv()
+            self.add(self.mine(z), self.up[0].at[z])
+
+        @pl.when(z < me.top)
+        def _():
+            self.copy(self.down, self.mine(z), z, me.below()).wait_recv()
+            self.add(self.mine(z), self.down[0].at[z])
+
+        self.out_ref[...] = self.mine(z)[...].astype(self.out_ref.dtype)
+
+    def finish(self):
+        me = self.me
+        for i, z in enumerate(self.zs):
+            for f, l in self.pairs():
+                self.to_sibling(z, f, l).wait_send()
+            for f in (1 - me.f, me.f):
+                self.to_last(z, f).wait_send()
+            self.to_first(z).wait_send()
+            if i < me.top:
+                self.copy(self.up, self.mine(z), z, me.above()).wait_send()
+
+    @staticmethod
+    def scratch(depth, shard, dtype):
+        dma = pltpu.SemaphoreType.DMA
+        counts = [depth * 4, depth * 4, depth * 2, depth, depth, depth]
+        sems = [depth * 4, depth * 4, depth * 2, depth, depth, depth * 4, depth * 2, depth, depth, depth]
+        return [pltpu.VMEM((count, *shard), dtype) for count in counts] + [dma((count,)) for count in sems]
+
+
+def scatter_kernel(depth, rows, part_ref, out_ref, *scratch):
+    scatter = Scatter(depth, rows, part_ref, out_ref, *scratch)
+    scatter.me.greet()
+    for step in scatter.steps:
+        step()
+    scatter.finish()
+
+
+def scatter_sum(part, depth, collective_id, out_dtype):
+    tokens, width = part.shape
+    rows = tokens // (depth * 8)
+    return pl.pallas_call(
+        functools.partial(scatter_kernel, depth, rows),
+        out_shape=jax.ShapeDtypeStruct((rows, width), out_dtype),
+        in_specs=[pl.BlockSpec(memory_space=pl.ANY)],
+        out_specs=pl.BlockSpec(memory_space=pltpu.VMEM),
+        scratch_shapes=Scatter.scratch(depth, (rows, width), part.dtype),
+        compiler_params=pltpu.CompilerParams(collective_id=collective_id, has_side_effects=True, vmem_limit_bytes=48 << 20),
+    )(part)
+
+
+LANES = 128
+NT = (((1,), (1,)), ((), ()))
+TN = (((0,), (0,)), ((), ()))
+
+
+def low_half(shape):
+    return lax.broadcasted_iota(jnp.int32, shape, 1) < LANES // 2
+
+
+def swap_halves(block):
+    return pltpu.roll(block, LANES // 2, 1)
+
+
+def split_kernel(parts, width, *refs):
+    scale_ref, extra_ref, out_ref = refs[len(parts) :]
+    depth = out_ref.shape[1]
+    low = low_half((depth, LANES))
+
+    @pl.loop(0, width // LANES)
+    def _(m):
+        base = 0
+        for count, rows_ref in zip(parts, refs):
+            for pair in range((count + 1) // 2):
+
+                def piece(part):
+                    lanes = pl.ds(pl.multiple_of(part * width + m * LANES, LANES), LANES)
+                    values = rows_ref[:, lanes].astype(jnp.float32)
+                    return values * scale_ref[...] if base == 0 else values
+
+                first = piece(2 * pair)
+                if 2 * pair + 1 < count:
+                    second = piece(2 * pair + 1)
+                    even = jnp.where(low, first, swap_halves(second))
+                    odd = jnp.where(low, swap_halves(first), second)
+                else:
+                    rest = extra_ref[...] if base == 0 else jnp.zeros_like(first)
+                    even = jnp.where(low, first, rest)
+                    odd = jnp.where(low, swap_halves(first), rest)
+                lanes = slice((base + pair) * LANES, (base + pair + 1) * LANES)
+                out_ref[2 * m, :, lanes] = even.astype(out_ref.dtype)
+                out_ref[2 * m + 1, :, lanes] = odd.astype(out_ref.dtype)
+            base += (count + 1) // 2
+
+
+def split_blocks(arrays, parts, scale, extra):
+    depth = arrays[0].shape[0]
+    width = arrays[0].shape[1] // parts[0]
+    padded = sum((count + 1) // 2 for count in parts) * LANES
+    return pl.pallas_call(
+        functools.partial(split_kernel, parts, width),
+        out_shape=jax.ShapeDtypeStruct((width // HD, depth, padded), arrays[0].dtype),
+        in_specs=[pl.BlockSpec(memory_space=pltpu.VMEM)] * (len(parts) + 2),
+        out_specs=pl.BlockSpec(memory_space=pltpu.VMEM),
+        compiler_params=pltpu.CompilerParams(vmem_limit_bytes=24 << 20),
+    )(*arrays, scale, extra)
+
+
+def join_kernel(parts, width, blocks_ref, out_ref, extra_ref):
+    depth = out_ref.shape[0]
+    low = low_half((depth, LANES))
+    extra_ref[...] = jnp.zeros_like(extra_ref)
+
+    @pl.loop(0, width // LANES)
+    def _(m):
+        for pair in range((parts + 1) // 2):
+            lanes = slice(pair * LANES, (pair + 1) * LANES)
+            even = blocks_ref[2 * m, :, lanes].astype(jnp.float32)
+            odd = blocks_ref[2 * m + 1, :, lanes].astype(jnp.float32)
+            first = pl.ds(pl.multiple_of(2 * pair * width + m * LANES, LANES), LANES)
+            out_ref[:, first] = jnp.where(low, even, swap_halves(odd))
+            if 2 * pair + 1 < parts:
+                second = pl.ds(pl.multiple_of((2 * pair + 1) * width + m * LANES, LANES), LANES)
+                out_ref[:, second] = jnp.where(low, swap_halves(even), odd)
+            else:
+                extra_ref[...] += even + odd
+
+
+def join_blocks(blocks, parts):
+    count, depth, _ = blocks.shape
+    width = count * HD
+    return pl.pallas_call(
+        functools.partial(join_kernel, parts, width),
+        out_shape=(
+            jax.ShapeDtypeStruct((depth, parts * width), jnp.float32),
+            jax.ShapeDtypeStruct((depth, LANES), jnp.float32),
+        ),
+        in_specs=[pl.BlockSpec(memory_space=pltpu.VMEM)],
+        out_specs=(pl.BlockSpec(memory_space=pltpu.VMEM), pl.BlockSpec(memory_space=pltpu.VMEM)),
+        compiler_params=pltpu.CompilerParams(vmem_limit_bytes=24 << 20),
+    )(blocks)
+
+
+SIDE = 256
+
+
+def turned(block, lane):
+    shift = ROT // 2
+    return jnp.where(lane % HD < shift, pltpu.roll(block, LANES - shift, 1), pltpu.roll(block, shift, 1))
+
+
+def gelu(t):
+    inner = math.sqrt(2.0 / math.pi) * (t + 0.044715 * (t * t * t))
+    return 0.5 * t * (1.0 + jnp.tanh(inner))
+
+
+def gelu_slope(t):
+    slope = math.sqrt(2.0 / math.pi)
+    bent = jnp.tanh(slope * (t + 0.044715 * (t * t * t)))
+    return 0.5 * (1.0 + bent) + 0.5 * t * (1.0 - bent * bent) * slope * (1.0 + 3.0 * 0.044715 * (t * t))
+
+
+def allowed_keys(start, first_query, keys):
+    query = first_query + lax.broadcasted_iota(jnp.int32, (SIDE, keys), 0)
+    key = lax.broadcasted_iota(jnp.int32, (SIDE, keys), 1)
+    return (key >= start) & (key <= query)
+
+
+def forward_kernel(depth, shard_rows, joint_width, hat_ref, weights_ref, bias_ref, cos_ref, sin_ref, start_ref, out_bias_ref, grad_ref,
+                   qk_ref, mid_ref, joined_ref, out_ref, grads_ref, keys_ref, values_ref, *scratch):
+    seq = hat_ref.shape[0]
+    here = pl.program_id(0)
+    low = low_half((SIDE, LANES))
+    lane = lax.broadcasted_iota(jnp.int32, (SIDE, LANES), 1)
+    scaling = HD ** (-0.5)
+    gather = Gather(depth, shard_rows, grad_ref, grads_ref, *scratch)
+    chunks = seq // SIDE
+    slots = spread_steps([gather.me.greet] + gather.steps, depth * chunks, [gather.finish])
+    for q in range(chunks):
+        run_slots(slots, here, q, depth, chunks)
+        rows = slice(q * SIDE, (q + 1) * SIDE)
+        joint = jnp.dot(hat_ref[rows, :], weights_ref[:, :joint_width], preferred_element_type=jnp.float32) + bias_ref[...]
+        qk = joint[:, :LANES]
+        qk = (qk * cos_ref[rows, :] + turned(qk, lane) * sin_ref[rows, :])
+        keys_ref[rows, :] = swap_halves(qk).astype(jnp.bfloat16)
+        query = jnp.where(low, qk * scaling, 0.0).astype(jnp.bfloat16)
+        qk_ref[rows, :] = qk.astype(jnp.bfloat16)
+        values_ref[rows, :] = jnp.where(low, joint[:, LANES : 2 * LANES], 0.0).astype(jnp.bfloat16)
+        count = (q + 1) * SIDE
+        scores = lax.dot_general(query, keys_ref[:count, :], NT, preferred_element_type=jnp.float32)
+        scores = jnp.where(allowed_keys(start_ref[rows, :], q * SIDE, count), scores, negative)
+        largest = jnp.max(scores, -1, keepdims=True)
+        weights = jnp.exp(scores - largest)
+        total = jnp.sum(weights, -1, keepdims=True)
+        weights = (weights * (1.0 / total)).astype(jnp.bfloat16)
+        attended = jnp.dot(weights, values_ref[:count, :], preferred_element_type=jnp.float32)
+        lse = largest + jnp.log(total)
+        mid_ref[rows, : 2 * LANES] = joint[:, LANES : 3 * LANES]
+        mid_ref[rows, 2 * LANES :] = jnp.where(low, joint[:, 3 * LANES :], lse)
+        joined_ref[rows, :LANES] = jnp.where(low, attended, gelu(joint[:, LANES : 2 * LANES])).astype(jnp.bfloat16)
+        joined_ref[rows, LANES : 2 * LANES] = gelu(joint[:, 2 * LANES : 3 * LANES]).astype(jnp.bfloat16)
+        joined_ref[rows, 2 * LANES :] = jnp.where(low, gelu(joint[:, 3 * LANES :]), 0.0).astype(jnp.bfloat16)
+        branch = lax.dot_general(joined_ref[rows, :], weights_ref[:, joint_width:], NT, preferred_element_type=jnp.float32)
+        out_ref[rows, :] = (branch + out_bias_ref[...]).astype(jnp.bfloat16)
+
+    @pl.when(here == pl.num_programs(0) - 1)
+    def _():
+        for step in slots[-1]:
+            step()
+
+
+def spread_steps(steps, count, after):
+    slots = [[] for _ in range(count + 1)]
+    for n, step in enumerate(steps):
+        slots[max(n - 1, 0) * (count - 1) // max(len(steps) - 2, 1) if n else 0].append(step)
+    slots[-1] = list(after)
+    return slots
+
+
+def run_slots(slots, here, q, blocks, chunks):
+    for block in range(blocks):
+        steps = slots[block * chunks + q]
+        if steps:
+
+            @pl.when(here == block)
+            def _():
+                for step in steps:
+                    step()
+
+
+def forward(hat_all, weights, joint_width, bias, cosine, sine, start, out_bias, grads, depth, seq, collective_id):
+    tokens, width = hat_all.shape
+    joined_width = weights.shape[1] - joint_width
+
+    def rows(columns):
+        return pl.BlockSpec((seq, columns), lambda b: (b, 0))
+
+    def whole(array):
+        return pl.BlockSpec(array.shape, lambda b: (0, 0), pipeline_mode=pl.Buffered(1))
+
+    return pl.pallas_call(
+        functools.partial(forward_kernel, depth, grads.shape[0], joint_width),
+        grid=(tokens // seq,),
+        out_shape=(
+            jax.ShapeDtypeStruct((tokens, LANES), jnp.bfloat16),
+            jax.ShapeDtypeStruct((tokens, joined_width), jnp.float32),
+            jax.ShapeDtypeStruct((tokens, joined_width), jnp.bfloat16),
+            jax.ShapeDtypeStruct((tokens, width), jnp.bfloat16),
+            jax.ShapeDtypeStruct((tokens, width), jnp.bfloat16),
+        ),
+        in_specs=[rows(width), whole(weights), whole(bias), rows(LANES), rows(LANES), rows(1), whole(out_bias), pl.BlockSpec(memory_space=pl.ANY)],
+        out_specs=(rows(LANES), rows(joined_width), rows(joined_width), rows(width), pl.BlockSpec(memory_space=pl.ANY)),
+        scratch_shapes=[pltpu.VMEM((seq, LANES), jnp.bfloat16), pltpu.VMEM((seq, LANES), jnp.bfloat16)] + Gather.scratch(depth),
+        compiler_params=pltpu.CompilerParams(collective_id=collective_id, has_side_effects=True, vmem_limit_bytes=56 << 20),
+    )(hat_all, weights, bias, cosine, sine, start, out_bias, grads)
+
+
+def backward_kernel(depth, shard_rows, joint_width, grad_ref, weights_ref, qk_ref, mid_ref, cos_ref, sin_ref, start_ref, branch_ref,
+                    d_joint_ref, d_hat_ref, sums_ref, own_ref, keys_ref, values_ref, d_key_ref, d_value_ref, d_query_ref, *scratch):
+    seq = grad_ref.shape[0]
+    low = low_half((SIDE, LANES))
+    lane = lax.broadcasted_iota(jnp.int32, (SIDE, LANES), 1)
+    scaling = HD ** (-0.5)
+    d_key_ref[...] = jnp.zeros_like(d_key_ref)
+    d_value_ref[...] = jnp.zeros_like(d_value_ref)
+
+    here = pl.program_id(0)
+    scatter = Scatter(depth, shard_rows, branch_ref, own_ref, *scratch)
+    chunks = seq // SIDE
+    slots = spread_steps([scatter.me.greet] + scatter.steps, depth * 2 * chunks, [scatter.finish])
+
+    @pl.when(here == 0)
+    def _():
+        sums_ref[...] = jnp.zeros_like(sums_ref)
+
+    for q in range(chunks):
+        run_slots(slots, here, q, depth, 2 * chunks)
+        rows = slice(q * SIDE, (q + 1) * SIDE)
+        d_joined = jnp.dot(grad_ref[rows, :], weights_ref[:, joint_width:], preferred_element_type=jnp.float32)
+        qk = qk_ref[rows, :].astype(jnp.float32)
+        keys_ref[rows, :] = jnp.where(low, swap_halves(qk), 0.0).astype(jnp.bfloat16)
+        query = jnp.where(low, qk * scaling, 0.0).astype(jnp.bfloat16)
+        values_ref[rows, :] = jnp.where(low, mid_ref[rows, :LANES], 0.0).astype(jnp.bfloat16)
+        d_out = jnp.where(low, d_joined[:, :LANES], 0.0).astype(jnp.bfloat16)
+        count = (q + 1) * SIDE
+        lse = mid_ref[rows, 3 * LANES - 1 : 3 * LANES]
+        scores = lax.dot_general(query, keys_ref[:count, :], NT, preferred_element_type=jnp.float32)
+        weights = jnp.where(allowed_keys(start_ref[rows, :], q * SIDE, count), jnp.exp(scores - lse), 0.0)
+        d_weights = lax.dot_general(d_out, values_ref[:count, :], NT, preferred_element_type=jnp.float32)
+        moved = weights * d_weights
+        d_scores = (moved - weights * jnp.sum(moved, -1, keepdims=True)).astype(jnp.bfloat16)
+        weights = weights.astype(jnp.bfloat16)
+        d_query_ref[rows, :] = jnp.dot(d_scores, keys_ref[:count, :], preferred_element_type=jnp.float32) * scaling
+        d_key_ref[:count, :] += lax.dot_general(d_scores, query, TN, preferred_element_type=jnp.float32)
+        d_value_ref[:count, :] += lax.dot_general(weights, d_out, TN, preferred_element_type=jnp.float32)
+        d_joint_ref[rows, LANES : 2 * LANES] = (d_joined[:, :LANES] * gelu_slope(mid_ref[rows, :LANES])).astype(jnp.bfloat16)
+        d_joint_ref[rows, 2 * LANES : 3 * LANES] = (
+            d_joined[:, LANES : 2 * LANES] * gelu_slope(mid_ref[rows, LANES : 2 * LANES])
+        ).astype(jnp.bfloat16)
+        d_joint_ref[rows, 3 * LANES :] = jnp.where(
+            low, d_joined[:, 2 * LANES :] * gelu_slope(mid_ref[rows, 2 * LANES :]), 0.0
+        ).astype(jnp.bfloat16)
+    for q in range(chunks):
+        run_slots(slots, here, chunks + q, depth, 2 * chunks)
+        rows = slice(q * SIDE, (q + 1) * SIDE)
+        d_qk = jnp.where(low, d_query_ref[rows, :], swap_halves(d_key_ref[rows, :]))
+        d_qk = d_qk * cos_ref[rows, :] - turned(d_qk, lane) * sin_ref[rows, :]
+        d_joint_ref[rows, :LANES] = d_qk.astype(jnp.bfloat16)
+        d_joint_ref[rows, LANES : 2 * LANES] = jnp.where(
+            low, d_value_ref[rows, :], d_joint_ref[rows, LANES : 2 * LANES].astype(jnp.float32)
+        ).astype(jnp.bfloat16)
+        d_joint = d_joint_ref[rows, :]
+        sums_ref[...] += jnp.sum(d_joint.astype(jnp.float32), 0, keepdims=True)
+        d_hat = lax.dot_general(d_joint, weights_ref[:, :joint_width], NT, preferred_element_type=jnp.float32)
+        d_hat_ref[rows, :] = d_hat.astype(jnp.bfloat16)
+
+    @pl.when(here == pl.num_programs(0) - 1)
+    def _():
+        for step in slots[-1]:
+            step()
+
+
+def backward(grad_all, weights, joint_width, qk, mid, cosine, sine, start, branch, depth, seq, collective_id):
+    tokens, width = grad_all.shape
+    joined_width = weights.shape[1] - joint_width
+    own = tokens // (depth * 8)
+
+    def rows(columns):
+        return pl.BlockSpec((seq, columns), lambda b: (b, 0))
+
+    def whole(array):
+        return pl.BlockSpec(array.shape, lambda b: (0, 0), pipeline_mode=pl.Buffered(1))
+
+    return pl.pallas_call(
+        functools.partial(backward_kernel, depth, own, joint_width),
+        grid=(tokens // seq,),
+        out_shape=(
+            jax.ShapeDtypeStruct((tokens, joint_width), jnp.bfloat16),
+            jax.ShapeDtypeStruct((tokens, width), jnp.bfloat16),
+            jax.ShapeDtypeStruct((1, joint_width), jnp.float32),
+            jax.ShapeDtypeStruct((own, width), jnp.bfloat16),
+        ),
+        in_specs=[rows(width), whole(weights), rows(LANES), rows(joined_width), rows(LANES), rows(LANES), rows(1), pl.BlockSpec(memory_space=pl.ANY)],
+        out_specs=(
+            rows(joint_width),
+            rows(width),
+            pl.BlockSpec((1, joint_width), lambda b: (0, 0)),
+            pl.BlockSpec((own, width), lambda b: (0, 0)),
+        ),
+        scratch_shapes=[pltpu.VMEM((seq, LANES), jnp.bfloat16)] * 2
+        + [pltpu.VMEM((seq, LANES), jnp.float32)] * 3
+        + Scatter.scratch(depth, (own, width), branch.dtype),
+        compiler_params=pltpu.CompilerParams(collective_id=collective_id, has_side_effects=True, vmem_limit_bytes=63 << 20),
+    )(grad_all, weights, qk, mid, cosine, sine, start, branch)
+
+
+def exchange(blocks):
+    return lax.all_to_all(blocks, AXES, split_axis=0, concat_axis=0, tiled=True)
+
+
+def on_device(
+    hidden_in, w_in_t, in_bias, ln_gain, ln_shift, w_out_t, out_bias, segment_ids, out_grad
+):
+    depth = lax.axis_size("dp")
+    devices = depth * lax.axis_size("ctx")
+    ctx = lax.axis_index("ctx")
+    me = lax.axis_index("dp") * lax.axis_size("ctx") + ctx
+    tok_rows, model_width = hidden_in.shape[1:]
+    seq_len = segment_ids.shape[1]
+    tokens = devices * tok_rows
+    own = model_width // devices
+    in_parts = in_bias.shape[0]
+    out_parts = w_out_t.shape[1] // model_width
+    in_width, out_width = in_parts * own, out_parts * own
+
+    gain, shift = ln_gain.astype(jnp.float32).T, ln_shift.astype(jnp.float32).T
+    own_seg = lax.dynamic_slice_in_dim(segment_ids[0], ctx * tok_rows, tok_rows)
+    begin = jnp.sum((segment_ids < own_seg[:, None]).astype(jnp.int32), 1)
+    begin = jnp.stack([begin // 256, begin % 256]).reshape(-1, own).T.astype(jnp.float32)
+    extra = jnp.concatenate(
+        [jnp.zeros((own, LANES // 2)), gain, shift, begin, jnp.zeros((own, LANES // 2 - 2 - begin.shape[1]))], 1
+    )
+    got = exchange(split_blocks((w_in_t.T, w_out_t), (in_parts, out_parts), gain, extra))
+    joint_width = (in_parts + 1) // 2 * LANES
+
+    inputs = hidden_in[0].astype(jnp.float32)
+    average = jnp.mean(inputs, -1, keepdims=True)
+    centred = inputs - average
+    inv_std = lax.rsqrt(jnp.mean(centred * centred, -1, keepdims=True) + epsilon)
+    hat = centred * inv_std
+    hat_all = gather_all(hat.astype(jnp.bfloat16), depth, 0)
+
+    weights = got.reshape(model_width, -1)
+    w_in = weights[:, :joint_width]
+    gain_all = w_in[:, in_width : in_width + 1].astype(jnp.float32)
+    shift_all = w_in[:, in_width + 1 : in_width + 2].astype(jnp.float32)
+    begin = got[:, :, in_width + 2 : in_width + 2 + 2 * tok_rows // own].astype(jnp.int32)
+    begin = begin.transpose(0, 2, 1).reshape(devices, 2, tok_rows)
+    begin = (begin[:, 0] * 256 + begin[:, 1]).reshape(tokens)
+    positions = (jnp.arange(tokens) % seq_len - begin).astype(jnp.float32)
+    half = ROT // 2
+    lane = jnp.arange(LANES) % HD
+    frequency = jnp.where(lane < ROT, 10000.0 ** (-2.0 * (lane % half).astype(jnp.float32) / ROT), 0.0)
+    angles = positions[:, None] * frequency[None, :]
+    cosine = jnp.cos(angles)
+    sine = jnp.sin(angles) * jnp.where(lane < half, -1.0, 1.0)[None]
+    bias = in_bias.astype(jnp.float32).reshape(1, in_width)
+    bias = jnp.pad(bias, ((0, 0), (0, joint_width - in_width)))
+    bias = bias + jnp.sum(shift_all / gain_all * w_in.astype(jnp.float32), 0, keepdims=True)
+    column = jnp.arange(model_width) // own
+    out_row = jnp.where(column == me, jnp.tile(out_bias.astype(jnp.float32), devices), 0.0)[None]
+    start = begin[:, None]
+    qk, mid, joined, branch, g_all = forward(
+        hat_all, weights, joint_width, bias, cosine, sine, start, out_row, out_grad[0], depth, seq_len, 1
+    )
+    d_joint, d_hat_part, joint_sums, branch_own = backward(
+        g_all, weights, joint_width, qk, mid, cosine, sine, start, branch, depth, seq_len, 2
+    )
+    result = (inputs + branch_own.astype(jnp.float32)).astype(jnp.bfloat16)
+    grad_out_local = lax.dot_general(g_all, joined, TN, preferred_element_type=jnp.float32).astype(jnp.bfloat16)
+    back_out = exchange(grad_out_local.reshape(devices, own, -1))
+    grad_hat = lax.dot_general(hat_all, d_joint, TN, preferred_element_type=jnp.float32)
+    weight_in = w_in.astype(jnp.float32)
+    gain_part = jnp.sum(weight_in * grad_hat, 1, keepdims=True) / gain_all
+    shift_part = jnp.sum(weight_in * joint_sums, 1, keepdims=True) / gain_all
+    back_lane = jnp.arange(joint_width)[None]
+    grad_in_local = gain_all * grad_hat + shift_all * joint_sums
+    grad_in_local = jnp.where(back_lane == in_width, gain_part, grad_in_local)
+    grad_in_local = jnp.where(back_lane == in_width + 1, shift_part, grad_in_local).astype(jnp.bfloat16)
+    back_in = exchange(grad_in_local.reshape(devices, own, -1))
+    d_hat = scatter_sum(d_hat_part, depth, 3, jnp.float32)
+    d_input = inv_std * (
+        d_hat - jnp.mean(d_hat, -1, keepdims=True) - hat * jnp.mean(d_hat * hat, -1, keepdims=True)
+    ) + out_grad[0].astype(jnp.float32)
+
+    grad_w_out, _ = join_blocks(back_out, out_parts)
+    grad_w_in, vectors = join_blocks(back_in, in_parts)
+    g_columns = lax.dynamic_slice_in_dim(g_all, me * own, own, 1)
+    return (
+        result[None],
+        d_input[None],
+        grad_w_in.T,
+        joint_sums[:, :in_width].reshape(in_parts, own),
+        vectors[:, LANES // 2][None],
+        vectors[:, LANES // 2 + 1][None],
+        grad_w_out,
+        jnp.sum(g_columns.astype(jnp.float32), 0),
+    )
+
+
 def solution(mesh):
     in_specs = (
         P("dp", "ctx", None),
@@ -374,6 +1133,8 @@
         P(("dp", "ctx"), None),
         P(("dp", "ctx")),
     )
+    tensor_parallel = mesh.shape["ctx"] == 8 and mesh.shape["dp"] * 8 == H
+    body = on_device if tensor_parallel else on_device_gathered
     return jax.shard_map(
-        on_device, mesh=mesh, in_specs=in_specs, out_specs=out_specs, check_vma=False
-    )
+        body, mesh=mesh, in_specs=in_specs, out_specs=out_specs, check_vma=False
+    )

time: 3010 us -> 575 us (0.19)
  waiting for transfers between devices: 2400 us -> 0.01 us
  Pallas kernels: 0 us -> 477 us
  matrix products: 241 us -> 29.9 us
  other arithmetic: 161 us -> 32.7 us
  blocking collectives: 88.1 us -> 0 us
  local copies, waits for them, and re-layouts: 90.6 us -> 10.5 us
    reduce_scatter x2 -> x0, waiting for transfers between devices: 1620 us -> none  [the longest x1 1600 us: on_device(): lax.psum_scatter(jnp.concatenate([in_term, out_term], 1), ('dp', 'ctx'),...]
    pallas_call x0 -> x7, Pallas kernels: none -> 477 us  [the longest x1 153 us: gather_all(): pl.pallas_call(functools.partial(gather_kernel, depth, rows), out_shape=j...]
    all_gather x4 -> x0, waiting for transfers between devices: 469 us -> none  [the longest x1 226 us: on_device(): weight_piece = lax.all_gather(w_in_t, ('dp', 'ctx'), axis=1, tiled=True)]
    unnamed x14 -> x0, waiting for transfers between devices: 310 us -> none
    dot_general x20 -> x2, matrix products: 241 us -> 29.9 us  [the longest x1 15.7 us: on_device(): lax.dot_general(hat_all, d_joint, TN, preferred_element_type=jnp.float32)]
    concatenate x4 -> x0, other arithmetic: 132 us -> none  [the longest x1 131 us: on_device(): jnp.concatenate([in_term, out_term], 1)]
    unnamed x1 -> x0, blocking collectives: 45.4 us -> none
    all_gather x1 -> x0, blocking collectives: 42.6 us -> none  [on_device(): bias_piece = lax.all_gather(in_bias, ('dp', 'ctx'), axis=1, tiled=True)]
  transfers between devices with their start and end apart: 10 -> 3, of which waited for: 9 -> 0; matrix products, arithmetic and copies ran while one was open for 12% -> 6% of each run, Pallas kernels for 0% -> 64%
where the time goes in v3:
time: 575 us; the launch traced here: 574 us
  Pallas kernels  477 us (83%)
  other arithmetic  32.7 us (6%)
  matrix products  29.9 us (5%)
  starting transfers between devices  23.6 us (4%)
  local copies, waits for them, and re-layouts  10.5 us (2%)
    pallas_call x1, Pallas kernels, gather_all(): pl.pallas_call(functools.partial(gather_kernel, depth, rows), out_shape=j...  153 us
    pallas_call x1, Pallas kernels, forward(): pl.pallas_call(functools.partial(forward_kernel, depth, grads.shape[0], j...  105 us
    pallas_call x1, Pallas kernels, backward(): pl.pallas_call(functools.partial(backward_kernel, depth, own, joint_width...  105 us
    pallas_call x1, Pallas kernels, scatter_sum(): pl.pallas_call(functools.partial(scatter_kernel, depth, rows), out_shape=...  102 us
    all_to_all x3, starting transfers between devices, exchange(): return lax.all_to_all(blocks, AXES, split_axis=0, concat_axis=0, tiled=True)  23.6 us
    dot_general x1, matrix products, on_device(): lax.dot_general(hat_all, d_joint, TN, preferred_element_type=jnp.float32)  15.7 us
    dot_general x1, matrix products, on_device(): lax.dot_general(g_all, joined, TN, preferred_element_type=jnp.float32)  14.2 us
  transfers between devices with their start and end apart: 3, of which 0 were waited for; matrix products, arithmetic and copies ran while one was open for 6% of the time, Pallas kernels for 64%

profile of v3, /device:TPU:0, one launch (start us, length us, event | category | flops | bytes accessed | tf_op | source)
XLA Modules:
  0.0 574.3 jit_solution(1027430348572342390)
XLA Ops:
  0.6 0.7 dynamic-slice_bitcast_fusion
  1.3 0.9 convert_reduce_fusion.4
  2.4 0.7 bitcast_convert_fusion.1
  3.2 0.7 bitcast_convert_fusion
  4.0 1.5 copy-done.1
  5.5 1.3 copy-done.2
  6.9 3.0 shard_map.153
  9.8 1.8 copy-done
  11.7 7.4 %all-to-all-start = ((bf16[32,64,896]{2,1,0:T(8,128)(2,1)}), bf16[32,64,896]{2,1,0:T(8,128)(2,1)}, u32[]{:S(2)}, u32[]{:S(2)}) async-start(bf16[32,64,896]{2,1,0:T(8,128)(2,1)} %copy-done), calls=%async_computation | async-start | bytes 7340032 | tf_op jit(solution)/shard_map/all_to_all | solution.py:1021
  19.7 1.1 fusion.10.own_ref
  20.8 152.9 %shard_map.152.hat_ref = bf16[4096,2048]{1,0:T(8,128)(2,1)} custom-call(bf16[128,2048]{1,0:T(8,128)(2,1)} %fusion.10.own_ref), custom_call_target="tpu_custom_call" | custom-call | tf_op jit(solution)/shard_map/pallas_call | solution.py:536
  174.5 1.3 convert_bitcast_fusion.1
  176.4 1.9 fusion.18
  178.3 2.1 fusion
  180.4 2.0 copy.34.start_ref
  182.9 9.3 %fusion.3 = (f32[4096,128]{1,0:T(8,128)}, f32[4096,128]{1,0:T(8,128)}) fusion(f32[128]{0:T(128)S(1)} %get-tuple-element.49, f32[128]{0:T(128)S(1)} %get-tuple-element.50, f32[4096]{0:T(1024)S(1)} %fusion.23), kind=kLoop, calls=%fused_computation.10 | loop fusion | flops 1048576 | bytes 4211712 | tf_op jit(solution)/shard_map/mul | solution.py:1069
  192.2 105.4 %shard_map.154 = (bf16[4096,128]{1,0:T(8,128)(2,1)}, f32[4096,384]{1,0:T(8,128)}, bf16[4096,384]{1,0:T(8,128)(2,1)}, bf16[4096,2048]{1,0:T(8,128)(2,1)}, bf16[4096,2048]{1,0:T(8,128)(2,1)}) custom-call(bf16[4096,2048]{1,0:T(8,128)(2,1)} %shard_map.152.hat_ref, bf16[2048,896]{1,0:T(8,128)(2,1)} %bitcast.9.weights_ref, f32[1,512]{1,0:T(1,128)} %convert_add_fusion.bias_ref, ...), custom_call_target="tpu_custom_call" | custom-call | tf_op jit(solution)/shard_map/pallas_call | solution.py:904
  297.7 14.2 %convolution_convert_fusion = bf16[2048,384]{1,0:T(8,128)(2,1)} fusion(bf16[4096,2048]{1,0:T(8,128)(2,1)} %get-tuple-element.20.grad_ref, bf16[4096,384]{1,0:T(8,128)(2,1)} %get-tuple-element.30), kind=kOutput, calls=%fused_computation.9 | convolution fusion | flops 6443237376 | bytes 21495808 | tf_op jit(solution)/shard_map/dot_general | solution.py:1083
  311.9 7.5 %all-to-all-start.2 = ((bf16[32,64,384]{2,1,0:T(8,128)(2,1)}), bf16[32,64,384]{2,1,0:T(8,128)(2,1)}, u32[]{:S(2)}, u32[]{:S(2)}) async-start(bf16[32,64,384]{2,1,0:T(8,128)(2,1)} %bitcast.22), calls=%async_computation.2 | async-start | bytes 3145728 | tf_op jit(solution)/shard_map/all_to_all | solution.py:1021
  319.5 105.1 %shard_map.155 = (bf16[4096,512]{1,0:T(8,128)(2,1)}, bf16[4096,2048]{1,0:T(8,128)(2,1)}, f32[1,512]{1,0:T(1,128)}, bf16[128,2048]{1,0:T(8,128)(2,1)}) custom-call(bf16[4096,2048]{1,0:T(8,128)(2,1)} %get-tuple-element.20.grad_ref, bf16[2048,896]{1,0:T(8,128)(2,1)} %bitcast.9.weights_ref, bf16[4096,128]{1,0:T(8,128)(2,1)} %get-tuple-element.21.qk_ref, ...), custom_call_target="tpu_custom_call" | custom-call | tf_op jit(solution)/shard_map/pallas_call | solution.py:997
  424.6 15.7 %fusion.1 = (f32[2048]{0:T(1024)S(1)}, f32[2048]{0:T(1024)S(1)}, f32[2048,512]{1,0:T(8,128)}) fusion(f32[512]{0:T(512)} %bitcast.88, bf16[2048,896]{1,0:T(8,128)(2,1)} %bitcast.9.weights_ref, bf16[4096,2048]{1,0:T(8,128)(2,1)} %shard_map.152.hat_ref, bf16[4096,512]{1,0:T(8,128)(2,1)} %get-tuple-element.27), kind=kOutput, calls=%fused_computation.4 | convolution fusion | flops 8595173376 | bytes 27281408 | tf_op jit(solution)/shard_map/dot_general | solution.py:1085
  441.0 2.4 fusion.19
  443.5 3.8 select_convert_fusion
  447.3 8.6 %all-to-all-start.1 = ((bf16[32,64,512]{2,1,0:T(8,128)(2,1)}), bf16[32,64,512]{2,1,0:T(8,128)(2,1)S(1)}, u32[]{:S(2)}, u32[]{:S(2)}) async-start(bf16[32,64,512]{2,1,0:T(8,128)(2,1)} %bitcast.84), calls=%async_computation.1 | async-start | bytes 4194304 | tf_op jit(solution)/shard_map/all_to_all | solution.py:1021
  455.9 102.3 %shard_map.156 = f32[128,2048]{1,0:T(8,128)S(1)} custom-call(bf16[4096,2048]{1,0:T(8,128)(2,1)} %get-tuple-element.25.part_ref), custom_call_target="tpu_custom_call" | custom-call | tf_op jit(solution)/shard_map/pallas_call | solution.py:705
  558.2 0.7 reshape.274
  558.9 2.4 convert_reduce_fusion
  561.2 1.4 fusion.31
  562.6 3.0 fusion.15
  565.6 4.4 shard_map.158
  570.0 3.5 shard_map.157
  573.6 0.7 slice_reduce_fusion
  (44 shorter events, 3.7 us)
Async XLA Ops:
  4.0 1.5 copy-start.1
  5.5 1.3 copy-start.2
  9.8 1.8 copy-start
  11.7 7.5 %copy-start.5 = (bf16[7,64]{1,0:T(8,128)(2,1)S(1)}, bf16[7,64]{1,0:T(8,128)(2,1)}, u32[]{:S(2)}) copy-start(bf16[7,64]{1,0:T(8,128)(2,1)} %param.11) | copy-start | bytes 2692
  11.7 7.5 %copy-start.3 = (bf16[1,128,2048]{2,1,0:T(8,128)(2,1)S(1)}, bf16[1,128,2048]{2,1,0:T(8,128)(2,1)}, u32[]{:S(2)}) copy-start(bf16[1,128,2048]{2,1,0:T(8,128)(2,1)} %param.9) | copy-start | bytes 1572868
  11.7 162.8 %all-to-all-start = ((bf16[32,64,896]{2,1,0:T(8,128)(2,1)}), bf16[32,64,896]{2,1,0:T(8,128)(2,1)}, u32[]{:S(2)}, u32[]{:S(2)}) async-start(bf16[32,64,896]{2,1,0:T(8,128)(2,1)} %copy-done), calls=%async_computation | async-start | bytes 7340032 | tf_op jit(solution)/shard_map/all_to_all | solution.py:1021
  20.8 153.0 %copy-start.6 = (bf16[64]{0:T(256)(128)(2,1)S(1)}, bf16[64]{0:T(256)(128)(2,1)}, u32[]{:S(2)}) copy-start(bf16[64]{0:T(256)(128)(2,1)} %param.15) | copy-start | bytes 388
  311.9 135.4 %all-to-all-start.2 = ((bf16[32,64,384]{2,1,0:T(8,128)(2,1)}), bf16[32,64,384]{2,1,0:T(8,128)(2,1)}, u32[]{:S(2)}, u32[]{:S(2)}) async-start(bf16[32,64,384]{2,1,0:T(8,128)(2,1)} %bitcast.22), calls=%async_computation.2 | async-start | bytes 3145728 | tf_op jit(solution)/shard_map/all_to_all | solution.py:1021
  440.3 3.2 copy-start.4
  447.3 122.8 %all-to-all-start.1 = ((bf16[32,64,512]{2,1,0:T(8,128)(2,1)}), bf16[32,64,512]{2,1,0:T(8,128)(2,1)S(1)}, u32[]{:S(2)}, u32[]{:S(2)}) async-start(bf16[32,64,512]{2,1,0:T(8,128)(2,1)} %bitcast.84), calls=%async_computation.1 | async-start | bytes 4194304 | tf_op jit(solution)/shard_map/all_to_all | solution.py:1021

commit v4 on v3

--- a/solution.py
+++ b/solution.py
@@ -406,6 +406,15 @@
         ends = jnp.where(self.z > 0, 1, 0) + jnp.where(self.z < self.top, 1, 0)
         pl.semaphore_wait(barrier, 3 + ends)
 
+    def partner(self, k):
+        return {"dp": self.z ^ (k // 8), "ctx": self.c ^ (k % 8)}
+
+    def greet_all(self):
+        barrier = pltpu.get_barrier_semaphore()
+        for k in range(1, self.depth * 8):
+            pl.semaphore_signal(barrier, inc=1, device_id=self.partner(k), device_id_type=MESH)
+        pl.semaphore_wait(barrier, self.depth * 8 - 1)
+
     def choose(self, rule):
         value = jnp.int32(0)
         for z in range(self.depth):
@@ -423,6 +432,12 @@
         return self.choose(rule)
 
 
+def layer_norm(inputs):
+    centred = inputs - jnp.mean(inputs, -1, keepdims=True)
+    inv_std = lax.rsqrt(jnp.mean(centred * centred, -1, keepdims=True) + epsilon)
+    return centred * inv_std, inv_std
+
+
 def push(source, target, send, receive, device):
     return pltpu.make_async_remote_copy(
         src_ref=source, dst_ref=target, send_sem=send, recv_sem=receive, device_id=device, device_id_type=MESH
@@ -430,26 +445,22 @@
 
 
 class Gather:
-    def __init__(self, depth, rows, own_ref, all_ref, local, sends, arrivals):
-        self.me, self.rows = Place(depth), rows
-        self.own_ref, self.all_ref, self.sends, self.arrivals = own_ref, all_ref, sends, arrivals
-        me = self.me
-        self.keep = pltpu.make_async_copy(own_ref, self.block(me.shard(me.z, me.f, me.l)), local)
+    def __init__(self, me, full, offset, rows, route, own_ref, all_ref, local, sends, arrivals):
+        self.me, self.full, self.offset, self.rows, self.route = me, full, offset, rows, route
+        self.own_ref, self.all_ref, self.sends, self.arrivals = own_ref.at[pl.ds(offset, rows)], all_ref, sends, arrivals
+        self.keep = pltpu.make_async_copy(self.own_ref, self.block(me.shard(me.z, me.f, me.l)), local)
         self.used, self.drains = 0, []
-        zs = [me.z] + [me.near(step) for step in range(depth - 1)]
+        zs = [me.z] + [me.near(step) for step in range(me.top)]
+        pairs = [(z, f) for z in zs for f in (me.f, 1 - me.f)]
         self.steps = [self.begin]
-        crossings = [(z, f) for z in zs for f in (me.f, 1 - me.f)]
-        relays = []
-        for z in zs:
-            if z is not me.z:
-                relays.append(functools.partial(self.along_line, z))
-            relays.append(functools.partial(self.along_first, z))
-        for n, relay in enumerate(relays):
-            self.steps += [relay, functools.partial(self.cross, *crossings[n])]
-        self.steps.append(functools.partial(self.cross, *crossings[-1]))
+        for n, pair in enumerate(pairs):
+            if n:
+                self.steps.append(functools.partial(self.relay, n, *pair))
+                self.steps.append(functools.partial(self.cross, *pairs[n - 1]))
+        self.steps.append(functools.partial(self.cross, *pairs[-1]))
 
     def block(self, shard):
-        return self.all_ref.at[pl.ds(pl.multiple_of(shard * self.rows, self.rows), self.rows)]
+        return self.all_ref.at[pl.ds(pl.multiple_of(shard * self.full + self.offset, self.rows), self.rows)]
 
     def send(self, source, shard, device, when=None):
         slot = self.used
@@ -481,22 +492,21 @@
         self.send(self.own_ref, shard, me.sibling())
         self.keep.start()
 
-    def along_line(self, z):
+    def relay(self, n, z, f):
         me = self.me
-        shard = me.shard(z, me.f, me.l)
+        shard = me.shard(z, f, me.l)
+        block = self.block(shard)
         self.arrived(shard)
-        self.send(self.block(shard), shard, me.above(), lambda: (z < me.z) & (me.z < me.top))
-        self.send(self.block(shard), shard, me.below(), lambda: (z > me.z) & (me.z > 0))
-        self.send(self.block(shard), shard, me.first())
-        self.send(self.block(shard), shard, me.last())
-        self.send(self.block(shard), shard, me.sibling())
-
-    def along_first(self, z):
-        me = self.me
-        shard = me.shard(z, 1 - me.f, me.l)
-        self.arrived(shard)
-        self.send(self.block(shard), shard, me.last())
-        self.send(self.block(shard), shard, me.sibling())
+        if self.route == "zf":
+            if n % 2 == 0:
+                self.send(block, shard, me.above(), lambda: (z < me.z) & (me.z < me.top))
+                self.send(block, shard, me.below(), lambda: (z > me.z) & (me.z > 0))
+                self.send(block, shard, me.first())
+        else:
+            self.send(block, shard, me.above(), lambda: ((z < me.z) if n > 1 else (z == me.z)) & (me.z < me.top))
+            self.send(block, shard, me.below(), lambda: ((z > me.z) if n > 1 else (z == me.z)) & (me.z > 0))
+        self.send(block, shard, me.last())
+        self.send(block, shard, me.sibling())
 
     def cross(self, z, f):
         me = self.me
@@ -514,59 +524,91 @@
         for drain in self.drains:
             drain()
 
+
+class Exchange:
+    def __init__(self, me, blocks_ref, got_ref, local, sends, arrivals):
+        self.me, self.blocks_ref, self.got_ref, self.sends, self.arrivals = me, blocks_ref, got_ref, sends, arrivals
+        self.mine = me.z * 8 + me.c
+        self.keep = pltpu.make_async_copy(blocks_ref.at[self.mine], got_ref.at[self.mine], local)
+        order = [high * 8 + low for low in range(8) for high in EXCHANGE_ORDER if high < me.depth]
+        self.order = [k for k in order if k]
+        self.steps = [functools.partial(self.start, k) for k in self.order] + [self.keep.start]
+
+    def copy(self, k):
+        peer = self.me.partner(k)
+        other = peer["dp"] * 8 + peer["ctx"]
+        return push(self.blocks_ref.at[other], self.got_ref.at[self.mine], self.sends.at[k], self.arrivals.at[k], peer)
+
+    def start(self, k):
+        self.copy(k).start()
+
+    def finish(self):
+        for k in self.order:
+            self.copy(k).wait_recv()
+        for k in self.order:
+            self.copy(k).wait_send()
+        self.keep.wait()
+
     @staticmethod
     def scratch(depth):
-        return [
-            pltpu.SemaphoreType.DMA(()),
-            pltpu.SemaphoreType.DMA((5 + 5 * (depth - 1) + 2 * depth + 2 * depth,)),
-            pltpu.SemaphoreType.DMA((depth * 8,)),
-        ]
-
-
-def gather_kernel(depth, rows, own_ref, all_ref, *scratch):
-    gather = Gather(depth, rows, own_ref, all_ref, *scratch)
-    gather.me.greet()
-    for step in gather.steps:
-        step()
-    gather.finish()
-
-
-def gather_all(own, depth, collective_id):
-    rows, width = own.shape
-    return pl.pallas_call(
-        functools.partial(gather_kernel, depth, rows),
-        out_shape=jax.ShapeDtypeStruct((depth * 8 * rows, width), own.dtype),
-        in_specs=[pl.BlockSpec(memory_space=pl.ANY)],
-        out_specs=pl.BlockSpec(memory_space=pl.ANY),
-        scratch_shapes=Gather.scratch(depth),
-        compiler_params=pltpu.CompilerParams(collective_id=collective_id, has_side_effects=True),
-    )(own)
+        return [pltpu.SemaphoreType.DMA(()), pltpu.SemaphoreType.DMA((depth * 8,)), pltpu.SemaphoreType.DMA((depth * 8,))]
+
+
+EXCHANGE_ORDER = (0, 1, 2, 3)
+ROUTES = ("zf", "zf")
+ADD_ROWS = 32
+
+
+def merged(main, side, ahead=0):
+    steps, done = list(main[:ahead]), 0
+    rest = main[ahead:]
+    for n, step in enumerate(rest):
+        upto = (n + 1) * len(side) // len(rest)
+        steps += side[done:upto] + [step]
+        done = upto
+    return steps
+
+
+def interleaved(parts):
+    most = max(len(part.steps) for part in parts)
+    return [part.steps[n] for n in range(most) for part in parts if n < len(part.steps)]
+
+
+def gather_parts(depth, full, routes, own_ref, all_ref, scratch):
+    me = Place(depth)
+    rows = full // len(routes)
+    return [
+        Gather(me, full, n * rows, rows, route, own_ref, all_ref, *scratch[3 * n : 3 * n + 3]) for n, route in enumerate(routes)
+    ]
+
+
+def gather_scratch(depth, routes):
+    return [
+        pltpu.SemaphoreType.DMA(()),
+        pltpu.SemaphoreType.DMA((9 + 8 * (depth - 1) + 2 * depth,)),
+        pltpu.SemaphoreType.DMA((depth * 8,)),
+    ] * len(routes)
 
 
 class Scatter:
-    def __init__(self, depth, rows, part_ref, out_ref, sums, from_sib, from_last, from_first, from_below, from_above,
+    def __init__(self, me, full, offset, rows, route, part_ref, out_ref, sums, from_sib, from_last, from_first, from_below, from_above,
                  loads, send_sib, send_last, send_first, send_line, got_sib, got_last, got_first, got_below, got_above):
-        self.me, self.rows, self.step = Place(depth), rows, min(rows, 16)
+        self.me, self.full, self.offset, self.rows, self.route, self.step = me, full, offset, rows, route, min(rows, ADD_ROWS)
         self.part_ref, self.out_ref, self.sums, self.loads = part_ref, out_ref, sums, loads
         self.sib, self.last, self.first = (from_sib, send_sib, got_sib), (from_last, send_last, got_last), (from_first, send_first, got_first)
         self.up, self.down = (from_below, send_line, got_below), (from_above, send_line, got_above)
-        me = self.me
-        self.zs = [me.far(i) for i in range(depth)]
+        self.zs = [me.far(i) for i in range(me.depth)]
         chip = [functools.partial(self.chip, z) for z in self.zs]
         plane = [functools.partial(self.plane, z) for z in self.zs]
         line = [functools.partial(self.line, z) for z in self.zs[:-1]] + [self.final]
-        self.steps = [self.begin, chip[0]]
-        for i in range(1, depth + 2):
-            if i < depth:
-                self.steps.append(chip[i])
-            if i <= depth:
-                self.steps.append(plane[i - 1])
-            if i >= 2:
-                self.steps.append(line[i - 2])
+        lag = 1 if route == "zf" else 0
+        self.steps = [self.begin] + chip
+        for i in range(me.depth + lag):
+            self.steps += plane[i : i + 1] + (line[i - lag : i - lag + 1] if i >= lag else [])
 
     def source(self, z, f, l, core):
-        me = self.me
-        return self.part_ref.at[pl.ds(pl.multiple_of(me.shard(z, f, l, core) * self.rows, self.rows), self.rows)]
+        row = self.me.shard(z, f, l, core) * self.full + self.offset
+        return self.part_ref.at[pl.ds(pl.multiple_of(row, self.rows), self.rows)]
 
     def at(self, z, f, l):
         return z * 4 + f * 2 + l
@@ -575,7 +617,7 @@
         @pl.loop(0, self.rows // self.step)
         def _(i):
             part = pl.ds(pl.multiple_of(i * self.step, self.step), self.step)
-            target[part, :] = (target[part, :].astype(jnp.float32) + source[part, :].astype(jnp.float32)).astype(target.dtype)
+            target[part, :] = target[part, :] + source[part, :]
 
     def copy(self, stage, source, slot, device, send_slot=None):
         landing, send, got = stage
@@ -592,8 +634,18 @@
         me = self.me
         return self.copy(self.first, self.sums.at[self.at(z, 1 - me.f, me.l)], z, me.first())
 
-    def mine(self, z):
-        return self.sums.at[self.at(z, self.me.f, self.me.l)]
+    def held(self, z, f):
+        return self.sums.at[self.at(z, f, self.me.l)]
+
+    def slot(self, z, f):
+        return z if self.route == "zf" else z * 2 + f
+
+    def along(self, z, f):
+        slot = self.slot(z, f)
+        return (
+            lambda: self.copy(self.up, self.held(z, f), slot, self.me.above()),
+            lambda: self.copy(self.down, self.held(z, f), slot, self.me.below()),
+        )
 
     def load(self, z, f, l):
         k = self.at(z, f, l)
@@ -602,6 +654,9 @@
     def pairs(self):
         me = self.me
         return [(f, l) for l in (1 - me.l, me.l) for f in (1 - me.f, me.f)]
+
+    def sides(self):
+        return (self.me.f,) if self.route == "zf" else (1 - self.me.f, self.me.f)
 
     def begin(self):
         me = self.me
@@ -625,52 +680,62 @@
     def plane(self, z):
         me = self.me
         for f in (1 - me.f, me.f):
-            k = self.at(z, f, me.l)
             self.to_last(z, f).wait_recv()
-            self.add(self.sums.at[k], self.last[0].at[z * 2 + f])
-        self.to_first(z).start()
+            self.add(self.held(z, f), self.last[0].at[z * 2 + f])
+        if self.route == "zf":
+            self.to_first(z).start()
+
+    def from_other_half(self, z):
+        self.to_first(z).wait_recv()
+        self.add(self.held(z, self.me.f), self.first[0].at[z])
 
     def line(self, z):
         me = self.me
-        self.to_first(z).wait_recv()
-        self.add(self.mine(z), self.first[0].at[z])
-        upward, downward = self.copy(self.up, self.mine(z), z, me.above()), self.copy(self.down, self.mine(z), z, me.below())
-
-        @pl.when((z > me.z) & (me.z > 0))
-        def _():
-            upward.wait_recv()
-            self.add(self.mine(z), self.up[0].at[z])
-
-        @pl.when((z < me.z) & (me.z < me.top))
-        def _():
-            downward.wait_recv()
-            self.add(self.mine(z), self.down[0].at[z])
-
-        @pl.when(z > me.z)
-        def _():
-            upward.start()
-
-        @pl.when(z < me.z)
-        def _():
-            downward.start()
+        if self.route == "zf":
+            self.from_other_half(z)
+        for f in self.sides():
+            upward, downward = self.along(z, f)
+
+            @pl.when((z > me.z) & (me.z > 0))
+            def _():
+                upward().wait_recv()
+                self.add(self.held(z, f), self.up[0].at[self.slot(z, f)])
+
+            @pl.when((z < me.z) & (me.z < me.top))
+            def _():
+                downward().wait_recv()
+                self.add(self.held(z, f), self.down[0].at[self.slot(z, f)])
+
+            @pl.when(z > me.z)
+            def _():
+                upward().start()
+
+            @pl.when(z < me.z)
+            def _():
+                downward().start()
 
     def final(self):
         me = self.me
         z = me.z
-        self.to_first(z).wait_recv()
-        self.add(self.mine(z), self.first[0].at[z])
-
-        @pl.when(z > 0)
-        def _():
-            self.copy(self.up, self.mine(z), z, me.above()).wait_recv()
-            self.add(self.mine(z), self.up[0].at[z])
-
-        @pl.when(z < me.top)
-        def _():
-            self.copy(self.down, self.mine(z), z, me.below()).wait_recv()
-            self.add(self.mine(z), self.down[0].at[z])
-
-        self.out_ref[...] = self.mine(z)[...].astype(self.out_ref.dtype)
+        if self.route == "zf":
+            self.from_other_half(z)
+        for f in self.sides():
+            upward, downward = self.along(z, f)
+
+            @pl.when(z > 0)
+            def _():
+                upward().wait_recv()
+                self.add(self.held(z, f), self.up[0].at[self.slot(z, f)])
+
+            @pl.when(z < me.top)
+            def _():
+                downward().wait_recv()
+                self.add(self.held(z, f), self.down[0].at[self.slot(z, f)])
+
+        if self.route != "zf":
+            self.to_first(z).start()
+            self.from_other_half(z)
+        self.out_ref[pl.ds(self.offset, self.rows), :] = self.held(z, me.f)[...].astype(self.out_ref.dtype)
 
     def finish(self):
         me = self.me
@@ -679,37 +744,32 @@
                 self.to_sibling(z, f, l).wait_send()
             for f in (1 - me.f, me.f):
                 self.to_last(z, f).wait_send()
-            self.to_first(z).wait_send()
+            if self.route == "zf" or i == me.top:
+                self.to_first(z).wait_send()
             if i < me.top:
-                self.copy(self.up, self.mine(z), z, me.above()).wait_send()
-
-    @staticmethod
-    def scratch(depth, shard, dtype):
-        dma = pltpu.SemaphoreType.DMA
-        counts = [depth * 4, depth * 4, depth * 2, depth, depth, depth]
-        sems = [depth * 4, depth * 4, depth * 2, depth, depth, depth * 4, depth * 2, depth, depth, depth]
-        return [pltpu.VMEM((count, *shard), dtype) for count in counts] + [dma((count,)) for count in sems]
-
-
-def scatter_kernel(depth, rows, part_ref, out_ref, *scratch):
-    scatter = Scatter(depth, rows, part_ref, out_ref, *scratch)
-    scatter.me.greet()
-    for step in scatter.steps:
-        step()
-    scatter.finish()
-
-
-def scatter_sum(part, depth, collective_id, out_dtype):
-    tokens, width = part.shape
-    rows = tokens // (depth * 8)
-    return pl.pallas_call(
-        functools.partial(scatter_kernel, depth, rows),
-        out_shape=jax.ShapeDtypeStruct((rows, width), out_dtype),
-        in_specs=[pl.BlockSpec(memory_space=pl.ANY)],
-        out_specs=pl.BlockSpec(memory_space=pltpu.VMEM),
-        scratch_shapes=Scatter.scratch(depth, (rows, width), part.dtype),
-        compiler_params=pltpu.CompilerParams(collective_id=collective_id, has_side_effects=True, vmem_limit_bytes=48 << 20),
-    )(part)
+                for f in self.sides():
+                    self.along(z, f)[0]().wait_send()
+
+
+def scatter_parts(depth, full, routes, part_ref, out_ref, scratch):
+    me = Place(depth)
+    rows = full // len(routes)
+    each = len(scratch) // len(routes)
+    return [
+        Scatter(me, full, n * rows, rows, route, part_ref, out_ref, *scratch[each * n : each * (n + 1)]) for n, route in enumerate(routes)
+    ]
+
+
+def scatter_scratch(depth, full, width, dtype, routes):
+    dma = pltpu.SemaphoreType.DMA
+    scratch = []
+    for route in routes:
+        line = depth if route == "zf" else depth * 2
+        counts = [depth * 4, depth * 4, depth * 2, depth, line, line]
+        sems = [depth * 4, depth * 4, depth * 2, depth, line, depth * 4, depth * 2, depth, line, line]
+        scratch += [pltpu.VMEM((count, full // len(routes), width), dtype) for count in counts]
+        scratch += [dma((count,)) for count in sems]
+    return scratch
 
 
 LANES = 128
@@ -725,7 +785,7 @@
     return pltpu.roll(block, LANES // 2, 1)
 
 
-def split_kernel(parts, width, *refs):
+def split_blocks(parts, width, *refs):
     scale_ref, extra_ref, out_ref = refs[len(parts) :]
     depth = out_ref.shape[1]
     low = low_half((depth, LANES))
@@ -755,18 +815,60 @@
                 out_ref[2 * m + 1, :, lanes] = odd.astype(out_ref.dtype)
             base += (count + 1) // 2
 
-
-def split_blocks(arrays, parts, scale, extra):
-    depth = arrays[0].shape[0]
-    width = arrays[0].shape[1] // parts[0]
-    padded = sum((count + 1) // 2 for count in parts) * LANES
+def head_kernel(depth, full, routes, parts_out, width, inputs_ref, w_in_ref, w_out_ref, scale_ref, extra_ref, all_ref, got_ref,
+                hat_ref, blocks_ref, w_in, w_out, loads, *scratch):
+    copies = [
+        pltpu.make_async_copy(source, target, loads.at[n]) for n, (source, target) in enumerate(((w_in_ref, w_in), (w_out_ref, w_out)))
+    ]
+    for copy in copies:
+        copy.start()
+
+    @pl.loop(0, full // 32)
+    def _(i):
+        rows = pl.ds(pl.multiple_of(i * 32, 32), 32)
+        hat_ref[rows, :] = layer_norm(inputs_ref[rows, :].astype(jnp.float32))[0].astype(hat_ref.dtype)
+
+    count = len(gather_scratch(depth, routes))
+    parts = gather_parts(depth, full, routes, hat_ref, all_ref, scratch[:count])
+    exchange = Exchange(parts[0].me, blocks_ref, got_ref, *scratch[count:])
+    parts[0].me.greet_all()
+    steps = interleaved(parts)
+    for step in steps[: len(parts)]:
+        step()
+    for copy in copies:
+        copy.wait()
+    split_blocks(parts_out, width, w_in, w_out, scale_ref, extra_ref, blocks_ref)
+    for step in merged(steps[len(parts) :], exchange.steps):
+        step()
+    for part in parts + [exchange]:
+        part.finish()
+
+
+def head(inputs, w_in, w_out, parts_out, scale, extra, depth, routes, collective_id):
+    rows, width = inputs.shape
+    own = w_in.shape[0]
+    devices = depth * 8
+    blocks = (devices, own, sum((count + 1) // 2 for count in parts_out) * LANES)
+    here, vmem = pl.BlockSpec(memory_space=pl.ANY), pl.BlockSpec(memory_space=pltpu.VMEM)
     return pl.pallas_call(
-        functools.partial(split_kernel, parts, width),
-        out_shape=jax.ShapeDtypeStruct((width // HD, depth, padded), arrays[0].dtype),
-        in_specs=[pl.BlockSpec(memory_space=pltpu.VMEM)] * (len(parts) + 2),
-        out_specs=pl.BlockSpec(memory_space=pltpu.VMEM),
-        compiler_params=pltpu.CompilerParams(vmem_limit_bytes=24 << 20),
-    )(*arrays, scale, extra)
+        functools.partial(head_kernel, depth, rows, routes, parts_out, width),
+        out_shape=(
+            jax.ShapeDtypeStruct((devices * rows, width), inputs.dtype),
+            jax.ShapeDtypeStruct(blocks, inputs.dtype),
+        ),
+        in_specs=[vmem, here, here, vmem, vmem],
+        out_specs=(here, here),
+        scratch_shapes=[
+            pltpu.VMEM((rows, width), inputs.dtype),
+            pltpu.VMEM(blocks, inputs.dtype),
+            pltpu.VMEM(w_in.shape, w_in.dtype),
+            pltpu.VMEM(w_out.shape, w_out.dtype),
+            pltpu.SemaphoreType.DMA((2,)),
+        ]
+        + gather_scratch(depth, routes)
+        + Exchange.scratch(depth),
+        compiler_params=pltpu.CompilerParams(collective_id=collective_id, has_side_effects=True, vmem_limit_bytes=32 << 20),
+    )(inputs, w_in, w_out, scale, extra)
 
 
 def join_kernel(parts, width, blocks_ref, out_ref, extra_ref):
@@ -829,34 +931,65 @@
     return (key >= start) & (key <= query)
 
 
-def forward_kernel(depth, shard_rows, joint_width, hat_ref, weights_ref, bias_ref, cos_ref, sin_ref, start_ref, out_bias_ref, grad_ref,
-                   qk_ref, mid_ref, joined_ref, out_ref, grads_ref, keys_ref, values_ref, *scratch):
+def document_starts(weights_ref, lanes, first, count):
+    pieces = []
+    for shard in range(count):
+        rows = pl.ds(pl.multiple_of((first + shard) * HD, HD), HD)
+        block = weights_ref[rows, lanes].astype(jnp.float32)
+        pieces += [block[:, HD + 2 + n : HD + 3 + n] * 256.0 + block[:, HD + 4 + n : HD + 5 + n] for n in range(2)]
+    return jnp.concatenate(pieces, 0)
+
+
+def forward_kernel(depth, shard_rows, joint_width, routes, hat_ref, weights_ref, bias_ref, waves_ref, out_bias_ref, grad_ref,
+                   qk_ref, mid_ref, cos_ref, sin_ref, joined_ref, out_ref, grads_ref, keys_ref, values_ref, shift_ref, *scratch):
     seq = hat_ref.shape[0]
     here = pl.program_id(0)
     low = low_half((SIDE, LANES))
     lane = lax.broadcasted_iota(jnp.int32, (SIDE, LANES), 1)
     scaling = HD ** (-0.5)
-    gather = Gather(depth, shard_rows, grad_ref, grads_ref, *scratch)
+    parts = gather_parts(depth, shard_rows, routes, grad_ref, grads_ref, scratch)
     chunks = seq // SIDE
-    slots = spread_steps([gather.me.greet] + gather.steps, depth * chunks, [gather.finish])
+    slots = spread_steps([parts[0].me.greet] + interleaved(parts), len(parts), depth * 2 * chunks, [part.finish for part in parts])
+    side_lanes = slice(joint_width - LANES, joint_width)
+
     for q in range(chunks):
-        run_slots(slots, here, q, depth, chunks)
+        run_slots(slots, here, 2 * q, depth, 2 * chunks)
+        if q == 0:
+
+            @pl.when(here == 0)
+            def _():
+                total = bias_ref[...]
+                for n in range(weights_ref.shape[0] // SIDE):
+                    some = slice(n * SIDE, (n + 1) * SIDE)
+                    side = weights_ref[some, side_lanes].astype(jnp.float32)
+                    ratio = side[:, HD + 1 : HD + 2] / side[:, HD : HD + 1]
+                    total = total + jnp.sum(ratio * weights_ref[some, :joint_width].astype(jnp.float32), 0, keepdims=True)
+                shift_ref[...] = total
+
         rows = slice(q * SIDE, (q + 1) * SIDE)
-        joint = jnp.dot(hat_ref[rows, :], weights_ref[:, :joint_width], preferred_element_type=jnp.float32) + bias_ref[...]
+        joint = jnp.dot(hat_ref[rows, :], weights_ref[:, :joint_width], preferred_element_type=jnp.float32) + shift_ref[...]
+        per_chunk = SIDE // shard_rows
+        start = document_starts(weights_ref, side_lanes, (here * chunks + q) * per_chunk, per_chunk)
+        index = q * SIDE + lax.broadcasted_iota(jnp.int32, (SIDE, 1), 0)
+        angles = (index.astype(jnp.float32) - start) * waves_ref[0:1, :]
+        cosine, sine = jnp.cos(angles), jnp.sin(angles) * waves_ref[1:2, :]
+        cos_ref[rows, :] = cosine
+        sin_ref[rows, :] = sine
         qk = joint[:, :LANES]
-        qk = (qk * cos_ref[rows, :] + turned(qk, lane) * sin_ref[rows, :])
+        qk = qk * cosine + turned(qk, lane) * sine
         keys_ref[rows, :] = swap_halves(qk).astype(jnp.bfloat16)
         query = jnp.where(low, qk * scaling, 0.0).astype(jnp.bfloat16)
         qk_ref[rows, :] = qk.astype(jnp.bfloat16)
         values_ref[rows, :] = jnp.where(low, joint[:, LANES : 2 * LANES], 0.0).astype(jnp.bfloat16)
         count = (q + 1) * SIDE
         scores = lax.dot_general(query, keys_ref[:count, :], NT, preferred_element_type=jnp.float32)
-        scores = jnp.where(allowed_keys(start_ref[rows, :], q * SIDE, count), scores, negative)
+        scores = jnp.where(allowed_keys(start.astype(jnp.int32), q * SIDE, count), scores, negative)
         largest = jnp.max(scores, -1, keepdims=True)
         weights = jnp.exp(scores - largest)
         total = jnp.sum(weights, -1, keepdims=True)
         weights = (weights * (1.0 / total)).astype(jnp.bfloat16)
         attended = jnp.dot(weights, values_ref[:count, :], preferred_element_type=jnp.float32)
+        run_slots(slots, here, 2 * q + 1, depth, 2 * chunks)
         lse = largest + jnp.log(total)
         mid_ref[rows, : 2 * LANES] = joint[:, LANES : 3 * LANES]
         mid_ref[rows, 2 * LANES :] = jnp.where(low, joint[:, 3 * LANES :], lse)
@@ -872,26 +1005,28 @@
             step()
 
 
-def spread_steps(steps, count, after):
+def spread_steps(steps, ahead, count, after):
     slots = [[] for _ in range(count + 1)]
-    for n, step in enumerate(steps):
-        slots[max(n - 1, 0) * (count - 1) // max(len(steps) - 2, 1) if n else 0].append(step)
+    slots[0] += steps[: 1 + ahead]
+    rest = steps[1 + ahead :]
+    for n, step in enumerate(rest):
+        slots[n * count // len(rest)].append(step)
     slots[-1] = list(after)
     return slots
 
 
-def run_slots(slots, here, q, blocks, chunks):
+def run_slots(slots, here, q, blocks, chunks, first=0):
     for block in range(blocks):
         steps = slots[block * chunks + q]
         if steps:
 
-            @pl.when(here == block)
+            @pl.when(here == block + first)
             def _():
                 for step in steps:
                     step()
 
 
-def forward(hat_all, weights, joint_width, bias, cosine, sine, start, out_bias, grads, depth, seq, collective_id):
+def forward(hat_all, weights, joint_width, bias, waves, out_bias, grads, depth, seq, routes, collective_id):
     tokens, width = hat_all.shape
     joined_width = weights.shape[1] - joint_width
 
@@ -901,45 +1036,68 @@
     def whole(array):
         return pl.BlockSpec(array.shape, lambda b: (0, 0), pipeline_mode=pl.Buffered(1))
 
+    def out(columns, kind):
+        return jax.ShapeDtypeStruct((tokens, columns), kind)
+
     return pl.pallas_call(
-        functools.partial(forward_kernel, depth, grads.shape[0], joint_width),
+        functools.partial(forward_kernel, depth, grads.shape[0], joint_width, routes),
         grid=(tokens // seq,),
         out_shape=(
-            jax.ShapeDtypeStruct((tokens, LANES), jnp.bfloat16),
-            jax.ShapeDtypeStruct((tokens, joined_width), jnp.float32),
-            jax.ShapeDtypeStruct((tokens, joined_width), jnp.bfloat16),
-            jax.ShapeDtypeStruct((tokens, width), jnp.bfloat16),
-            jax.ShapeDtypeStruct((tokens, width), jnp.bfloat16),
+            out(LANES, jnp.bfloat16),
+            out(joined_width, jnp.float32),
+            out(LANES, jnp.float32),
+            out(LANES, jnp.float32),
+            out(joined_width, jnp.bfloat16),
+            out(width, jnp.bfloat16),
+            out(width, jnp.bfloat16),
         ),
-        in_specs=[rows(width), whole(weights), whole(bias), rows(LANES), rows(LANES), rows(1), whole(out_bias), pl.BlockSpec(memory_space=pl.ANY)],
-        out_specs=(rows(LANES), rows(joined_width), rows(joined_width), rows(width), pl.BlockSpec(memory_space=pl.ANY)),
-        scratch_shapes=[pltpu.VMEM((seq, LANES), jnp.bfloat16), pltpu.VMEM((seq, LANES), jnp.bfloat16)] + Gather.scratch(depth),
+        in_specs=[rows(width), whole(weights), whole(bias), whole(waves), whole(out_bias), pl.BlockSpec(memory_space=pl.ANY)],
+        out_specs=(
+            rows(LANES), rows(joined_width), rows(LANES), rows(LANES), rows(joined_width), rows(width),
+            pl.BlockSpec(memory_space=pl.ANY),
+        ),
+        scratch_shapes=[pltpu.VMEM((seq, LANES), jnp.bfloat16)] * 2
+        + [pltpu.VMEM((1, joint_width), jnp.float32)]
+        + gather_scratch(depth, routes),
         compiler_params=pltpu.CompilerParams(collective_id=collective_id, has_side_effects=True, vmem_limit_bytes=56 << 20),
-    )(hat_all, weights, bias, cosine, sine, start, out_bias, grads)
-
-
-def backward_kernel(depth, shard_rows, joint_width, grad_ref, weights_ref, qk_ref, mid_ref, cos_ref, sin_ref, start_ref, branch_ref,
-                    d_joint_ref, d_hat_ref, sums_ref, own_ref, keys_ref, values_ref, d_key_ref, d_value_ref, d_query_ref, *scratch):
-    seq = grad_ref.shape[0]
+    )(hat_all, weights, bias, waves, out_bias, grads)
+
+
+LATEST = 27
+
+
+def backward_kernel(depth, shard_rows, joint_width, routes, grad_ref, hat_ref, weights_ref, qk_ref, mid_ref, cos_ref, sin_ref, branch_ref,
+                    d_hat_ref, sums_ref, back_ref, own_ref,
+                    keys_ref, values_ref, d_key_ref, d_value_ref, d_query_ref, d_joint_ref, total_ref, *scratch):
+    seq = qk_ref.shape[0]
+    chunks = seq // SIDE
+    here, stage = pl.program_id(0), pl.program_id(1)
     low = low_half((SIDE, LANES))
     lane = lax.broadcasted_iota(jnp.int32, (SIDE, LANES), 1)
     scaling = HD ** (-0.5)
-    d_key_ref[...] = jnp.zeros_like(d_key_ref)
-    d_value_ref[...] = jnp.zeros_like(d_value_ref)
-
-    here = pl.program_id(0)
-    scatter = Scatter(depth, shard_rows, branch_ref, own_ref, *scratch)
-    chunks = seq // SIDE
-    slots = spread_steps([scatter.me.greet] + scatter.steps, depth * 2 * chunks, [scatter.finish])
-
-    @pl.when(here == 0)
-    def _():
-        sums_ref[...] = jnp.zeros_like(sums_ref)
-
-    for q in range(chunks):
-        run_slots(slots, here, q, depth, 2 * chunks)
-        rows = slice(q * SIDE, (q + 1) * SIDE)
-        d_joined = jnp.dot(grad_ref[rows, :], weights_ref[:, joint_width:], preferred_element_type=jnp.float32)
+    side_lanes = slice(joint_width - LANES, joint_width)
+    parts = scatter_parts(depth, shard_rows, routes, branch_ref, own_ref, scratch)
+    main, ahead = interleaved(parts), (1 + depth) * len(parts)
+    slots = [[] for _ in range(depth * 2 * chunks)] + [[part.finish for part in parts]]
+    slots[0] += [parts[0].me.greet] + main[: len(parts)]
+    for n, step in enumerate(main[len(parts) : ahead]):
+        slots[1 + n // len(parts)].append(step)
+    for n, step in enumerate(main[ahead:]):
+        slots[1 + depth + n * LATEST // (len(main) - ahead)].append(step)
+
+    def first_stage(q, rows):
+        if q == 0:
+            d_key_ref[...] = jnp.zeros_like(d_key_ref)
+            d_value_ref[...] = jnp.zeros_like(d_value_ref)
+
+            @pl.when(here == 0)
+            def _():
+                sums_ref[...] = jnp.zeros_like(sums_ref)
+                total_ref[...] = jnp.zeros_like(total_ref)
+
+        d_joined = jnp.dot(grad_ref[...], weights_ref[:, joint_width:], preferred_element_type=jnp.float32)
+        per_chunk = SIDE // shard_rows
+        start = document_starts(weights_ref, side_lanes, (here * chunks + q) * per_chunk, per_chunk).astype(jnp.int32)
         qk = qk_ref[rows, :].astype(jnp.float32)
         keys_ref[rows, :] = jnp.where(low, swap_halves(qk), 0.0).astype(jnp.bfloat16)
         query = jnp.where(low, qk * scaling, 0.0).astype(jnp.bfloat16)
@@ -948,7 +1106,7 @@
         count = (q + 1) * SIDE
         lse = mid_ref[rows, 3 * LANES - 1 : 3 * LANES]
         scores = lax.dot_general(query, keys_ref[:count, :], NT, preferred_element_type=jnp.float32)
-        weights = jnp.where(allowed_keys(start_ref[rows, :], q * SIDE, count), jnp.exp(scores - lse), 0.0)
+        weights = jnp.where(allowed_keys(start, q * SIDE, count), jnp.exp(scores - lse), 0.0)
         d_weights = lax.dot_general(d_out, values_ref[:count, :], NT, preferred_element_type=jnp.float32)
         moved = weights * d_weights
         d_scores = (moved - weights * jnp.sum(moved, -1, keepdims=True)).astype(jnp.bfloat16)
@@ -963,9 +1121,8 @@
         d_joint_ref[rows, 3 * LANES :] = jnp.where(
             low, d_joined[:, 2 * LANES :] * gelu_slope(mid_ref[rows, 2 * LANES :]), 0.0
         ).astype(jnp.bfloat16)
-    for q in range(chunks):
-        run_slots(slots, here, chunks + q, depth, 2 * chunks)
-        rows = slice(q * SIDE, (q + 1) * SIDE)
+
+    def second_stage(q, rows):
         d_qk = jnp.where(low, d_query_ref[rows, :], swap_halves(d_key_ref[rows, :]))
         d_qk = d_qk * cos_ref[rows, :] - turned(d_qk, lane) * sin_ref[rows, :]
         d_joint_ref[rows, :LANES] = d_qk.astype(jnp.bfloat16)
@@ -975,50 +1132,167 @@
         d_joint = d_joint_ref[rows, :]
         sums_ref[...] += jnp.sum(d_joint.astype(jnp.float32), 0, keepdims=True)
         d_hat = lax.dot_general(d_joint, weights_ref[:, :joint_width], NT, preferred_element_type=jnp.float32)
-        d_hat_ref[rows, :] = d_hat.astype(jnp.bfloat16)
-
-    @pl.when(here == pl.num_programs(0) - 1)
+        d_hat_ref[...] = d_hat.astype(jnp.bfloat16)
+        if q % 2 == 1:
+            both = slice(rows.start - SIDE, rows.stop)
+            total_ref[...] += lax.dot_general(d_joint_ref[both, :], hat_ref[...], TN, preferred_element_type=jnp.float32)
+
+    for at in range(2 * chunks):
+
+        @pl.when(stage == at)
+        def _():
+            run_slots(slots, here, at, depth, 2 * chunks)
+            rows = slice(at % chunks * SIDE, (at % chunks + 1) * SIDE)
+            if at < chunks:
+                first_stage(at, rows)
+            else:
+                second_stage(at - chunks, rows)
+
+    @pl.when((here == pl.num_programs(0) - 1) & (stage == 2 * chunks - 1))
     def _():
+        side_lane = lax.broadcasted_iota(jnp.int32, (SIDE, LANES), 1)
+        for n in range(back_ref.shape[0] // SIDE):
+            some = slice(n * SIDE, (n + 1) * SIDE)
+            side = weights_ref[some, side_lanes].astype(jnp.float32)
+            gain, shift = side[:, HD : HD + 1], side[:, HD + 1 : HD + 2]
+            weight = weights_ref[some, :joint_width].astype(jnp.float32)
+            total = total_ref[:, some].T
+            back = gain * total + shift * sums_ref[...]
+            gain_part = jnp.sum(weight * total, 1, keepdims=True) / gain
+            shift_part = jnp.sum(weight * sums_ref[...], 1, keepdims=True) / gain
+            last = jnp.where(side_lane == HD, gain_part, back[:, side_lanes])
+            last = jnp.where(side_lane == HD + 1, shift_part, last)
+            back_ref[some, : joint_width - LANES] = back[:, : joint_width - LANES].astype(jnp.bfloat16)
+            back_ref[some, side_lanes] = last.astype(jnp.bfloat16)
         for step in slots[-1]:
             step()
 
 
-def backward(grad_all, weights, joint_width, qk, mid, cosine, sine, start, branch, depth, seq, collective_id):
+def backward(grad_all, hat_all, weights, joint_width, qk, mid, cosine, sine, branch, depth, seq, routes, collective_id):
     tokens, width = grad_all.shape
     joined_width = weights.shape[1] - joint_width
     own = tokens // (depth * 8)
+    chunks = seq // SIDE
 
     def rows(columns):
-        return pl.BlockSpec((seq, columns), lambda b: (b, 0))
-
-    def whole(array):
-        return pl.BlockSpec(array.shape, lambda b: (0, 0), pipeline_mode=pl.Buffered(1))
+        return pl.BlockSpec((seq, columns), lambda b, s: (b, 0))
+
+    def whole(shape, **mode):
+        return pl.BlockSpec(shape, lambda b, s: (0, 0), **mode)
+
+    def early(columns):
+        return pl.BlockSpec((SIDE, columns), lambda b, s: (b * chunks + jnp.minimum(s, chunks - 1), 0))
+
+    def late(columns):
+        return pl.BlockSpec((SIDE, columns), lambda b, s: (b * chunks + jnp.maximum(s - chunks, 0), 0))
 
     return pl.pallas_call(
-        functools.partial(backward_kernel, depth, own, joint_width),
-        grid=(tokens // seq,),
+        functools.partial(backward_kernel, depth, own, joint_width, routes),
+        grid=(tokens // seq, 2 * chunks),
         out_shape=(
-            jax.ShapeDtypeStruct((tokens, joint_width), jnp.bfloat16),
             jax.ShapeDtypeStruct((tokens, width), jnp.bfloat16),
             jax.ShapeDtypeStruct((1, joint_width), jnp.float32),
+            jax.ShapeDtypeStruct((width, joint_width), jnp.bfloat16),
             jax.ShapeDtypeStruct((own, width), jnp.bfloat16),
         ),
-        in_specs=[rows(width), whole(weights), rows(LANES), rows(joined_width), rows(LANES), rows(LANES), rows(1), pl.BlockSpec(memory_space=pl.ANY)],
-        out_specs=(
-            rows(joint_width),
-            rows(width),
-            pl.BlockSpec((1, joint_width), lambda b: (0, 0)),
-            pl.BlockSpec((own, width), lambda b: (0, 0)),
-        ),
+        in_specs=[
+            early(width),
+            pl.BlockSpec((2 * SIDE, width), lambda b, s: ((b * chunks + jnp.maximum(s - chunks, 0)) // 2, 0)),
+            whole(weights.shape, pipeline_mode=pl.Buffered(1)),
+            rows(LANES), rows(joined_width), rows(LANES), rows(LANES), pl.BlockSpec(memory_space=pl.ANY),
+        ],
+        out_specs=(late(width), whole((1, joint_width)), whole((width, joint_width)), whole((own, width))),
         scratch_shapes=[pltpu.VMEM((seq, LANES), jnp.bfloat16)] * 2
         + [pltpu.VMEM((seq, LANES), jnp.float32)] * 3
-        + Scatter.scratch(depth, (own, width), branch.dtype),
+        + [pltpu.VMEM((seq, joint_width), jnp.bfloat16), pltpu.VMEM((joint_width, width), jnp.float32)]
+        + scatter_scratch(depth, own, width, branch.dtype, routes),
         compiler_params=pltpu.CompilerParams(collective_id=collective_id, has_side_effects=True, vmem_limit_bytes=63 << 20),
-    )(grad_all, weights, qk, mid, cosine, sine, start, branch)
-
-
-def exchange(blocks):
-    return lax.all_to_all(blocks, AXES, split_axis=0, concat_axis=0, tiled=True)
+    )(grad_all, hat_all, weights, qk, mid, cosine, sine, branch)
+
+
+def tail_kernel(depth, full, routes, joined_ref, grads_ref, part_ref, blocks_ref, inputs_ref, grad_ref,
+                out_ref, column_ref, got_in_ref, got_out_ref, total_ref, back_ref, *scratch):
+    here = pl.program_id(0)
+    count = len(scatter_scratch(depth, full, 1, part_ref.dtype, routes))
+    each = len(Exchange.scratch(depth))
+    parts = scatter_parts(depth, full, routes, part_ref, out_ref, scratch[:count])
+    me = parts[0].me
+    early = Exchange(me, blocks_ref, got_in_ref, *scratch[count : count + each])
+    late = Exchange(me, back_ref, got_out_ref, *scratch[count + each :])
+    chunks = part_ref.shape[0] // grads_ref.shape[0]
+    main, ahead = interleaved(parts), (1 + depth) * len(parts)
+    slots = [[] for _ in range(chunks)]
+    slots[0] += [me.greet_all] + main[: len(parts)] + early.steps
+    for n, step in enumerate(main[len(parts) : ahead]):
+        slots[1 + n // len(parts)].append(step)
+    slots[-1] += main[ahead : ahead + len(parts)]
+    for at in range(chunks):
+        run_slots(slots, here, at, 1, chunks, at)
+
+    @pl.when(here == 0)
+    def _():
+        total_ref[...] = jnp.zeros_like(total_ref)
+        column_ref[...] = jnp.zeros_like(column_ref)
+
+    grads = grads_ref[...]
+    column_ref[...] += jnp.sum(grads.astype(jnp.float32), 0, keepdims=True)
+    total_ref[...] += lax.dot_general(joined_ref[...], grads, TN, preferred_element_type=jnp.float32)
+
+    @pl.when(here == chunks - 1)
+    def _():
+        depth_rows = back_ref.shape[1]
+        for n in range(total_ref.shape[1] // SIDE):
+            turned_part = total_ref[:, n * SIDE : (n + 1) * SIDE].T.astype(back_ref.dtype)
+            for m in range(SIDE // depth_rows):
+                back_ref[n * (SIDE // depth_rows) + m] = turned_part[m * depth_rows : (m + 1) * depth_rows]
+        for step in late.steps + main[ahead + len(parts) :]:
+            step()
+
+        @pl.loop(0, full // 32)
+        def _(i):
+            rows = pl.ds(pl.multiple_of(i * 32, 32), 32)
+            hat, inv_std = layer_norm(inputs_ref[rows, :].astype(jnp.float32))
+            d_hat = out_ref[rows, :]
+            d_hat = d_hat - jnp.mean(d_hat, -1, keepdims=True) - hat * jnp.mean(d_hat * hat, -1, keepdims=True)
+            out_ref[rows, :] = inv_std * d_hat + grad_ref[rows, :].astype(jnp.float32)
+
+        for part in parts + [early, late]:
+            part.finish()
+
+
+def tail(joined, grads_all, part, blocks, inputs, grads, depth, routes, collective_id):
+    tokens, width = part.shape
+    joined_width = joined.shape[1]
+    devices = depth * 8
+    rows = tokens // devices
+    chunk = 2 * SIDE
+    back = (devices, width // devices, joined_width)
+    here = pl.BlockSpec(memory_space=pl.ANY)
+
+    def whole(shape, **mode):
+        return pl.BlockSpec(shape, lambda i: (0, 0), **mode)
+
+    def some(columns):
+        return pl.BlockSpec((chunk, columns), lambda i: (i, 0))
+
+    once = {"pipeline_mode": pl.Buffered(1)}
+    return pl.pallas_call(
+        functools.partial(tail_kernel, depth, rows, routes),
+        grid=(tokens // chunk,),
+        out_shape=(
+            jax.ShapeDtypeStruct((rows, width), jnp.float32),
+            jax.ShapeDtypeStruct((1, width), jnp.float32),
+            jax.ShapeDtypeStruct(blocks.shape, blocks.dtype),
+            jax.ShapeDtypeStruct(back, joined.dtype),
+        ),
+        in_specs=[some(joined_width), some(width), here, here, whole(inputs.shape, **once), whole(grads.shape, **once)],
+        out_specs=(whole((rows, width)), whole((1, width)), here, here),
+        scratch_shapes=[pltpu.VMEM((joined_width, width), jnp.float32), pltpu.VMEM(back, joined.dtype)]
+        + scatter_scratch(depth, rows, width, part.dtype, routes)
+        + Exchange.scratch(depth)
+        + Exchange.scratch(depth),
+        compiler_params=pltpu.CompilerParams(collective_id=collective_id, has_side_effects=True, vmem_limit_bytes=60 << 20),
+    )(joined, grads_all, part, blocks, inputs, grads)
 
 
 def on_device(
@@ -1030,11 +1304,11 @@
     me = lax.axis_index("dp") * lax.axis_size("ctx") + ctx
     tok_rows, model_width = hidden_in.shape[1:]
     seq_len = segment_ids.shape[1]
-    tokens = devices * tok_rows
     own = model_width // devices
     in_parts = in_bias.shape[0]
     out_parts = w_out_t.shape[1] // model_width
-    in_width, out_width = in_parts * own, out_parts * own
+    in_width = in_parts * own
+    joint_width = (in_parts + 1) // 2 * LANES
 
     gain, shift = ln_gain.astype(jnp.float32).T, ln_shift.astype(jnp.float32).T
     own_seg = lax.dynamic_slice_in_dim(segment_ids[0], ctx * tok_rows, tok_rows)
@@ -1043,62 +1317,29 @@
     extra = jnp.concatenate(
         [jnp.zeros((own, LANES // 2)), gain, shift, begin, jnp.zeros((own, LANES // 2 - 2 - begin.shape[1]))], 1
     )
-    got = exchange(split_blocks((w_in_t.T, w_out_t), (in_parts, out_parts), gain, extra))
-    joint_width = (in_parts + 1) // 2 * LANES
-
-    inputs = hidden_in[0].astype(jnp.float32)
-    average = jnp.mean(inputs, -1, keepdims=True)
-    centred = inputs - average
-    inv_std = lax.rsqrt(jnp.mean(centred * centred, -1, keepdims=True) + epsilon)
-    hat = centred * inv_std
-    hat_all = gather_all(hat.astype(jnp.bfloat16), depth, 0)
+    inputs = hidden_in[0]
+    hat_all, got = head(inputs, w_in_t.T, w_out_t, (in_parts, out_parts), gain, extra, depth, ("zf", "fz"), 0)
 
     weights = got.reshape(model_width, -1)
-    w_in = weights[:, :joint_width]
-    gain_all = w_in[:, in_width : in_width + 1].astype(jnp.float32)
-    shift_all = w_in[:, in_width + 1 : in_width + 2].astype(jnp.float32)
-    begin = got[:, :, in_width + 2 : in_width + 2 + 2 * tok_rows // own].astype(jnp.int32)
-    begin = begin.transpose(0, 2, 1).reshape(devices, 2, tok_rows)
-    begin = (begin[:, 0] * 256 + begin[:, 1]).reshape(tokens)
-    positions = (jnp.arange(tokens) % seq_len - begin).astype(jnp.float32)
     half = ROT // 2
     lane = jnp.arange(LANES) % HD
-    frequency = jnp.where(lane < ROT, 10000.0 ** (-2.0 * (lane % half).astype(jnp.float32) / ROT), 0.0)
-    angles = positions[:, None] * frequency[None, :]
-    cosine = jnp.cos(angles)
-    sine = jnp.sin(angles) * jnp.where(lane < half, -1.0, 1.0)[None]
-    bias = in_bias.astype(jnp.float32).reshape(1, in_width)
-    bias = jnp.pad(bias, ((0, 0), (0, joint_width - in_width)))
-    bias = bias + jnp.sum(shift_all / gain_all * w_in.astype(jnp.float32), 0, keepdims=True)
+    frequency = 10000.0 ** (-2.0 * (lane % half).astype(jnp.float32) / ROT)
+    waves = jnp.stack([jnp.where(lane < ROT, frequency, 0.0), jnp.where(lane < half, -1.0, 1.0)])
+    bias = jnp.pad(in_bias.astype(jnp.float32).reshape(1, in_width), ((0, 0), (0, joint_width - in_width)))
     column = jnp.arange(model_width) // own
     out_row = jnp.where(column == me, jnp.tile(out_bias.astype(jnp.float32), devices), 0.0)[None]
-    start = begin[:, None]
-    qk, mid, joined, branch, g_all = forward(
-        hat_all, weights, joint_width, bias, cosine, sine, start, out_row, out_grad[0], depth, seq_len, 1
-    )
-    d_joint, d_hat_part, joint_sums, branch_own = backward(
-        g_all, weights, joint_width, qk, mid, cosine, sine, start, branch, depth, seq_len, 2
-    )
-    result = (inputs + branch_own.astype(jnp.float32)).astype(jnp.bfloat16)
-    grad_out_local = lax.dot_general(g_all, joined, TN, preferred_element_type=jnp.float32).astype(jnp.bfloat16)
-    back_out = exchange(grad_out_local.reshape(devices, own, -1))
-    grad_hat = lax.dot_general(hat_all, d_joint, TN, preferred_element_type=jnp.float32)
-    weight_in = w_in.astype(jnp.float32)
-    gain_part = jnp.sum(weight_in * grad_hat, 1, keepdims=True) / gain_all
-    shift_part = jnp.sum(weight_in * joint_sums, 1, keepdims=True) / gain_all
-    back_lane = jnp.arange(joint_width)[None]
-    grad_in_local = gain_all * grad_hat + shift_all * joint_sums
-    grad_in_local = jnp.where(back_lane == in_width, gain_part, grad_in_local)
-    grad_in_local = jnp.where(back_lane == in_width + 1, shift_part, grad_in_local).astype(jnp.bfloat16)
-    back_in = exchange(grad_in_local.reshape(devices, own, -1))
-    d_hat = scatter_sum(d_hat_part, depth, 3, jnp.float32)
-    d_input = inv_std * (
-        d_hat - jnp.mean(d_hat, -1, keepdims=True) - hat * jnp.mean(d_hat * hat, -1, keepdims=True)
-    ) + out_grad[0].astype(jnp.float32)
-
+    qk, mid, cosine, sine, joined, branch, g_all = forward(
+        hat_all, weights, joint_width, bias, waves, out_row, out_grad[0], depth, seq_len, ("zf", "fz"), 1
+    )
+    d_hat_part, joint_sums, back_in, branch_own = backward(
+        g_all, hat_all, weights, joint_width, qk, mid, cosine, sine, branch, depth, seq_len, ROUTES, 2
+    )
+    result = (inputs.astype(jnp.float32) + branch_own.astype(jnp.float32)).astype(jnp.bfloat16)
+    d_input, column_sums, back_in, back_out = tail(
+        joined, g_all, d_hat_part, back_in.reshape(devices, own, -1), inputs, out_grad[0], depth, ROUTES, 3
+    )
     grad_w_out, _ = join_blocks(back_out, out_parts)
     grad_w_in, vectors = join_blocks(back_in, in_parts)
-    g_columns = lax.dynamic_slice_in_dim(g_all, me * own, own, 1)
     return (
         result[None],
         d_input[None],
@@ -1107,7 +1348,7 @@
         vectors[:, LANES // 2][None],
         vectors[:, LANES // 2 + 1][None],
         grad_w_out,
-        jnp.sum(g_columns.astype(jnp.float32), 0),
+        lax.dynamic_slice_in_dim(column_sums[0], me * own, own),
     )
 
 

time: 575 us -> 475 us (0.83)
  matrix products: 29.9 us -> 0 us
  other arithmetic: 32.7 us -> 4.93 us
  starting transfers between devices: 23.6 us -> 0 us
  Pallas kernels: 477 us -> 455 us
    dot_general x2 -> x0, matrix products: 29.9 us -> none  [the longest x1 15.7 us: on_device(): lax.dot_general(hat_all, d_joint, TN, preferred_element_type=jnp.float32)]
    all_to_all x3 -> x0, starting transfers between devices: 23.6 us -> none  [exchange(): return lax.all_to_all(blocks, AXES, split_axis=0, concat_axis=0, tiled=True)]
    pallas_call x1, Pallas kernels: 105 us -> 87.1 us  [forward(): pl.pallas_call(functools.partial(forward_kernel, depth, grads.shape[0], j...]
    mul x1 -> x0, other arithmetic: 9.34 us -> none  [on_device(): sine = jnp.sin(angles) * jnp.where(lane < half, -1.0, 1.0)[None]]
    reduce_sum x5 -> x0, other arithmetic: 6.24 us -> none  [the longest x1 2.36 us: on_device(): jnp.sum(g_columns.astype(jnp.float32), 0)]
    pallas_call x3 -> x2, Pallas kernels: 258 us -> 256 us  [the longest x1 132 us: head(): pl.pallas_call(functools.partial(head_kernel, depth, rows, routes, parts_...]
  transfers between devices with their start and end apart: 3 -> 0, of which waited for: 0 -> 0; matrix products, arithmetic and copies ran while one was open for 6% -> 0% of each run, Pallas kernels for 64% -> 0%
where the time goes in v4:
time: 475 us; the launch traced here: 474 us
  Pallas kernels  455 us (96%)
  local copies, waits for them, and re-layouts  13.4 us (3%)
  other arithmetic  4.93 us (1%)
    pallas_call x1, Pallas kernels, head(): pl.pallas_call(functools.partial(head_kernel, depth, rows, routes, parts_...  132 us
    pallas_call x1, Pallas kernels, tail(): pl.pallas_call(functools.partial(tail_kernel, depth, rows, routes), grid=...  125 us
    pallas_call x1, Pallas kernels, backward(): pl.pallas_call(functools.partial(backward_kernel, depth, own, joint_width...  105 us
    pallas_call x1, Pallas kernels, forward(): pl.pallas_call(functools.partial(forward_kernel, depth, grads.shape[0], j...  87.1 us

profile of v4, /device:TPU:0, one launch (start us, length us, event | category | flops | bytes accessed | tf_op | source)
XLA Modules:
  0.0 473.8 jit_solution(18419719662426319386)
XLA Ops:
  0.6 0.7 dynamic-slice_bitcast_fusion.1
  1.3 0.9 convert_reduce_fusion
  2.2 0.7 bitcast_convert_fusion.1
  2.8 0.7 bitcast_convert_fusion
  3.5 0.1 convert_element_type.42
  3.6 0.6 pad_maximum_fusion.waves_ref
  4.2 0.8 reshape.233
  5.0 0.6 pad_convert_fusion.bias_ref
  5.6 0.7 tile.4
  6.2 0.1 tile.10
  6.3 0.6 compare_select_fusion.out_bias_ref
  6.9 0.1 copy.25
  7.0 0.1 copy.28.scale_ref
  7.1 0.1 copy.27
  7.2 0.1 concatenate.3.extra_ref
  7.3 1.0 copy-done.1
  8.4 1.5 copy-done.4
  9.9 1.3 copy-done.6
  11.2 131.9 %shard_map.152 = (bf16[4096,2048]{1,0:T(8,128)(2,1)}, bf16[32,64,896]{2,1,0:T(8,128)(2,1)S(1)}) custom-call(bf16[128,2048]{1,0:T(8,128)(2,1)S(1)} %bitcast.42, bf16[64,14336]{1,0:T(8,128)(2,1)S(1)} %bitcast.43, bf16[64,10240]{1,0:T(8,128)(2,1)S(1)} %copy-done.6, f32[64,1]{1,0:T(8,128)S(1)} %copy.28.scale_ref, f32[64,128]{1,0:T(8,128)S(1)} %concatenate.3.extra_ref), custom_call_target="tpu_custom_call" | custom-call | tf_op jit(solution)/shard_map/pallas_call | solution.py:853
  143.1 1.8 copy-done
  144.9 87.1 %shard_map.153 = (bf16[4096,128]{1,0:T(8,128)(2,1)}, f32[4096,384]{1,0:T(8,128)}, f32[4096,128]{1,0:T(8,128)}, f32[4096,128]{1,0:T(8,128)}, bf16[4096,384]{1,0:T...) custom-call(bf16[4096,2048]{1,0:T(8,128)(2,1)} %get-tuple-element.28.hat_ref, ...), custom_call_target="tpu_custom_call" | custom-call | tf_op jit(solution)/shard_map/pallas_call | solution.py:1042
  232.1 104.6 %shard_map.154 = (bf16[4096,2048]{1,0:T(8,128)(2,1)}, f32[1,512]{1,0:T(1,128)}, bf16[2048,512]{1,0:T(8,128)(2,1)}, bf16[128,2048]{1,0:T(8,128)(2,1)}) custom-call(bf16[4096,2048]{1,0:T(8,128)(2,1)} %get-tuple-element.30.grad_ref.grads_ref, bf16[4096,2048]{1,0:T(8,128)(2,1)} %get-tuple-element.28.hat_ref, bf16[2048,896]{1,0:T(8,128)(2,1)} %bitcast.40, ...), custom_call_target="tpu_custom_call" | custom-call | tf_op jit(solution)/shard_map/pallas_call | solution.py:1189
  336.7 0.0 copy-start.2
  336.7 124.6 %shard_map.155 = (f32[128,2048]{1,0:T(8,128)}, f32[1,2048]{1,0:T(1,128)}, bf16[32,64,512]{2,1,0:T(8,128)(2,1)}, bf16[32,64,384]{2,1,0:T(8,128)(2,1)}) custom-call(bf16[4096,384]{1,0:T(8,128)(2,1)} %get-tuple-element.37.joined_ref, bf16[4096,2048]{1,0:T(8,128)(2,1)} %get-tuple-element.30.grad_ref.grads_ref, bf16[4096,2048]{1,0:T(8,128)(2,1)} %get-tuple-element.38.part_ref, ...), custom_call_target="tpu_custom_call" | custom-call | tf_op jit(solution)/shard_map/pallas_call | solution.py:1279
  461.3 0.9 fusion
  462.3 1.3 dynamic-slice_bitcast_fusion
  463.5 0.7 reshape.235
  464.2 1.4 copy-done.5
  465.6 3.0 shard_map.157
  468.6 3.5 shard_map.156
  472.1 0.7 slice_reduce_fusion
  472.8 1.0 copy.30
  (20 shorter events, 0.1 us)
Async XLA Ops:
  7.3 1.0 copy-start.1
  8.4 1.5 copy-start.4
  9.9 1.3 copy-start.6
  143.1 1.8 copy-start
  336.7 124.6 %copy-start.2 = (bf16[1,128,2048]{2,1,0:T(8,128)(2,1)S(1)}, bf16[1,128,2048]{2,1,0:T(8,128)(2,1)}, u32[]{:S(2)}) copy-start(bf16[1,128,2048]{2,1,0:T(8,128)(2,1)} %param.9) | copy-start | bytes 1572868
  336.7 124.6 %copy-start.8 = (bf16[128,2048]{1,0:T(8,128)(2,1)S(1)}, bf16[128,2048]{1,0:T(8,128)(2,1)}, u32[]{:S(2)}) copy-start(bf16[128,2048]{1,0:T(8,128)(2,1)} %get-tuple-element.36) | copy-start | bytes 1572868
  336.7 126.8 %copy-start.9 = (f32[1,512]{1,0:T(1,128)S(1)}, f32[1,512]{1,0:T(1,128)}, u32[]{:S(2)}) copy-start(f32[1,512]{1,0:T(1,128)} %get-tuple-element.43) | copy-start | bytes 6148
  461.3 7.3 %copy-start.3 = (bf16[32,64,512]{2,1,0:T(8,128)(2,1)S(1)}, bf16[32,64,512]{2,1,0:T(8,128)(2,1)}, u32[]{:S(2)}) copy-start(bf16[32,64,512]{2,1,0:T(8,128)(2,1)} %get-tuple-element.41.blocks_ref) | copy-start | bytes 6291460
  464.2 1.4 copy-start.5
  465.6 7.2 %copy-start.7 = (f32[128,2048]{1,0:T(8,128)S(1)}, f32[128,2048]{1,0:T(8,128)}, u32[]{:S(2)}) copy-start(f32[128,2048]{1,0:T(8,128)} %get-tuple-element.40) | copy-start | bytes 3145732

commit v5 on v4

--- a/solution.py
+++ b/solution.py
@@ -3,6 +3,7 @@
 
 import jax
 import jax.numpy as jnp
+import numpy as np
 from jax import lax
 from jax.experimental import pallas as pl
 from jax.experimental.pallas import tpu as pltpu
@@ -530,7 +531,7 @@
         self.me, self.blocks_ref, self.got_ref, self.sends, self.arrivals = me, blocks_ref, got_ref, sends, arrivals
         self.mine = me.z * 8 + me.c
         self.keep = pltpu.make_async_copy(blocks_ref.at[self.mine], got_ref.at[self.mine], local)
-        order = [high * 8 + low for low in range(8) for high in EXCHANGE_ORDER if high < me.depth]
+        order = [high * 8 + low for low in LOWS for high in range(me.depth)]
         self.order = [k for k in order if k]
         self.steps = [functools.partial(self.start, k) for k in self.order] + [self.keep.start]
 
@@ -554,7 +555,7 @@
         return [pltpu.SemaphoreType.DMA(()), pltpu.SemaphoreType.DMA((depth * 8,)), pltpu.SemaphoreType.DMA((depth * 8,))]
 
 
-EXCHANGE_ORDER = (0, 1, 2, 3)
+LOWS = (0, 1, 2, 3, 4, 5, 6, 7)
 ROUTES = ("zf", "zf")
 ADD_ROWS = 32
 
@@ -867,7 +868,7 @@
         ]
         + gather_scratch(depth, routes)
         + Exchange.scratch(depth),
-        compiler_params=pltpu.CompilerParams(collective_id=collective_id, has_side_effects=True, vmem_limit_bytes=32 << 20),
+        compiler_params=pltpu.CompilerParams(collective_id=collective_id, has_side_effects=True, vmem_limit_bytes=HEAD_VMEM),
     )(inputs, w_in, w_out, scale, extra)
 
 
@@ -907,6 +908,7 @@
 
 
 SIDE = 256
+HEAD_VMEM = 62 << 20
 
 
 def turned(block, lane):
@@ -914,15 +916,12 @@
     return jnp.where(lane % HD < shift, pltpu.roll(block, LANES - shift, 1), pltpu.roll(block, shift, 1))
 
 
-def gelu(t):
-    inner = math.sqrt(2.0 / math.pi) * (t + 0.044715 * (t * t * t))
-    return 0.5 * t * (1.0 + jnp.tanh(inner))
-
-
-def gelu_slope(t):
-    slope = math.sqrt(2.0 / math.pi)
-    bent = jnp.tanh(slope * (t + 0.044715 * (t * t * t)))
-    return 0.5 * (1.0 + bent) + 0.5 * t * (1.0 - bent * bent) * slope * (1.0 + 3.0 * 0.044715 * (t * t))
+def gelu_and_slope(t):
+    scale = math.sqrt(2.0 / math.pi)
+    square = t * t
+    bent = jnp.tanh(scale * (t + 0.044715 * (square * t)))
+    half = 0.5 * (1.0 + bent)
+    return t * half, half + 0.5 * t * (1.0 - bent * bent) * scale * (1.0 + 3.0 * 0.044715 * square)
 
 
 def allowed_keys(start, first_query, keys):
@@ -949,7 +948,7 @@
     scaling = HD ** (-0.5)
     parts = gather_parts(depth, shard_rows, routes, grad_ref, grads_ref, scratch)
     chunks = seq // SIDE
-    slots = spread_steps([parts[0].me.greet] + interleaved(parts), len(parts), depth * 2 * chunks, [part.finish for part in parts])
+    slots = spread_steps([parts[0].me.greet] + interleaved(parts), len(parts), depth * 2 * chunks, IDLE, [part.finish for part in parts])
     side_lanes = slice(joint_width - LANES, joint_width)
 
     for q in range(chunks):
@@ -991,11 +990,15 @@
         attended = jnp.dot(weights, values_ref[:count, :], preferred_element_type=jnp.float32)
         run_slots(slots, here, 2 * q + 1, depth, 2 * chunks)
         lse = largest + jnp.log(total)
-        mid_ref[rows, : 2 * LANES] = joint[:, LANES : 3 * LANES]
-        mid_ref[rows, 2 * LANES :] = jnp.where(low, joint[:, 3 * LANES :], lse)
-        joined_ref[rows, :LANES] = jnp.where(low, attended, gelu(joint[:, LANES : 2 * LANES])).astype(jnp.bfloat16)
-        joined_ref[rows, LANES : 2 * LANES] = gelu(joint[:, 2 * LANES : 3 * LANES]).astype(jnp.bfloat16)
-        joined_ref[rows, 2 * LANES :] = jnp.where(low, gelu(joint[:, 3 * LANES :]), 0.0).astype(jnp.bfloat16)
+        hidden, slope = gelu_and_slope(joint[:, LANES : 2 * LANES])
+        mid_ref[rows, :LANES] = jnp.where(low, joint[:, LANES : 2 * LANES], slope)
+        joined_ref[rows, :LANES] = jnp.where(low, attended, hidden).astype(jnp.bfloat16)
+        hidden, slope = gelu_and_slope(joint[:, 2 * LANES : 3 * LANES])
+        mid_ref[rows, LANES : 2 * LANES] = slope
+        joined_ref[rows, LANES : 2 * LANES] = hidden.astype(jnp.bfloat16)
+        hidden, slope = gelu_and_slope(jnp.where(low, joint[:, 3 * LANES :], 0.0))
+        mid_ref[rows, 2 * LANES :] = jnp.where(low, slope, lse)
+        joined_ref[rows, 2 * LANES :] = hidden.astype(jnp.bfloat16)
         branch = lax.dot_general(joined_ref[rows, :], weights_ref[:, joint_width:], NT, preferred_element_type=jnp.float32)
         out_ref[rows, :] = (branch + out_bias_ref[...]).astype(jnp.bfloat16)
 
@@ -1005,13 +1008,13 @@
             step()
 
 
-def spread_steps(steps, ahead, count, after):
+def spread_steps(steps, ahead, count, idle, after):
     slots = [[] for _ in range(count + 1)]
     slots[0] += steps[: 1 + ahead]
     rest = steps[1 + ahead :]
     for n, step in enumerate(rest):
-        slots[n * count // len(rest)].append(step)
-    slots[-1] = list(after)
+        slots[min(n * (count - idle) // len(rest), count)].append(step)
+    slots[-1] += after
     return slots
 
 
@@ -1059,11 +1062,12 @@
         scratch_shapes=[pltpu.VMEM((seq, LANES), jnp.bfloat16)] * 2
         + [pltpu.VMEM((1, joint_width), jnp.float32)]
         + gather_scratch(depth, routes),
-        compiler_params=pltpu.CompilerParams(collective_id=collective_id, has_side_effects=True, vmem_limit_bytes=56 << 20),
+        compiler_params=pltpu.CompilerParams(collective_id=collective_id, has_side_effects=True, vmem_limit_bytes=63 << 20),
     )(hat_all, weights, bias, waves, out_bias, grads)
 
 
-LATEST = 27
+LATEST = 30
+IDLE = -4
 
 
 def backward_kernel(depth, shard_rows, joint_width, routes, grad_ref, hat_ref, weights_ref, qk_ref, mid_ref, cos_ref, sin_ref, branch_ref,
@@ -1082,8 +1086,10 @@
     slots[0] += [parts[0].me.greet] + main[: len(parts)]
     for n, step in enumerate(main[len(parts) : ahead]):
         slots[1 + n // len(parts)].append(step)
+    due = slots[:-1] + [[]]
     for n, step in enumerate(main[ahead:]):
-        slots[1 + depth + n * LATEST // (len(main) - ahead)].append(step)
+        due[min(1 + depth + n * LATEST // (len(main) - ahead), len(due) - 1)].append(step)
+    slots = due[:-1] + [due[-1] + slots[-1]]
 
     def first_stage(q, rows):
         if q == 0:
@@ -1114,12 +1120,12 @@
         d_query_ref[rows, :] = jnp.dot(d_scores, keys_ref[:count, :], preferred_element_type=jnp.float32) * scaling
         d_key_ref[:count, :] += lax.dot_general(d_scores, query, TN, preferred_element_type=jnp.float32)
         d_value_ref[:count, :] += lax.dot_general(weights, d_out, TN, preferred_element_type=jnp.float32)
-        d_joint_ref[rows, LANES : 2 * LANES] = (d_joined[:, :LANES] * gelu_slope(mid_ref[rows, :LANES])).astype(jnp.bfloat16)
+        d_joint_ref[rows, LANES : 2 * LANES] = (d_joined[:, :LANES] * mid_ref[rows, :LANES]).astype(jnp.bfloat16)
         d_joint_ref[rows, 2 * LANES : 3 * LANES] = (
-            d_joined[:, LANES : 2 * LANES] * gelu_slope(mid_ref[rows, LANES : 2 * LANES])
+            d_joined[:, LANES : 2 * LANES] * mid_ref[rows, LANES : 2 * LANES]
         ).astype(jnp.bfloat16)
         d_joint_ref[rows, 3 * LANES :] = jnp.where(
-            low, d_joined[:, 2 * LANES :] * gelu_slope(mid_ref[rows, 2 * LANES :]), 0.0
+            low, d_joined[:, 2 * LANES :] * mid_ref[rows, 2 * LANES :], 0.0
         ).astype(jnp.bfloat16)
 
     def second_stage(q, rows):
@@ -1210,6 +1216,10 @@
     )(grad_all, hat_all, weights, qk, mid, cosine, sine, branch)
 
 
+def TAIL(side, main):
+    return side + main
+
+
 def tail_kernel(depth, full, routes, joined_ref, grads_ref, part_ref, blocks_ref, inputs_ref, grad_ref,
                 out_ref, column_ref, got_in_ref, got_out_ref, total_ref, back_ref, *scratch):
     here = pl.program_id(0)
@@ -1245,7 +1255,7 @@
             turned_part = total_ref[:, n * SIDE : (n + 1) * SIDE].T.astype(back_ref.dtype)
             for m in range(SIDE // depth_rows):
                 back_ref[n * (SIDE // depth_rows) + m] = turned_part[m * depth_rows : (m + 1) * depth_rows]
-        for step in late.steps + main[ahead + len(parts) :]:
+        for step in TAIL(late.steps, main[ahead + len(parts) :]):
             step()
 
         @pl.loop(0, full // 32)
@@ -1322,9 +1332,9 @@
 
     weights = got.reshape(model_width, -1)
     half = ROT // 2
-    lane = jnp.arange(LANES) % HD
-    frequency = 10000.0 ** (-2.0 * (lane % half).astype(jnp.float32) / ROT)
-    waves = jnp.stack([jnp.where(lane < ROT, frequency, 0.0), jnp.where(lane < half, -1.0, 1.0)])
+    lane = np.arange(LANES) % HD
+    frequency = np.float32(10000.0) ** (-2.0 * (lane % half).astype(np.float32) / np.float32(ROT))
+    waves = np.stack([np.where(lane < ROT, frequency, 0.0), np.where(lane < half, -1.0, 1.0)]).astype(np.float32)
     bias = jnp.pad(in_bias.astype(jnp.float32).reshape(1, in_width), ((0, 0), (0, joint_width - in_width)))
     column = jnp.arange(model_width) // own
     out_row = jnp.where(column == me, jnp.tile(out_bias.astype(jnp.float32), devices), 0.0)[None]
@@ -1332,11 +1342,11 @@
         hat_all, weights, joint_width, bias, waves, out_row, out_grad[0], depth, seq_len, ("zf", "fz"), 1
     )
     d_hat_part, joint_sums, back_in, branch_own = backward(
-        g_all, hat_all, weights, joint_width, qk, mid, cosine, sine, branch, depth, seq_len, ROUTES, 2
+        g_all, hat_all, weights, joint_width, qk, mid, cosine, sine, branch, depth, seq_len, ("zf",) * 4, 2
     )
     result = (inputs.astype(jnp.float32) + branch_own.astype(jnp.float32)).astype(jnp.bfloat16)
     d_input, column_sums, back_in, back_out = tail(
-        joined, g_all, d_hat_part, back_in.reshape(devices, own, -1), inputs, out_grad[0], depth, ROUTES, 3
+        joined, g_all, d_hat_part, back_in.reshape(devices, own, -1), inputs, out_grad[0], depth, ("zf",), 3
     )
     grad_w_out, _ = join_blocks(back_out, out_parts)
     grad_w_in, vectors = join_blocks(back_in, in_parts)

time: 475 us -> 462 us (0.973)
  Pallas kernels: 455 us -> 448 us
  local copies, waits for them, and re-layouts: 13.4 us -> 8.29 us
    pallas_call x1, Pallas kernels: 105 us -> 97.5 us  [backward(): pl.pallas_call(functools.partial(backward_kernel, depth, own, joint_width...]
    unnamed x21 -> x15, local copies, waits for them, and re-layouts: 8.09 us -> 2.4 us
where the time goes in v5:
time: 462 us; the launch traced here: 461 us
  Pallas kernels  448 us (97%)
  local copies, waits for them, and re-layouts  8.29 us (2%)
    pallas_call x1, Pallas kernels, head(): pl.pallas_call(functools.partial(head_kernel, depth, rows, routes, parts_...  133 us
    pallas_call x1, Pallas kernels, tail(): pl.pallas_call(functools.partial(tail_kernel, depth, rows, routes), grid=...  124 us
    pallas_call x1, Pallas kernels, backward(): pl.pallas_call(functools.partial(backward_kernel, depth, own, joint_width...  97.5 us
    pallas_call x1, Pallas kernels, forward(): pl.pallas_call(functools.partial(forward_kernel, depth, grads.shape[0], j...  86.6 us

profile of v5, /device:TPU:0, one launch (start us, length us, event | category | flops | bytes accessed | tf_op | source)
XLA Modules:
  0.0 461.2 jit_solution(7580611344152254150)
XLA Ops:
  0.6 0.7 dynamic-slice_bitcast_fusion.1
  1.3 0.9 convert_reduce_fusion
  2.2 0.7 bitcast_convert_fusion.1
  2.8 0.7 bitcast_convert_fusion
  3.5 0.1 convert_element_type.32
  3.6 0.8 reshape.156
  4.4 0.6 pad_convert_fusion.bias_ref
  5.0 0.7 tile.4
  5.6 0.1 tile.10
  5.7 0.6 compare_select_fusion.out_bias_ref
  6.3 0.1 copy.25
  6.4 0.1 copy.28.scale_ref
  6.5 0.1 copy.27
  6.6 0.7 concatenate.3.extra_ref
  7.3 0.0 copy-done.5
  7.3 132.8 %shard_map.161 = (bf16[4096,2048]{1,0:T(8,128)(2,1)}, bf16[32,64,896]{2,1,0:T(8,128)(2,1)}) custom-call(bf16[128,2048]{1,0:T(8,128)(2,1)} %bitcast.41, bf16[64,14336]{1,0:T(8,128)(2,1)} %bitcast.46, bf16[64,10240]{1,0:T(8,128)(2,1)} %w_out_ref.1, f32[64,1]{1,0:T(8,128)} %copy-done.5, f32[64,128]{1,0:T(8,128)} %concatenate.3.extra_ref), custom_call_target="tpu_custom_call" | custom-call | tf_op jit(solution)/shard_map/pallas_call | solution.py:854
  140.1 86.6 %shard_map.162 = (bf16[4096,128]{1,0:T(8,128)(2,1)}, f32[4096,384]{1,0:T(8,128)}, f32[4096,128]{1,0:T(8,128)}, f32[4096,128]{1,0:T(8,128)}, bf16[4096,384]{1,0:T...) custom-call(bf16[4096,2048]{1,0:T(8,128)(2,1)} %get-tuple-element.28.hat_ref, ...), custom_call_target="tpu_custom_call" | custom-call | tf_op jit(solution)/shard_map/pallas_call | solution.py:1045
  226.7 97.5 %shard_map.163 = (bf16[4096,2048]{1,0:T(8,128)(2,1)}, f32[1,512]{1,0:T(1,128)}, bf16[2048,512]{1,0:T(8,128)(2,1)}, bf16[128,2048]{1,0:T(8,128)(2,1)}) custom-call(bf16[4096,2048]{1,0:T(8,128)(2,1)} %get-tuple-element.30.grad_ref.grads_ref, bf16[4096,2048]{1,0:T(8,128)(2,1)} %get-tuple-element.28.hat_ref, bf16[2048,896]{1,0:T(8,128)(2,1)} %bitcast.40, ...), custom_call_target="tpu_custom_call" | custom-call | tf_op jit(solution)/shard_map/pallas_call | solution.py:1195
  324.2 0.0 copy-start.2
  324.2 0.0 copy-start.4
  324.2 0.0 copy-start.6
  324.2 124.5 %shard_map.164 = (f32[128,2048]{1,0:T(8,128)}, f32[1,2048]{1,0:T(1,128)}, bf16[32,64,512]{2,1,0:T(8,128)(2,1)}, bf16[32,64,384]{2,1,0:T(8,128)(2,1)}) custom-call(bf16[4096,384]{1,0:T(8,128)(2,1)} %get-tuple-element.37.joined_ref, bf16[4096,2048]{1,0:T(8,128)(2,1)} %get-tuple-element.30.grad_ref.grads_ref, bf16[4096,2048]{1,0:T(8,128)(2,1)} %get-tuple-element.38.part_ref, ...), custom_call_target="tpu_custom_call" | custom-call | tf_op jit(solution)/shard_map/pallas_call | solution.py:1289
  448.7 0.0 copy-start
  448.7 0.0 copy-done.2
  448.7 0.9 fusion
  449.7 1.2 dynamic-slice_bitcast_fusion
  450.9 0.7 reshape.158
  451.6 1.4 copy-done.1
  453.0 3.0 shard_map.166
  456.0 3.5 shard_map.165
  459.5 0.7 slice_reduce_fusion
  460.2 1.0 copy.30
  (12 shorter events, 0.1 us)
Async XLA Ops:
  6.5 0.8 copy-start.5
  324.2 124.5 %copy-start.2 = (bf16[1,128,2048]{2,1,0:T(8,128)(2,1)S(1)}, bf16[1,128,2048]{2,1,0:T(8,128)(2,1)}, u32[]{:S(2)}) copy-start(bf16[1,128,2048]{2,1,0:T(8,128)(2,1)} %param.10) | copy-start | bytes 1572868
  324.2 124.5 %copy-start.4 = (bf16[128,2048]{1,0:T(8,128)(2,1)S(1)}, bf16[128,2048]{1,0:T(8,128)(2,1)}, u32[]{:S(2)}) copy-start(bf16[128,2048]{1,0:T(8,128)(2,1)} %get-tuple-element.36) | copy-start | bytes 1572868
  324.2 126.7 %copy-start.6 = (f32[1,512]{1,0:T(1,128)S(1)}, f32[1,512]{1,0:T(1,128)}, u32[]{:S(2)}) copy-start(f32[1,512]{1,0:T(1,128)} %get-tuple-element.43) | copy-start | bytes 6148
  448.7 7.3 %copy-start = (bf16[32,64,512]{2,1,0:T(8,128)(2,1)S(1)}, bf16[32,64,512]{2,1,0:T(8,128)(2,1)}, u32[]{:S(2)}) copy-start(bf16[32,64,512]{2,1,0:T(8,128)(2,1)} %get-tuple-element.41.blocks_ref) | copy-start | bytes 6291460
  451.6 1.4 copy-start.1
  453.0 7.2 %copy-start.3 = (f32[128,2048]{1,0:T(8,128)S(1)}, f32[128,2048]{1,0:T(8,128)}, u32[]{:S(2)}) copy-start(f32[128,2048]{1,0:T(8,128)} %get-tuple-element.40) | copy-start | bytes 3145732

commit v6 on v5

--- a/solution.py
+++ b/solution.py
@@ -940,7 +940,7 @@
 
 
 def forward_kernel(depth, shard_rows, joint_width, routes, hat_ref, weights_ref, bias_ref, waves_ref, out_bias_ref, grad_ref,
-                   qk_ref, mid_ref, cos_ref, sin_ref, joined_ref, out_ref, grads_ref, keys_ref, values_ref, shift_ref, *scratch):
+                   qk_ref, mid_ref, cos_ref, sin_ref, joined_ref, out_ref, grads_ref, keys_ref, values_ref, shift_ref, out_row_ref, *scratch):
     seq = hat_ref.shape[0]
     here = pl.program_id(0)
     low = low_half((SIDE, LANES))
@@ -957,7 +957,13 @@
 
             @pl.when(here == 0)
             def _():
-                total = bias_ref[...]
+                both = jnp.concatenate([out_bias_ref[...].astype(jnp.float32)] * 2, 1)
+                both = jnp.concatenate([both] * (out_row_ref.shape[1] // LANES), 1)
+                owner = lax.broadcasted_iota(jnp.int32, both.shape, 1) // HD
+                out_row_ref[...] = jnp.where(owner == parts[0].me.z * 8 + parts[0].me.c, both, 0.0)
+                pieces = [bias_ref[n : n + 1, :].astype(jnp.float32) for n in range(bias_ref.shape[0])]
+                pieces += [jnp.zeros_like(pieces[0])] * (joint_width // HD - len(pieces))
+                total = jnp.concatenate(pieces, 1)
                 for n in range(weights_ref.shape[0] // SIDE):
                     some = slice(n * SIDE, (n + 1) * SIDE)
                     side = weights_ref[some, side_lanes].astype(jnp.float32)
@@ -1000,7 +1006,7 @@
         mid_ref[rows, 2 * LANES :] = jnp.where(low, slope, lse)
         joined_ref[rows, 2 * LANES :] = hidden.astype(jnp.bfloat16)
         branch = lax.dot_general(joined_ref[rows, :], weights_ref[:, joint_width:], NT, preferred_element_type=jnp.float32)
-        out_ref[rows, :] = (branch + out_bias_ref[...]).astype(jnp.bfloat16)
+        out_ref[rows, :] = (branch + out_row_ref[...]).astype(jnp.bfloat16)
 
     @pl.when(here == pl.num_programs(0) - 1)
     def _():
@@ -1060,7 +1066,7 @@
             pl.BlockSpec(memory_space=pl.ANY),
         ),
         scratch_shapes=[pltpu.VMEM((seq, LANES), jnp.bfloat16)] * 2
-        + [pltpu.VMEM((1, joint_width), jnp.float32)]
+        + [pltpu.VMEM((1, joint_width), jnp.float32), pltpu.VMEM((1, width), jnp.float32)]
         + gather_scratch(depth, routes),
         compiler_params=pltpu.CompilerParams(collective_id=collective_id, has_side_effects=True, vmem_limit_bytes=63 << 20),
     )(hat_all, weights, bias, waves, out_bias, grads)
@@ -1216,8 +1222,7 @@
     )(grad_all, hat_all, weights, qk, mid, cosine, sine, branch)
 
 
-def TAIL(side, main):
-    return side + main
+PLANE_SLOT = 7
 
 
 def tail_kernel(depth, full, routes, joined_ref, grads_ref, part_ref, blocks_ref, inputs_ref, grad_ref,
@@ -1235,7 +1240,7 @@
     slots[0] += [me.greet_all] + main[: len(parts)] + early.steps
     for n, step in enumerate(main[len(parts) : ahead]):
         slots[1 + n // len(parts)].append(step)
-    slots[-1] += main[ahead : ahead + len(parts)]
+    slots[PLANE_SLOT] += main[ahead : ahead + len(parts)]
     for at in range(chunks):
         run_slots(slots, here, at, 1, chunks, at)
 
@@ -1255,7 +1260,7 @@
             turned_part = total_ref[:, n * SIDE : (n + 1) * SIDE].T.astype(back_ref.dtype)
             for m in range(SIDE // depth_rows):
                 back_ref[n * (SIDE // depth_rows) + m] = turned_part[m * depth_rows : (m + 1) * depth_rows]
-        for step in TAIL(late.steps, main[ahead + len(parts) :]):
+        for step in late.steps + main[ahead + len(parts) :]:
             step()
 
         @pl.loop(0, full // 32)
@@ -1335,11 +1340,8 @@
     lane = np.arange(LANES) % HD
     frequency = np.float32(10000.0) ** (-2.0 * (lane % half).astype(np.float32) / np.float32(ROT))
     waves = np.stack([np.where(lane < ROT, frequency, 0.0), np.where(lane < half, -1.0, 1.0)]).astype(np.float32)
-    bias = jnp.pad(in_bias.astype(jnp.float32).reshape(1, in_width), ((0, 0), (0, joint_width - in_width)))
-    column = jnp.arange(model_width) // own
-    out_row = jnp.where(column == me, jnp.tile(out_bias.astype(jnp.float32), devices), 0.0)[None]
     qk, mid, cosine, sine, joined, branch, g_all = forward(
-        hat_all, weights, joint_width, bias, waves, out_row, out_grad[0], depth, seq_len, ("zf", "fz"), 1
+        hat_all, weights, joint_width, in_bias, waves, out_bias[None], out_grad[0], depth, seq_len, ("zf", "fz"), 1
     )
     d_hat_part, joint_sums, back_in, branch_own = backward(
         g_all, hat_all, weights, joint_width, qk, mid, cosine, sine, branch, depth, seq_len, ("zf",) * 4, 2

time: 462 us -> 459 us (level)
  no operation moved by 1% of the time
where the time goes in v6:
time: 459 us
  Pallas kernels  448 us (98%)
  local copies, waits for them, and re-layouts  6.79 us (1%)
    pallas_call x1, Pallas kernels, head(): pl.pallas_call(functools.partial(head_kernel, depth, rows, routes, parts_...  133 us
    pallas_call x1, Pallas kernels, tail(): pl.pallas_call(functools.partial(tail_kernel, depth, rows, routes), grid=...  125 us
    pallas_call x1, Pallas kernels, backward(): pl.pallas_call(functools.partial(backward_kernel, depth, own, joint_width...  97.5 us
    pallas_call x1, Pallas kernels, forward(): pl.pallas_call(functools.partial(forward_kernel, depth, grads.shape[0], j...  86.6 us

profile of v6, /device:TPU:0, one launch (start us, length us, event | category | flops | bytes accessed | tf_op | source)
XLA Modules:
  0.0 458.6 jit_solution(7678631786091072619)
XLA Ops:
  0.6 0.7 dynamic-slice_bitcast_fusion.1
  1.3 0.9 convert_reduce_fusion
  2.2 0.7 bitcast_convert_fusion.1
  2.8 0.7 bitcast_convert_fusion
  3.5 0.1 convert_element_type.26
  3.6 0.1 copy.25
  3.7 0.1 copy.28.scale_ref
  3.8 0.0 copy-start.5
  3.8 0.1 copy.27
  3.9 0.7 concatenate.3.extra_ref
  4.6 0.0 copy-done.5
  4.6 132.8 %shard_map.161 = (bf16[4096,2048]{1,0:T(8,128)(2,1)}, bf16[32,64,896]{2,1,0:T(8,128)(2,1)}) custom-call(bf16[128,2048]{1,0:T(8,128)(2,1)} %bitcast.42, bf16[64,14336]{1,0:T(8,128)(2,1)} %bitcast.47, bf16[64,10240]{1,0:T(8,128)(2,1)} %w_out_ref.1, f32[64,1]{1,0:T(8,128)} %copy-done.5, f32[64,128]{1,0:T(8,128)} %concatenate.3.extra_ref), custom_call_target="tpu_custom_call" | custom-call | tf_op jit(solution)/shard_map/pallas_call | solution.py:854
  137.4 86.6 %shard_map.162 = (bf16[4096,128]{1,0:T(8,128)(2,1)}, f32[4096,384]{1,0:T(8,128)}, f32[4096,128]{1,0:T(8,128)}, f32[4096,128]{1,0:T(8,128)}, bf16[4096,384]{1,0:T...) custom-call(bf16[4096,2048]{1,0:T(8,128)(2,1)} %get-tuple-element.28.hat_ref, ...), custom_call_target="tpu_custom_call" | custom-call | tf_op jit(solution)/shard_map/pallas_call | solution.py:1051
  224.0 97.5 %shard_map.163 = (bf16[4096,2048]{1,0:T(8,128)(2,1)}, f32[1,512]{1,0:T(1,128)}, bf16[2048,512]{1,0:T(8,128)(2,1)}, bf16[128,2048]{1,0:T(8,128)(2,1)}) custom-call(bf16[4096,2048]{1,0:T(8,128)(2,1)} %get-tuple-element.30.grad_ref.grads_ref, bf16[4096,2048]{1,0:T(8,128)(2,1)} %get-tuple-element.28.hat_ref, bf16[2048,896]{1,0:T(8,128)(2,1)} %bitcast.41, ...), custom_call_target="tpu_custom_call" | custom-call | tf_op jit(solution)/shard_map/pallas_call | solution.py:1201
  321.5 0.0 copy-start.2
  321.5 0.0 copy-start.4
  321.5 0.0 copy-start.6
  321.5 124.6 %shard_map.164 = (f32[128,2048]{1,0:T(8,128)}, f32[1,2048]{1,0:T(1,128)}, bf16[32,64,512]{2,1,0:T(8,128)(2,1)}, bf16[32,64,384]{2,1,0:T(8,128)(2,1)}) custom-call(bf16[4096,384]{1,0:T(8,128)(2,1)} %get-tuple-element.37.joined_ref, bf16[4096,2048]{1,0:T(8,128)(2,1)} %get-tuple-element.30.grad_ref.grads_ref, bf16[4096,2048]{1,0:T(8,128)(2,1)} %get-tuple-element.38.part_ref, ...), custom_call_target="tpu_custom_call" | custom-call | tf_op jit(solution)/shard_map/pallas_call | solution.py:1294
  446.1 0.0 copy-start
  446.1 0.0 copy-done.2
  446.1 0.0 copy-done.4
  446.1 0.9 fusion
  447.1 1.2 dynamic-slice_bitcast_fusion
  448.3 0.0 copy-done.6
  448.3 0.7 reshape.105
  449.0 1.4 copy-done.1
  450.4 3.0 shard_map.166
  453.4 0.0 copy-done
  453.4 3.5 shard_map.165
  456.9 0.7 slice_reduce_fusion
  457.6 0.0 copy-done.3
  457.6 1.0 copy.30
  (7 shorter events, 0.0 us)
Async XLA Ops:
  3.8 0.8 copy-start.5
  321.5 124.6 %copy-start.2 = (bf16[1,128,2048]{2,1,0:T(8,128)(2,1)S(1)}, bf16[1,128,2048]{2,1,0:T(8,128)(2,1)}, u32[]{:S(2)}) copy-start(bf16[1,128,2048]{2,1,0:T(8,128)(2,1)} %param.10) | copy-start | bytes 1572868
  321.5 124.6 %copy-start.4 = (bf16[128,2048]{1,0:T(8,128)(2,1)S(1)}, bf16[128,2048]{1,0:T(8,128)(2,1)}, u32[]{:S(2)}) copy-start(bf16[128,2048]{1,0:T(8,128)(2,1)} %get-tuple-element.36) | copy-start | bytes 1572868
  321.5 126.8 %copy-start.6 = (f32[1,512]{1,0:T(1,128)S(1)}, f32[1,512]{1,0:T(1,128)}, u32[]{:S(2)}) copy-start(f32[1,512]{1,0:T(1,128)} %get-tuple-element.43) | copy-start | bytes 6148
  446.1 7.3 %copy-start = (bf16[32,64,512]{2,1,0:T(8,128)(2,1)S(1)}, bf16[32,64,512]{2,1,0:T(8,128)(2,1)}, u32[]{:S(2)}) copy-start(bf16[32,64,512]{2,1,0:T(8,128)(2,1)} %get-tuple-element.41.blocks_ref) | copy-start | bytes 6291460
  449.0 1.4 copy-start.1
  450.4 7.2 %copy-start.3 = (f32[128,2048]{1,0:T(8,128)S(1)}, f32[128,2048]{1,0:T(8,128)}, u32[]{:S(2)}) copy-start(f32[128,2048]{1,0:T(8,128)} %get-tuple-element.40) | copy-start | bytes 3145732
